TPU v7x, 8 devices: a whole 2x2x1 slice. The times are simulated.
8 devices in a mesh: rep: 1 (over z), dp: 8 (over x, y, core).
Axes of the slice: x: 2, y: 2, z: 1, core: 2. Of those that a mesh axis runs over, the one named last changes fastest.
Arguments:
- g_w_gate: bfloat16 [8, 2, 1152, 4608], P(('rep', 'dp'))
- g_w_up: bfloat16 [8, 2, 1152, 4608], P(('rep', 'dp'))
- g_w_down: bfloat16 [8, 2, 4608, 1152], P(('rep', 'dp'))
- w_gate: bfloat16 [2, 1152, 4608], replicated
- w_up: bfloat16 [2, 1152, 4608], replicated
- w_down: bfloat16 [2, 4608, 1152], replicated
- m_w_gate: float32 [2, 1152, 4608], P(None, 'dp')
- m_w_up: float32 [2, 1152, 4608], P(None, 'dp')
- m_w_down: float32 [2, 4608, 1152], P(None, 'dp')
- v_w_gate: float32 [2, 1152, 4608], P(None, 'dp')
- v_w_up: float32 [2, 1152, 4608], P(None, 'dp')
- v_w_down: float32 [2, 4608, 1152], P(None, 'dp')
Outputs:
- output 1: bfloat16 [2, 1152, 4608], P('rep')
- output 2: bfloat16 [2, 1152, 4608], P('rep')
- output 3: bfloat16 [2, 4608, 1152], P('rep')
- output 4: float32 [2, 1152, 4608], P('rep', 'dp')
- output 5: float32 [2, 1152, 4608], P('rep', 'dp')
- output 6: float32 [2, 4608, 1152], P('rep', 'dp')
- output 7: float32 [2, 1152, 4608], P('rep', 'dp')
- output 8: float32 [2, 1152, 4608], P('rep', 'dp')
- output 9: float32 [2, 4608, 1152], P('rep', 'dp')
All inputs are finite; a program needn't handle non-finite values.
Results may differ from a plain program's by a relative error of at most 0.022.
Values are sent between devices in bfloat16 or wider.
A program may use at most 2 GiB of HBM per device.

v0:
```python
import jax
import jax.numpy as jnp
from jax import lax
from jax.sharding import PartitionSpec as P


def adamw(w, m, v, g):
    m = 0.9 * m + 0.1 * g
    v = 0.95 * v + 0.05 * g * g
    step = m * lax.rsqrt(v + 1e-8) + 0.1 * w
    return (w - 0.02 * step).astype(jnp.bfloat16), m, v


def solution(mesh):
    def step(*arrays):
        terms, weights, m, v = (arrays[i : i + 3] for i in (0, 3, 6, 9))
        gradients = [lax.psum_scatter(t[0], "dp", scatter_dimension=1, tiled=True).astype(jnp.float32) for t in terms]
        me = lax.axis_index("dp")
        own = [lax.dynamic_slice_in_dim(w, me * one.shape[1], one.shape[1], 1).astype(jnp.float32) for w, one in zip(weights, m, strict=True)]
        new = [adamw(w, m, v, g) for w, m, v, g in zip(own, m, v, gradients, strict=True)]
        whole = [lax.all_gather(one[0], "dp", axis=1, tiled=True) for one in new]
        return (*whole, *(one[1] for one in new), *(one[2] for one in new))

    all_of, cut = P(None, None, None), P(None, "dp", None)
    return jax.shard_map(
        step,
        mesh=mesh,
        in_specs=(P(("rep", "dp"), None, None, None),) * 3 + (all_of,) * 3 + (cut,) * 6,
        out_specs=(P("rep", None, None),) * 3 + (P("rep", "dp", None),) * 6,
        check_vma=False,
    )
```

profile of v0, /device:TPU:0, one launch (start us, length us, event | category | flops | bytes accessed | tf_op | source)
XLA Modules:
  0.0 771.0 jit_solution(53455739551966029)
XLA Ops:
  7.2 0.0 reduce-scatter.8.cloned.1.call-start
  7.2 0.7 reduce-scatter.8.cloned.1.call-update
  7.9 0.0 reduce-scatter.6.cloned.1.call-start
  8.0 0.7 reduce-scatter.6.cloned.1.call-update
  8.7 0.0 reduce-scatter.4.cloned.1.call-start
  8.7 0.7 reduce-scatter.4.cloned.1.call-update
  9.4 0.0 all-gather.8.cloned.1.call-start
  9.4 133.0 %reduce-scatter.8.cloned.1.call-done = bf16[2,576,1152]{2,1,0:T(8,128)(2,1)} async-done(((bf16[2,4608,1152]{2,1,0:T(8,128)(2,1)}), bf16[2,576,1152]{2,1,0:T(8,128)(2,1)}) %reduce-scatter.8.cloned.1.call-update) | async-done | bytes 2654224 | tf_op jit(solution)/shard_map/reduce_scatter | solution.py:17
  142.5 11.0 %fusion.10 = (bf16[2,576,1152]{2,1,0:T(8,128)(2,1)}, f32[2,576,1152]{2,1,0:T(8,128)}, f32[2,576,1152]{2,1,0:T(8,128)}) fusion(bf16[2,4608,1152]{2,1,0:T(8,128)(2,1)} %param.17, s32[]{:T(128)S(6)} %select_n.8, bf16[2,576,1152]{2,1,0:T(8,128)(2,1)} %reduce-scatter.8.cloned.1.call-done, f32[2,576,1152]{2,1,0:T(8,128)} %param.23, f32[2,576,1152]{2,1,0:T(8,128)} %param.20), kind=kLoop, calls=%fused_computation.22 | loop fusion | flops 21233664 | bytes 29196292 | tf_op jit(solution)/shard_map/convert_element_type | solution.py:11
  153.4 0.0 all-gather.8.cloned.1.call-update
  153.4 0.0 all-gather.6.cloned.1.call-start
  153.5 120.6 %reduce-scatter.6.cloned.1.call-done = bf16[2,144,4608]{2,1,0:T(8,128)(2,1)} async-done(((bf16[2,1152,4608]{2,1,0:T(8,128)(2,1)}), bf16[2,144,4608]{2,1,0:T(8,128)(2,1)}) %reduce-scatter.6.cloned.1.call-update) | async-done | bytes 2654224 | tf_op jit(solution)/shard_map/reduce_scatter | solution.py:17
  274.1 10.8 %fusion.6 = (bf16[2,144,4608]{2,1,0:T(8,128)(2,1)}, f32[2,144,4608]{2,1,0:T(8,128)}, f32[2,144,4608]{2,1,0:T(8,128)}) fusion(bf16[2,1152,4608]{2,1,0:T(8,128)(2,1)} %param.16, s32[]{:T(128)S(6)} %select_n.7, bf16[2,144,4608]{2,1,0:T(8,128)(2,1)} %reduce-scatter.6.cloned.1.call-done, f32[2,144,4608]{2,1,0:T(8,128)} %param.22, f32[2,144,4608]{2,1,0:T(8,128)} %param.19), kind=kLoop, calls=%fused_computation.18 | loop fusion | flops 21233664 | bytes 29196292 | tf_op jit(solution)/shard_map/convert_element_type | solution.py:11
  284.9 0.0 all-gather.6.cloned.1.call-update
  284.9 0.0 all-gather.4.cloned.1.call-start
  285.0 120.8 %reduce-scatter.4.cloned.1.call-done = bf16[2,144,4608]{2,1,0:T(8,128)(2,1)} async-done(((bf16[2,1152,4608]{2,1,0:T(8,128)(2,1)}), bf16[2,144,4608]{2,1,0:T(8,128)(2,1)}) %reduce-scatter.4.cloned.1.call-update) | async-done | bytes 2654224 | tf_op jit(solution)/shard_map/reduce_scatter | solution.py:17
  405.8 10.8 %fusion.2 = (bf16[2,144,4608]{2,1,0:T(8,128)(2,1)}, f32[2,144,4608]{2,1,0:T(8,128)}, f32[2,144,4608]{2,1,0:T(8,128)}) fusion(bf16[2,1152,4608]{2,1,0:T(8,128)(2,1)} %param.15, s32[]{:T(128)S(6)} %select_n.7, bf16[2,144,4608]{2,1,0:T(8,128)(2,1)} %reduce-scatter.4.cloned.1.call-done, f32[2,144,4608]{2,1,0:T(8,128)} %param.21, f32[2,144,4608]{2,1,0:T(8,128)} %param.18), kind=kLoop, calls=%fused_computation.14 | loop fusion | flops 21233664 | bytes 29196292 | tf_op jit(solution)/shard_map/convert_element_type | solution.py:11
  416.5 0.0 all-gather.4.cloned.1.call-update
  416.6 94.5 %all-gather.8.cloned.1.call-done = bf16[2,4608,1152]{2,1,0:T(8,128)(2,1)} async-done(((bf16[2,576,1152]{2,1,0:T(8,128)(2,1)}), bf16[2,4608,1152]{2,1,0:T(8,128)(2,1)}) %all-gather.8.cloned.1.call-update) | async-done | bytes 21233680 | tf_op jit(solution)/shard_map/all_gather | solution.py:21
  511.0 105.3 %all-gather.6.cloned.1.call-done = bf16[2,1152,4608]{2,1,0:T(8,128)(2,1)} async-done(((bf16[2,144,4608]{2,1,0:T(8,128)(2,1)}), bf16[2,1152,4608]{2,1,0:T(8,128)(2,1)}) %all-gather.6.cloned.1.call-update) | async-done | bytes 21233680 | tf_op jit(solution)/shard_map/all_gather | solution.py:21
  616.3 105.3 %all-gather.4.cloned.1.call-done = bf16[2,1152,4608]{2,1,0:T(8,128)(2,1)} async-done(((bf16[2,144,4608]{2,1,0:T(8,128)(2,1)}), bf16[2,1152,4608]{2,1,0:T(8,128)(2,1)}) %all-gather.4.cloned.1.call-update) | async-done | bytes 21233680 | tf_op jit(solution)/shard_map/all_gather | solution.py:21
  721.6 0.0 copy-start
  721.6 21.0 %copy.24 = bf16[2,1152,4608]{2,1,0:T(8,128)(2,1)} copy(bf16[2,1152,4608]{2,1,0:T(8,128)(2,1)} %all-gather.4.cloned.1.call-done) | data formatting | bytes 42467328
  742.6 0.0 copy-done
  742.6 10.8 %copy.25 = bf16[2,1152,4608]{2,1,0:T(8,128)(2,1)} copy(bf16[2,1152,4608]{2,1,0:T(8,128)(2,1)S(1)} %copy-done) | data formatting | bytes 42467328
  753.3 0.0 slice-done
  753.3 0.0 slice-done.1
  753.3 0.0 slice-done.2
  753.3 1.8 slice-done.3
  755.1 1.4 slice-done.4
  756.5 0.0 slice-done.5
  756.5 7.6 copy.26
  (7 shorter events, 0.0 us)
Async XLA Ops:
  7.2 135.3 %reduce-scatter.8.cloned.1.call-start = ((), (), s32[]{:S(2)}) async-start(), calls=%async_computation.7 | async-start | bytes 23887872 | tf_op jit(solution)/shard_map/reduce_scatter | solution.py:17
  7.9 266.2 %reduce-scatter.6.cloned.1.call-start = ((), (), s32[]{:S(2)}) async-start(), calls=%async_computation.5 | async-start | bytes 23887872 | tf_op jit(solution)/shard_map/reduce_scatter | solution.py:17
  8.7 397.1 %reduce-scatter.4.cloned.1.call-start = ((), (), s32[]{:S(2)}) async-start(), calls=%async_computation.3 | async-start | bytes 23887872 | tf_op jit(solution)/shard_map/reduce_scatter | solution.py:17
  9.4 501.6 %all-gather.8.cloned.1.call-start = ((), (), s32[]{:S(2)}) async-start(), calls=%async_computation.8 | async-start | bytes 23887872 | tf_op jit(solution)/shard_map/all_gather | solution.py:21
  153.4 462.9 %all-gather.6.cloned.1.call-start = ((), (), s32[]{:S(2)}) async-start(), calls=%async_computation.6 | async-start | bytes 23887872 | tf_op jit(solution)/shard_map/all_gather | solution.py:21
  284.9 436.7 %all-gather.4.cloned.1.call-start = ((), (), s32[]{:S(2)}) async-start(), calls=%async_computation.4 | async-start | bytes 23887872 | tf_op jit(solution)/shard_map/all_gather | solution.py:21
  721.6 21.0 %copy-start = (bf16[2,1152,4608]{2,1,0:T(8,128)(2,1)S(1)}, bf16[2,1152,4608]{2,1,0:T(8,128)(2,1)}, u32[]{:S(2)}) copy-start(bf16[2,1152,4608]{2,1,0:T(8,128)(2,1)} %all-gather.6.cloned.1.call-done) | copy-start | bytes 63700996
  721.6 31.8 %slice-start = ((s8[21233664]{0:T(1024)(128)(4,1)}), s8[4194304]{0:T(1024)(128)(4,1)S(1)}, s32[]{:S(2)}) async-start(s8[21233664]{0:T(1024)(128)(4,1)} %bitcast.6), calls=%async_computation.9 | async-start | bytes 8388608
  721.6 31.8 %slice-start.1 = ((s8[21233664]{0:T(1024)(128)(4,1)}), s8[4194304]{0:T(1024)(128)(4,1)S(1)}, s32[]{:S(2)}) async-start(s8[21233664]{0:T(1024)(128)(4,1)} %bitcast.6), calls=%async_computation.10 | async-start | bytes 8388608
  721.6 31.8 %slice-start.2 = ((s8[21233664]{0:T(1024)(128)(4,1)}), s8[4194304]{0:T(1024)(128)(4,1)S(1)}, s32[]{:S(2)}) async-start(s8[21233664]{0:T(1024)(128)(4,1)} %bitcast.6), calls=%async_computation.11 | async-start | bytes 8388608
  721.6 33.5 %slice-start.3 = ((s8[21233664]{0:T(1024)(128)(4,1)}), s8[4194304]{0:T(1024)(128)(4,1)S(1)}, s32[]{:S(2)}) async-start(s8[21233664]{0:T(1024)(128)(4,1)} %bitcast.6), calls=%async_computation.12 | async-start | bytes 8388608
  742.6 13.9 %slice-start.4 = ((s8[21233664]{0:T(1024)(128)(4,1)}), s8[4194304]{0:T(1024)(128)(4,1)S(1)}, s32[]{:S(2)}) async-start(s8[21233664]{0:T(1024)(128)(4,1)} %bitcast.6), calls=%async_computation.13 | async-start | bytes 8388608
  742.6 13.9 %slice-start.5 = ((s8[21233664]{0:T(1024)(128)(4,1)}), s8[262144]{0:T(1024)(128)(4,1)S(1)}, s32[]{:S(2)}) async-start(s8[21233664]{0:T(1024)(128)(4,1)} %bitcast.6), calls=%async_computation.14 | async-start | bytes 524288
Sparse Core Ops, SparseCore 0:
  11.5 130.8 reduce-scatter.7
  146.0 128.0 reduce-scatter.5
  277.7 128.0 reduce-scatter.3
  408.0 102.9 all-gather.7
  513.3 102.9 all-gather.5
  618.5 102.9 all-gather.3
where the time goes:
time: 771 us
  waiting for transfers between devices  682 us (88%)
  local copies, waits for them, and re-layouts  42.6 us (6%)
  other arithmetic  32.5 us (4%)
  between operations  14.1 us (2%)
    reduce_scatter x3, waiting for transfers between devices, step(): lax.psum_scatter(t[0], 'dp', scatter_dimension=1, tiled=True)  374 us
    all_gather x3, waiting for transfers between devices, step(): whole = [lax.all_gather(one[0], 'dp', axis=1, tiled=True) for one in new]  305 us
    unnamed x17, local copies, waits for them, and re-layouts  42.6 us
    convert_element_type x3, other arithmetic, adamw(): return ((w - 0.02 * step).astype(jnp.bfloat16), m, v)  32.5 us
  transfers between devices with their start and end apart: 6, of which 6 were waited for; matrix products, arithmetic and copies ran while one was open for 4% of the time, Pallas kernels for 0%

commit v1 on v0

v1 whole, which is shorter than its diff:
```python
import functools

import jax
import jax.numpy as jnp
from jax import lax
from jax.experimental import pallas as pl
from jax.experimental.pallas import tpu as pltpu
from jax.sharding import PartitionSpec as P

MESH = pl.DeviceIdType.MESH
LAG = 2


def chunk_list(rows_of, weights, layers):
    out = []
    pairs = [(w, l) for w in range(weights) for l in range(layers)]
    for i, (w, l) in enumerate(pairs):
        unit = rows_of[w] // 9
        parts = [3, 3, 3]
        if i == 0:
            parts = [1, 2, 3, 3]
        if i == len(pairs) - 1:
            parts = [3, 3, 2, 1]
        first = 0
        for p in parts:
            out.append((w, l, first * unit, p * unit))
            first += p
    return out


class Copies:
    def __init__(self, send, recv, local):
        self.send, self.recv, self.local = send, recv, local
        self.ids, self.nlocal, self.remote, self.here = {}, 0, {}, {}

    def start_remote(self, key, src, dst, peer):
        n = self.ids.setdefault(key, len(self.ids))
        c = pltpu.make_async_remote_copy(src, dst, self.send.at[n], self.recv.at[n], device_id={"dp": peer}, device_id_type=MESH)
        c.start()
        self.remote[key] = [c, True, True]

    def wait_recv(self, key):
        c = self.remote[key]
        assert c[2]
        c[0].wait_recv()
        c[2] = False

    def wait_send(self, key):
        c = self.remote.get(key)
        if c is not None and c[1]:
            c[0].wait_send()
            c[1] = False

    def start(self, key, slot, src, dst):
        c = pltpu.make_async_copy(src, dst, self.local.at[slot])
        c.start()
        self.here[key] = c

    def wait(self, key):
        c = self.here.pop(key, None)
        if c is not None:
            c.wait()

    def drain(self):
        for c in self.here.values():
            c.wait()
        for c in self.remote.values():
            if c[1]:
                c[0].wait_send()
            if c[2]:
                c[0].wait_recv()


OWN, PART, SENDA, KEEPA, RECVA, SENDB, KEEPB, RECVB, GOUT, WNEW = 2, 2, 3, 3, 1, 2, 3, 1, 2, 4
L_OWN, L_PART, L_RECVA, L_RECVB, L_M, L_V, L_W, L_G, L_WN, L_ALL = 0, 2, 4, 5, 6, 7, 8, 9, 11, 15


def body(chunks, group, kinds, *refs):
    g, w, m, v = refs[0:3], refs[3:6], refs[6:9], refs[9:12]
    wn, gs, pland, aland, bland = refs[12:15], refs[15:18], refs[18:21], refs[21:24], refs[24:27]
    bufs = (refs[27:40], refs[40:53])
    send, recv, local = refs[53:56]

    me = lax.axis_index("dp")
    x, y, c = me // 4, (me // 2) % 2, me % 2
    xy = 2 * x + y
    peer_x, peer_y, mate = me + 4 - 8 * x, me + 2 - 4 * y, me + 1 - 2 * c
    peer_a = peer_x + c * (peer_y - peer_x)
    peer_b = peer_y + c * (peer_x - peer_y)
    xy_x, xy_y = xy + 2 - 4 * x, xy + 1 - 2 * y
    xy_a = xy_x + c * (xy_y - xy_x)
    xy_b = xy_y + c * (xy_x - xy_y)
    xy_ab = 3 - xy

    barrier = pltpu.get_barrier_semaphore()
    for peer in (peer_a, peer_b, mate):
        pl.semaphore_signal(barrier, inc=1, device_id={"dp": peer}, device_id_type=MESH)
    pl.semaphore_wait(barrier, 3)

    cp = Copies(send, recv, local)
    count = len(chunks)

    def at(k):
        wi, layer, first, rows = chunks[k]
        return wi, layer, pl.ds(first, rows), rows, bufs[kinds[wi]], group[wi]

    def exchange(k):
        wi, layer, rs, _, _, _ = at(k)
        cp.start_remote(("d", k), g[wi].at[layer, :, 1 - c, rs, :], pland[wi].at[layer, :, rs, :], mate)

    def load_terms(k):
        wi, layer, rs, rows, b, _ = at(k)
        cp.wait_recv(("d", k))
        cp.start(("own", k), L_OWN + k % OWN, g[wi].at[layer, :, c, rs, :], b[0].at[k % OWN, :, pl.ds(0, rows), :])
        cp.start(("part", k), L_PART + k % PART, pland[wi].at[layer, :, rs, :], b[1].at[k % PART, :, pl.ds(0, rows), :])

    def load_a(k):
        wi, layer, rs, rows, b, _ = at(k)
        cp.wait_recv(("a", k))
        cp.start(("recva", k), L_RECVA, aland[wi].at[layer, :, rs, :], b[4].at[:, pl.ds(0, rows), :])

    def load_b(k):
        wi, layer, rs, rows, b, _ = at(k)
        top = pl.ds(0, rows)
        cp.start(("m", k), L_M, m[wi].at[layer, rs, :], b[8].at[top, :])
        cp.start(("v", k), L_V, v[wi].at[layer, rs, :], b[9].at[top, :])
        cp.start(("w", k), L_W, w[wi].at[layer, xy, c, rs, :], b[10].at[top, :])
        cp.wait_recv(("b", k))
        cp.start(("recvb", k), L_RECVB, bland[wi].at[layer, rs, :], b[7].at[top, :])

    def forward_b(k):
        wi, layer, rs, _, _, _ = at(k)
        cp.wait_recv(("gb", k))
        part = wn[wi].at[layer, xy_b, c, rs, :]
        cp.start_remote(("gab", k), part, part, peer_a)
        cp.start_remote(("mb", k), part, part, mate)

    def forward_a(k):
        wi, layer, rs, _, _, _ = at(k)
        for kind, place in (("ga", xy_a), ("gab", xy_ab)):
            cp.wait_recv((kind, k))
            part = wn[wi].at[layer, place, c, rs, :]
            cp.start_remote(("m" + kind, k), part, part, mate)

    def sum_mates(k):
        wi, layer, rs, rows, b, step = at(k)
        own, part, senda, keepa = b[0], b[1], b[2], b[3]
        cp.wait(("own", k))
        cp.wait(("part", k))
        cp.wait_send(("a", k - SENDA))
        so, sp, ss, sk = k % OWN, k % PART, k % SENDA, k % KEEPA

        def sums(i, _):
            r = pl.ds(pl.multiple_of(i * step, step), step)
            for j, place in ((0, xy_ab), (1, xy_a)):
                t = own[so, place, r, :].astype(jnp.float32) + part[sp, place, r, :].astype(jnp.float32)
                senda[ss, j, r, :] = t.astype(jnp.bfloat16)
            for j, place in ((0, xy_b), (1, xy)):
                t = own[so, place, r, :].astype(jnp.float32) + part[sp, place, r, :].astype(jnp.float32)
                keepa[sk, j, r, :] = t
            return 0

        lax.fori_loop(0, rows // step, sums, 0)
        cp.start_remote(("a", k), senda.at[ss, :, pl.ds(0, rows), :], aland[wi].at[layer, :, rs, :], peer_a)

    def sum_a(k):
        wi, layer, rs, rows, b, step = at(k)
        keepa, recva, sendb, keepb = b[3], b[4], b[5], b[6]
        cp.wait(("recva", k))
        cp.wait_send(("b", k - SENDB))
        sk, ss, sb = k % KEEPA, k % SENDB, k % KEEPB

        def sums(i, _):
            r = pl.ds(pl.multiple_of(i * step, step), step)
            sendb[ss, r, :] = (keepa[sk, 0, r, :] + recva[0, r, :].astype(jnp.float32)).astype(jnp.bfloat16)
            keepb[sb, r, :] = keepa[sk, 1, r, :] + recva[1, r, :].astype(jnp.float32)
            return 0

        lax.fori_loop(0, rows // step, sums, 0)
        cp.start_remote(("b", k), sendb.at[ss, pl.ds(0, rows), :], bland[wi].at[layer, rs, :], peer_b)

    def update(k):
        wi, layer, rs, rows, b, step = at(k)
        keepb, recvb, mb, vb, wb, gb, nb = b[6], b[7], b[8], b[9], b[10], b[11], b[12]
        for kind in ("recvb", "m", "v", "w"):
            cp.wait((kind, k))
        cp.wait(("gout", k - GOUT))
        cp.wait(("wout", k - WNEW))
        for kind in ("gb", "ga", "mo"):
            cp.wait_send((kind, k - WNEW))
        sb, sg, sn = k % KEEPB, k % GOUT, k % WNEW

        def new(i, _):
            r = pl.ds(pl.multiple_of(i * step, step), step)
            total = (keepb[sb, r, :] + recvb[r, :].astype(jnp.float32)).astype(jnp.bfloat16)
            gb[sg, r, :] = total
            gf = total.astype(jnp.float32)
            m1 = 0.9 * mb[r, :] + 0.1 * gf
            v1 = 0.95 * vb[r, :] + 0.05 * gf * gf
            w0 = wb[r, :].astype(jnp.float32)
            nb[sn, r, :] = (w0 - 0.02 * (m1 * lax.rsqrt(v1 + 1e-8) + 0.1 * w0)).astype(jnp.bfloat16)
            return 0

        lax.fori_loop(0, rows // step, new, 0)
        top = pl.ds(0, rows)
        src, dst = nb.at[sn, top, :], wn[wi].at[layer, xy, c, rs, :]
        cp.start_remote(("gb", k), src, dst, peer_b)
        cp.start_remote(("ga", k), src, dst, peer_a)
        cp.start_remote(("mo", k), src, dst, mate)
        cp.start(("wout", k), L_WN + sn, src, dst)
        cp.start(("gout", k), L_G + sg, gb.at[sg, top, :], gs[wi].at[layer, rs, :])

    def when(k, f):
        if 0 <= k < count:
            f(k)

    when(0, exchange)
    when(1, exchange)
    when(0, load_terms)
    for s in range(count + 4 * LAG):
        when(s + 2, exchange)
        when(s + 1, load_terms)
        when(s - LAG, load_a)
        when(s - 2 * LAG, load_b)
        when(s - 3 * LAG, forward_b)
        when(s - 4 * LAG, forward_a)
        when(s, sum_mates)
        when(s - LAG, sum_a)
        when(s - 2 * LAG, update)
    cp.drain()


def solution(mesh):
    n = mesh.shape["dp"]

    def step(*arrays):
        terms, weights, m, v = (arrays[i : i + 3] for i in (0, 3, 6, 9))
        layers = weights[0].shape[0]
        rows = [one.shape[1] for one in m]
        cols = [one.shape[2] for one in m]
        kinds, shapes = [], []
        for one in zip(rows, cols):
            if one not in shapes:
                shapes.append(one)
            kinds.append(shapes.index(one))
        group = [r // 9 for r in rows]
        chunks = chunk_list(rows, 3, layers)

        def blocks(a, r):
            return a.reshape(layers, n // 2, 2, r, a.shape[-1])

        gb = [blocks(t[0], r) for t, r in zip(terms, rows)]
        wb = [blocks(t, r) for t, r in zip(weights, rows)]
        bf, f32 = jnp.bfloat16, jnp.float32
        out = [jax.ShapeDtypeStruct((layers, n // 2, 2, r, q), bf) for r, q in zip(rows, cols)]
        out += [jax.ShapeDtypeStruct((layers, r, q), bf) for r, q in zip(rows, cols)]
        out += [jax.ShapeDtypeStruct((layers, n // 2, r, q), bf) for r, q in zip(rows, cols)]
        out += [jax.ShapeDtypeStruct((layers, 2, r, q), bf) for r, q in zip(rows, cols)]
        out += [jax.ShapeDtypeStruct((layers, r, q), bf) for r, q in zip(rows, cols)]
        scratch = []
        for r, q in shapes:
            u = (r // 3, q)
            scratch += [
                pltpu.VMEM((OWN, n // 2, *u), bf),
                pltpu.VMEM((PART, n // 2, *u), bf),
                pltpu.VMEM((SENDA, 2, *u), bf),
                pltpu.VMEM((KEEPA, 2, *u), f32),
                pltpu.VMEM((2, *u), bf),
                pltpu.VMEM((SENDB, *u), bf),
                pltpu.VMEM((KEEPB, *u), f32),
                pltpu.VMEM(u, bf),
                pltpu.VMEM(u, f32),
                pltpu.VMEM(u, f32),
                pltpu.VMEM(u, bf),
                pltpu.VMEM((GOUT, *u), bf),
                pltpu.VMEM((WNEW, *u), bf),
            ]
        copies = 10 * len(chunks)
        scratch += [pltpu.SemaphoreType.DMA((copies,)), pltpu.SemaphoreType.DMA((copies,)), pltpu.SemaphoreType.DMA((L_ALL,))]
        hbm = pl.BlockSpec(memory_space=pl.ANY)
        res = pl.pallas_call(
            functools.partial(body, chunks, group, kinds),
            out_shape=out,
            in_specs=[hbm] * 12,
            out_specs=[hbm] * len(out),
            scratch_shapes=scratch,
            compiler_params=pltpu.CompilerParams(collective_id=0, has_side_effects=True, vmem_limit_bytes=60 * 2**20),
            name="sum_step_gather",
        )(*gb, *wb, *m, *v)
        whole = [one.reshape(w.shape) for one, w in zip(res[0:3], weights)]
        total = [one.astype(f32) for one in res[3:6]]
        new_m = [0.9 * a + 0.1 * t for a, t in zip(m, total)]
        new_v = [0.95 * a + 0.05 * t * t for a, t in zip(v, total)]
        return (*whole, *new_m, *new_v)

    all_of, cut = P(None, None, None), P(None, "dp", None)
    return jax.shard_map(
        step,
        mesh=mesh,
        in_specs=(P(("rep", "dp"), None, None, None),) * 3 + (all_of,) * 3 + (cut,) * 6,
        out_specs=(P("rep", None, None),) * 3 + (P("rep", "dp", None),) * 6,
        check_vma=False,
    )
```

time: 771 us -> 598 us (0.78)
  waiting for transfers between devices: 682 us -> 0 us
  Pallas kernels: 0 us -> 526 us
  between operations: 14.1 us -> 0.72 us
    pallas_call x0 -> x1, Pallas kernels: none -> 526 us  [step(): pl.pallas_call(functools.partial(body, chunks, group, kinds), out_shape=o...]
    reduce_scatter x3 -> x0, waiting for transfers between devices: 374 us -> none  [step(): lax.psum_scatter(t[0], 'dp', scatter_dimension=1, tiled=True)]
    all_gather x3 -> x0, waiting for transfers between devices: 305 us -> none  [step(): whole = [lax.all_gather(one[0], 'dp', axis=1, tiled=True) for one in new]]
    convert_element_type x3 -> x0, other arithmetic: 32.5 us -> none  [adamw(): return ((w - 0.02 * step).astype(jnp.bfloat16), m, v)]
    add x0 -> x2, other arithmetic: none -> 24.8 us  [step(): new_v = [0.95 * a + 0.05 * t * t for a, t in zip(v, total)]]
    unnamed x17 -> x19, local copies, waits for them, and re-layouts: 42.6 us -> 45.8 us
  transfers between devices with their start and end apart: 6 -> 0, of which waited for: 6 -> 0; matrix products, arithmetic and copies ran while one was open for 4% -> 0% of each run, Pallas kernels for 0% -> 0%
where the time goes in v1:
time: 598 us; the launch traced here: 597 us
  Pallas kernels  526 us (88%)
  local copies, waits for them, and re-layouts  45.8 us (8%)
  other arithmetic  24.8 us (4%)
    pallas_call x1, Pallas kernels, step(): pl.pallas_call(functools.partial(body, chunks, group, kinds), out_shape=o...  526 us
    unnamed x19, local copies, waits for them, and re-layouts  45.8 us
    add x2, other arithmetic, step(): new_v = [0.95 * a + 0.05 * t * t for a, t in zip(v, total)]  24.8 us

profile of v1, /device:TPU:0, one launch (start us, length us, event | category | flops | bytes accessed | tf_op | source)
XLA Modules:
  0.0 597.2 jit_solution(15866028846418772299)
XLA Ops:
  0.6 525.9 %sum_step_gather.1 = (bf16[2,4,2,144,4608]{4,3,2,1,0:T(8,128)(2,1)}, bf16[2,4,2,144,4608]{4,3,2,1,0:T(8,128)(2,1)}, bf16[2,4,2,576,1152]{4,3,2,1,0:T(8,128)(2,1)...) custom-call(bf16[2,4,2,144,4608]{4,3,2,1,0:T(8,128)(2,1)} %bitcast.1, ...), custom_call_target="tpu_custom_call" | custom-call | tf_op jit(solution)/shard_map/sum_step_gather/pallas_call | solution.py:281
  526.6 0.0 copy-start
  526.6 0.0 copy-start.1
  526.6 10.6 %fusion.5 = (f32[2,576,1152]{2,1,0:T(8,128)}, f32[2,576,1152]{2,1,0:T(8,128)}) fusion(bf16[2,576,1152]{2,1,0:T(8,128)(2,1)} %get-tuple-element.20, f32[2,576,1152]{2,1,0:T(8,128)} %refs_11_.1, f32[2,576,1152]{2,1,0:T(8,128)} %refs_8_.1), kind=kLoop, calls=%fused_computation.11 | loop fusion | flops 10616832 | bytes 23887872 | tf_op jit(solution)/shard_map/add | solution.py:293
  537.2 0.0 copy-done
  537.2 0.0 copy-done.1
  537.2 14.2 %fusion.3 = (f32[2,144,4608]{2,1,0:T(8,128)}, f32[2,144,4608]{2,1,0:T(8,128)}, f32[2,144,4608]{2,1,0:T(8,128)}, f32[2,144,4608]{2,1,0:T(8,128)}) fusion(bf16[2,144,4608]{2,1,0:T(8,128)(2,1)S(1)} %copy-done.1, f32[2,144,4608]{2,1,0:T(8,128)} %refs_9_.1, f32[2,144,4608]{2,1,0:T(8,128)S(1)} %copy-done, bf16[2,144,4608]{2,1,0:T(8,128)(2,1)} %get-tuple-element.19, ...), kind=kLoop, calls=%fused_computation.9 | loop fusion | flops 21233664 | bytes 47775744 | tf_op jit(solution)/shard_map/add | solution.py:293
  551.4 0.0 slice-start
  551.4 0.0 slice-start.1
  551.4 0.0 slice-start.2
  551.4 19.3 %copy.24 = bf16[2,1152,4608]{2,1,0:T(8,128)(2,1)} copy(bf16[2,1152,4608]{2,1,0:T(8,128)(2,1)} %bitcast.13) | data formatting | bytes 42467328
  570.7 0.0 slice-start.3
  570.7 0.0 slice-start.4
  570.7 0.0 slice-start.5
  570.7 18.8 %copy.25 = bf16[2,1152,4608]{2,1,0:T(8,128)(2,1)} copy(bf16[2,1152,4608]{2,1,0:T(8,128)(2,1)} %bitcast.12) | data formatting | bytes 42467328
  589.5 0.0 slice-done
  589.5 0.0 slice-done.1
  589.5 0.0 slice-done.2
  589.5 0.0 slice-done.3
  589.5 0.0 slice-done.4
  589.5 0.0 slice-done.5
  589.5 7.6 %copy.26 = bf16[2,4608,1152]{2,1,0:T(8,128)(2,1)} copy(bf16[2,4608,1152]{2,1,0:T(8,128)(2,1)S(1)} %bitcast.11) | data formatting | bytes 42467328
  (1 shorter events, 0.0 us)
Async XLA Ops:
  526.6 10.6 %copy-start = (f32[2,144,4608]{2,1,0:T(8,128)S(1)}, f32[2,144,4608]{2,1,0:T(8,128)}, u32[]{:S(2)}) copy-start(f32[2,144,4608]{2,1,0:T(8,128)} %refs_6_.1) | copy-start | bytes 15925252
  526.6 10.6 %copy-start.1 = (bf16[2,144,4608]{2,1,0:T(8,128)(2,1)S(1)}, bf16[2,144,4608]{2,1,0:T(8,128)(2,1)}, u32[]{:S(2)}) copy-start(bf16[2,144,4608]{2,1,0:T(8,128)(2,1)} %get-tuple-element.18) | copy-start | bytes 7962628
  551.4 38.1 %slice-start = ((s8[21233664]{0:T(1024)(128)(4,1)}), s8[4194304]{0:T(1024)(128)(4,1)S(1)}, s32[]{:S(2)}) async-start(s8[21233664]{0:T(1024)(128)(4,1)} %bitcast.9), calls=%async_computation | async-start | bytes 8388608
  551.4 38.1 %slice-start.1 = ((s8[21233664]{0:T(1024)(128)(4,1)}), s8[4194304]{0:T(1024)(128)(4,1)S(1)}, s32[]{:S(2)}) async-start(s8[21233664]{0:T(1024)(128)(4,1)} %bitcast.9), calls=%async_computation.1 | async-start | bytes 8388608
  551.4 38.1 %slice-start.2 = ((s8[21233664]{0:T(1024)(128)(4,1)}), s8[4194304]{0:T(1024)(128)(4,1)S(1)}, s32[]{:S(2)}) async-start(s8[21233664]{0:T(1024)(128)(4,1)} %bitcast.9), calls=%async_computation.2 | async-start | bytes 8388608
  570.7 18.8 %slice-start.3 = ((s8[21233664]{0:T(1024)(128)(4,1)}), s8[4194304]{0:T(1024)(128)(4,1)S(1)}, s32[]{:S(2)}) async-start(s8[21233664]{0:T(1024)(128)(4,1)} %bitcast.9), calls=%async_computation.3 | async-start | bytes 8388608
  570.7 18.8 %slice-start.4 = ((s8[21233664]{0:T(1024)(128)(4,1)}), s8[4194304]{0:T(1024)(128)(4,1)S(1)}, s32[]{:S(2)}) async-start(s8[21233664]{0:T(1024)(128)(4,1)} %bitcast.9), calls=%async_computation.4 | async-start | bytes 8388608
  570.7 18.8 %slice-start.5 = ((s8[21233664]{0:T(1024)(128)(4,1)}), s8[262144]{0:T(1024)(128)(4,1)S(1)}, s32[]{:S(2)}) async-start(s8[21233664]{0:T(1024)(128)(4,1)} %bitcast.9), calls=%async_computation.5 | async-start | bytes 524288

commit v2 on v1

--- a/solution.py
+++ b/solution.py
@@ -6,6 +6,7 @@
 from jax.experimental import pallas as pl
 from jax.experimental.pallas import tpu as pltpu
 from jax.sharding import PartitionSpec as P
+
 
 MESH = pl.DeviceIdType.MESH
 LAG = 2
@@ -71,11 +72,11 @@
                 c[0].wait_recv()
 
 
-OWN, PART, SENDA, KEEPA, RECVA, SENDB, KEEPB, RECVB, GOUT, WNEW = 2, 2, 3, 3, 1, 2, 3, 1, 2, 4
+OWN, PART, SENDA, KEEPA, SENDB, KEEPB, GOUT, WNEW = 2, 2, 3, 3, 2, 3, 2, 4
 L_OWN, L_PART, L_RECVA, L_RECVB, L_M, L_V, L_W, L_G, L_WN, L_ALL = 0, 2, 4, 5, 6, 7, 8, 9, 11, 15
 
 
-def body(chunks, group, kinds, *refs):
+def body(chunks, group, kinds, outside, *refs):
     g, w, m, v = refs[0:3], refs[3:6], refs[6:9], refs[9:12]
     wn, gs, pland, aland, bland = refs[12:15], refs[15:18], refs[18:21], refs[21:24], refs[24:27]
     bufs = (refs[27:40], refs[40:53])
@@ -181,6 +182,7 @@
 
     def update(k):
         wi, layer, rs, rows, b, step = at(k)
+        inside = wi not in outside
         keepb, recvb, mb, vb, wb, gb, nb = b[6], b[7], b[8], b[9], b[10], b[11], b[12]
         for kind in ("recvb", "m", "v", "w"):
             cp.wait((kind, k))
@@ -203,15 +205,19 @@
 
         lax.fori_loop(0, rows // step, new, 0)
         top = pl.ds(0, rows)
-        src, dst = nb.at[sn, top, :], wn[wi].at[layer, xy, c, rs, :]
-        cp.start_remote(("gb", k), src, dst, peer_b)
-        cp.start_remote(("ga", k), src, dst, peer_a)
-        cp.start_remote(("mo", k), src, dst, mate)
+        src = nb.at[sn, top, :]
+        if inside:
+            dst = wn[wi].at[layer, xy, c, rs, :]
+            cp.start_remote(("gb", k), src, dst, peer_b)
+            cp.start_remote(("ga", k), src, dst, peer_a)
+            cp.start_remote(("mo", k), src, dst, mate)
+        else:
+            dst = wn[wi].at[layer, rs, :]
         cp.start(("wout", k), L_WN + sn, src, dst)
         cp.start(("gout", k), L_G + sg, gb.at[sg, top, :], gs[wi].at[layer, rs, :])
 
-    def when(k, f):
-        if 0 <= k < count:
+    def when(k, f, gathers=False):
+        if 0 <= k < count and not (gathers and chunks[k][0] in outside):
             f(k)
 
     when(0, exchange)
@@ -222,18 +228,119 @@
         when(s + 1, load_terms)
         when(s - LAG, load_a)
         when(s - 2 * LAG, load_b)
-        when(s - 3 * LAG, forward_b)
-        when(s - 4 * LAG, forward_a)
+        when(s - 3 * LAG, forward_b, True)
+        when(s - 4 * LAG, forward_a, True)
         when(s, sum_mates)
         when(s - LAG, sum_a)
         when(s - 2 * LAG, update)
     cp.drain()
 
 
+def copy_blocks(a):
+    layers, places, cores, r, q = a.shape
+
+    def kernel(src, dst):
+        dst[...] = src[...]
+
+    spec = pl.BlockSpec((None, None, None, r, q), lambda i, j, k: (i, j, k, 0, 0))
+    return pl.pallas_call(
+        kernel,
+        out_shape=jax.ShapeDtypeStruct(a.shape, a.dtype),
+        grid=(layers, places, cores),
+        in_specs=[spec],
+        out_specs=spec,
+        cost_estimate=pl.CostEstimate(flops=4 * 10**9, bytes_accessed=4 * a.size, transcendentals=0),
+        name="copy_blocks",
+    )(a)
+
+
+def place_blocks(pieces, places, n, into=None):
+    layers, r, q = pieces[0].shape
+    count = len(pieces) * layers
+
+    def kernel(*refs):
+        src = refs[: len(pieces)]
+        dst, buf, sin, sout = refs[-4:]
+        me = lax.axis_index("dp")
+        x, y, c = me // 4, (me // 2) % 2, me % 2
+        loads, stores = [], []
+        for p in range(len(pieces)):
+            xy, core = places[p](x, y, c)
+            for l in range(layers):
+                i = p * layers + l
+                loads.append(pltpu.make_async_copy(src[p].at[l], buf.at[i], sin.at[i]))
+                stores.append(pltpu.make_async_copy(buf.at[i], dst.at[l, xy, core], sout.at[i]))
+        for one in loads:
+            one.start()
+        for one, two in zip(loads, stores):
+            one.wait()
+            two.start()
+        for two in stores:
+            two.wait()
+
+    hbm = pl.BlockSpec(memory_space=pl.ANY)
+    more = [] if into is None else [into]
+    return pl.pallas_call(
+        kernel,
+        out_shape=jax.ShapeDtypeStruct((layers, n // 2, 2, r, q), pieces[0].dtype),
+        in_specs=[hbm] * (len(pieces) + len(more)),
+        out_specs=hbm,
+        scratch_shapes=[
+            pltpu.VMEM((count, r, q), pieces[0].dtype),
+            pltpu.SemaphoreType.DMA((count,)),
+            pltpu.SemaphoreType.DMA((count,)),
+        ],
+        input_output_aliases={len(pieces): 0} if more else {},
+        cost_estimate=pl.CostEstimate(flops=10**9, bytes_accessed=4 * count * r * q, transcendentals=0),
+        name="place_blocks",
+    )(*pieces, *more)
+
+
+def gather(own, n):
+    to_a = [(d, d ^ (2 if d % 2 else 4)) for d in range(n)]
+    to_b = [(d, d ^ (4 if d % 2 else 2)) for d in range(n)]
+    to_mate = [(d, d ^ 1) for d in range(n)]
+
+    def send(what, pairs):
+        return lax.ppermute(what, "dp", pairs)
+
+    from_b = send(own, to_b)
+    from_a = send(own, to_a)
+    mate_own = send(own, to_mate)
+    from_ab = send(from_b, to_a)
+    mate_b = send(from_b, to_mate)
+    mate_a = send(from_a, to_mate)
+    mate_ab = send(from_ab, to_mate)
+
+    def at_x(x, y):
+        return 2 * (1 - x) + y
+
+    def at_y(x, y):
+        return 2 * x + 1 - y
+
+    def a_of(x, y, c):
+        return at_x(x, y) + c * (at_y(x, y) - at_x(x, y))
+
+    def b_of(x, y, c):
+        return at_y(x, y) + c * (at_x(x, y) - at_y(x, y))
+
+    places = [
+        lambda x, y, c: (2 * x + y, c),
+        lambda x, y, c: (a_of(x, y, c), c),
+        lambda x, y, c: (b_of(x, y, c), c),
+        lambda x, y, c: (2 * x + y, 1 - c),
+        lambda x, y, c: (b_of(x, y, c), 1 - c),
+        lambda x, y, c: (a_of(x, y, c), 1 - c),
+    ]
+    first = place_blocks([own, from_a, from_b, mate_own, mate_a, mate_b], places, n)
+    last = [lambda x, y, c: (3 - 2 * x - y, c), lambda x, y, c: (3 - 2 * x - y, 1 - c)]
+    return place_blocks([from_ab, mate_ab], last, n, into=first)
+
+
 def solution(mesh):
     n = mesh.shape["dp"]
 
-    def step(*arrays):
+    def inner(*arrays):
         terms, weights, m, v = (arrays[i : i + 3] for i in (0, 3, 6, 9))
         layers = weights[0].shape[0]
         rows = [one.shape[1] for one in m]
@@ -252,7 +359,8 @@
         gb = [blocks(t[0], r) for t, r in zip(terms, rows)]
         wb = [blocks(t, r) for t, r in zip(weights, rows)]
         bf, f32 = jnp.bfloat16, jnp.float32
-        out = [jax.ShapeDtypeStruct((layers, n // 2, 2, r, q), bf) for r, q in zip(rows, cols)]
+        out = [jax.ShapeDtypeStruct((layers, n // 2, 2, r, q), bf) for r, q in zip(rows[:2], cols)]
+        out += [jax.ShapeDtypeStruct((layers, rows[2], cols[2]), bf)]
         out += [jax.ShapeDtypeStruct((layers, r, q), bf) for r, q in zip(rows, cols)]
         out += [jax.ShapeDtypeStruct((layers, n // 2, r, q), bf) for r, q in zip(rows, cols)]
         out += [jax.ShapeDtypeStruct((layers, 2, r, q), bf) for r, q in zip(rows, cols)]
@@ -279,7 +387,7 @@
         scratch += [pltpu.SemaphoreType.DMA((copies,)), pltpu.SemaphoreType.DMA((copies,)), pltpu.SemaphoreType.DMA((L_ALL,))]
         hbm = pl.BlockSpec(memory_space=pl.ANY)
         res = pl.pallas_call(
-            functools.partial(body, chunks, group, kinds),
+            functools.partial(body, chunks, group, kinds, (2,)),
             out_shape=out,
             in_specs=[hbm] * 12,
             out_specs=[hbm] * len(out),
@@ -287,7 +395,9 @@
             compiler_params=pltpu.CompilerParams(collective_id=0, has_side_effects=True, vmem_limit_bytes=60 * 2**20),
             name="sum_step_gather",
         )(*gb, *wb, *m, *v)
-        whole = [one.reshape(w.shape) for one, w in zip(res[0:3], weights)]
+        whole = [copy_blocks(one) for one in res[0:2]]
+        whole += [gather(res[2], n)]
+        whole = [one.reshape(w.shape) for one, w in zip(whole, weights)]
         total = [one.astype(f32) for one in res[3:6]]
         new_m = [0.9 * a + 0.1 * t for a, t in zip(m, total)]
         new_v = [0.95 * a + 0.05 * t * t for a, t in zip(v, total)]
@@ -295,7 +405,7 @@
 
     all_of, cut = P(None, None, None), P(None, "dp", None)
     return jax.shard_map(
-        step,
+        inner,
         mesh=mesh,
         in_specs=(P(("rep", "dp"), None, None, None),) * 3 + (all_of,) * 3 + (cut,) * 6,
         out_specs=(P("rep", None, None),) * 3 + (P("rep", "dp", None),) * 6,

time: 598 us -> 591 us (0.988)
  waiting for transfers between devices: 0 us -> 60.2 us
  local copies, waits for them, and re-layouts: 45.8 us -> 0.01 us
  Pallas kernels: 526 us -> 499 us
    ppermute x0 -> x7, waiting for transfers between devices: none -> 60.2 us  [send(): return lax.ppermute(what, 'dp', pairs)]
    unnamed x19 -> x4, local copies, waits for them, and re-layouts: 45.8 us -> 0.01 us
    pallas_call x1 -> x5, Pallas kernels: 526 us -> 499 us  [the longest x1 443 us: inner(): pl.pallas_call(functools.partial(body, chunks, group, kinds, (2,)), out_s...]
  transfers between devices with their start and end apart: 0 -> 7, of which waited for: 0 -> 2; matrix products, arithmetic and copies ran while one was open for 0% -> 4% of each run, Pallas kernels for 0% -> 9%
where the time goes in v2:
time: 591 us; the launch traced here: 589 us
  Pallas kernels  499 us (84%)
  waiting for transfers between devices  60.2 us (10%)
  other arithmetic  26.2 us (4%)
    pallas_call x1, Pallas kernels, inner(): pl.pallas_call(functools.partial(body, chunks, group, kinds, (2,)), out_s...  443 us
    ppermute x7, waiting for transfers between devices, send(): return lax.ppermute(what, 'dp', pairs)  60.2 us
    pallas_call x2, Pallas kernels, copy_blocks(): pl.pallas_call(kernel, out_shape=jax.ShapeDtypeStruct(a.shape, a.dtype),...  40.4 us
    add x2, other arithmetic, inner(): new_v = [0.95 * a + 0.05 * t * t for a, t in zip(v, total)]  26.2 us
    pallas_call x2, Pallas kernels, place_blocks(): pl.pallas_call(kernel, out_shape=jax.ShapeDtypeStruct((layers, n // 2, 2,...  15.9 us
  transfers between devices with their start and end apart: 7, of which 2 were waited for; matrix products, arithmetic and copies ran while one was open for 4% of the time, Pallas kernels for 9%

profile of v2, /device:TPU:0, one launch (start us, length us, event | category | flops | bytes accessed | tf_op | source)
XLA Modules:
  0.0 589.4 jit_solution(15934259021381366480)
XLA Ops:
  0.6 443.0 %sum_step_gather.1 = (bf16[2,4,2,144,4608]{4,3,2,1,0:T(8,128)(2,1)}, bf16[2,4,2,144,4608]{4,3,2,1,0:T(8,128)(2,1)}, bf16[2,576,1152]{2,1,0:T(8,128)(2,1)}, bf16[...) custom-call(bf16[2,4,2,144,4608]{4,3,2,1,0:T(8,128)(2,1)} %bitcast.1, ...), custom_call_target="tpu_custom_call" | custom-call | tf_op jit(solution)/shard_map/sum_step_gather/pallas_call | solution.py:389
  443.6 1.0 collective-permute-start
  444.6 0.7 collective-permute-start.3
  445.3 58.9 %collective-permute-done.refs_2_ = bf16[2,576,1152]{2,1,0:T(8,128)(2,1)} collective-permute-done((bf16[2,576,1152]{2,1,0:T(8,128)(2,1)}, bf16[2,576,1152]{2,1,0:T(8,128)(2,1)}, u32[]{:S(2)}, u32[]{:S(2)}) %collective-permute-start) | collective-permute-done | bytes 2654240 | tf_op jit(solution)/shard_map/ppermute | solution.py:305
  504.2 0.6 collective-permute-start.1
  504.8 0.0 collective-permute-start.4
  504.8 0.0 copy-start
  504.8 20.2 %copy_blocks.2 = bf16[2,4,2,144,4608]{4,3,2,1,0:T(8,128)(2,1)} custom-call(bf16[2,4,2,144,4608]{4,3,2,1,0:T(8,128)(2,1)} %get-tuple-element.15.src), custom_call_target="tpu_custom_call" | custom-call | flops 4000000000 | bytes 42467328 | tf_op jit(solution)/shard_map/copy_blocks/pallas_call | solution.py:246
  525.0 0.0 copy-done
  525.0 9.7 %fusion.5 = (f32[2,576,1152]{2,1,0:T(8,128)}, f32[2,576,1152]{2,1,0:T(8,128)}) fusion(bf16[2,576,1152]{2,1,0:T(8,128)(2,1)S(1)} %copy-done, f32[2,576,1152]{2,1,0:T(8,128)} %refs_11_.1, f32[2,576,1152]{2,1,0:T(8,128)} %refs_8_.1), kind=kLoop, calls=%fused_computation.11 | loop fusion | flops 10616832 | bytes 23887872 | tf_op jit(solution)/shard_map/add | solution.py:403
  534.7 0.5 collective-permute-start.6
  535.2 0.0 collective-permute-done.3.refs_1_
  535.2 0.0 collective-permute-start.5
  535.2 1.3 collective-permute-done.1.refs_0_
  536.5 0.0 collective-permute-start.2
  536.5 0.0 copy-start.1
  536.5 20.2 %copy_blocks.3 = bf16[2,4,2,144,4608]{4,3,2,1,0:T(8,128)(2,1)} custom-call(bf16[2,4,2,144,4608]{4,3,2,1,0:T(8,128)(2,1)} %get-tuple-element.16.src), custom_call_target="tpu_custom_call" | custom-call | flops 4000000000 | bytes 42467328 | tf_op jit(solution)/shard_map/copy_blocks/pallas_call | solution.py:246
  556.7 0.0 copy-done.1
  556.7 16.5 %fusion.3 = (f32[2,144,4608]{2,1,0:T(8,128)}, f32[2,144,4608]{2,1,0:T(8,128)}, f32[2,144,4608]{2,1,0:T(8,128)}, f32[2,144,4608]{2,1,0:T(8,128)}) fusion(bf16[2,144,4608]{2,1,0:T(8,128)(2,1)S(1)} %copy-done.1, f32[2,144,4608]{2,1,0:T(8,128)} %refs_9_.1, f32[2,144,4608]{2,1,0:T(8,128)} %refs_6_.1, bf16[2,144,4608]{2,1,0:T(8,128)(2,1)} %get-tuple-element.19, ...), kind=kLoop, calls=%fused_computation.9 | loop fusion | flops 21233664 | bytes 47775744 | tf_op jit(solution)/shard_map/add | solution.py:403
  573.3 0.0 collective-permute-done.4.refs_3_
  573.3 0.0 collective-permute-done.5.refs_4_
  573.3 0.0 collective-permute-done.6.refs_5_
  573.3 11.6 %place_blocks.2.refs_2_ = bf16[2,4,2,576,1152]{4,3,2,1,0:T(8,128)(2,1)} custom-call(bf16[2,576,1152]{2,1,0:T(8,128)(2,1)} %get-tuple-element.17.refs_0_, bf16[2,576,1152]{2,1,0:T(8,128)(2,1)} %collective-permute-done.3.refs_1_, bf16[2,576,1152]{2,1,0:T(8,128)(2,1)} %collective-permute-done.refs_2_, bf16[2,576,1152]{2,1,0:T(8,128)(2,1)} %collective-permute-done.4.refs_3_, ...), custom_call_target="tpu_custom_call" | custom-call | flops 1000000000 | bytes 31850496 | tf_op jit(solution)/shard_map/place_blocks/pallas_call | solution.py:283
  584.9 0.0 collective-permute-done.2.refs_1_
  584.9 4.3 place_blocks.3
Async XLA Ops:
  443.6 60.6 %collective-permute-start = (bf16[2,576,1152]{2,1,0:T(8,128)(2,1)}, bf16[2,576,1152]{2,1,0:T(8,128)(2,1)}, u32[]{:S(2)}, u32[]{:S(2)}) collective-permute-start(bf16[2,576,1152]{2,1,0:T(8,128)(2,1)} %get-tuple-element.17.refs_0_), channel_id=1, source_target_pairs={{0,2},{1,5},{2,0},{3,7},{4,6},{5,1},{6,4},{7,3}} | collective-permute-start | bytes 7962632 | tf_op jit(solution)/shard_map/ppermute | solution.py:305
  444.6 90.5 %collective-permute-start.3 = (bf16[2,576,1152]{2,1,0:T(8,128)(2,1)}, bf16[2,576,1152]{2,1,0:T(8,128)(2,1)}, u32[]{:S(2)}, u32[]{:S(2)}) collective-permute-start(bf16[2,576,1152]{2,1,0:T(8,128)(2,1)} %get-tuple-element.17.refs_0_), channel_id=1, source_target_pairs={{0,4},{1,3},{2,6},{3,1},{4,0},{5,7},{6,2},{7,5}} | collective-permute-start | bytes 7962632 | tf_op jit(solution)/shard_map/ppermute | solution.py:305
  504.2 32.3 %collective-permute-start.1 = (bf16[2,576,1152]{2,1,0:T(8,128)(2,1)}, bf16[2,576,1152]{2,1,0:T(8,128)(2,1)}, u32[]{:S(2)}, u32[]{:S(2)}) collective-permute-start(bf16[2,576,1152]{2,1,0:T(8,128)(2,1)} %collective-permute-done.refs_2_), channel_id=1, source_target_pairs={{0,4},{1,3},{2,6},{3,1},{4,0},{5,7},{6,2},{7,5}} | collective-permute-start | bytes 7962632 | tf_op jit(solution)/shard_map/ppermute | solution.py:305
  504.8 68.5 %collective-permute-start.4 = (bf16[2,576,1152]{2,1,0:T(8,128)(2,1)}, bf16[2,576,1152]{2,1,0:T(8,128)(2,1)}, u32[]{:S(2)}, u32[]{:S(2)}) collective-permute-start(bf16[2,576,1152]{2,1,0:T(8,128)(2,1)} %get-tuple-element.17.refs_0_), channel_id=1, source_target_pairs={{0,1},{1,0},{2,3},{3,2},{4,5},{5,4},{6,7},{7,6}} | collective-permute-start | bytes 7962632 | tf_op jit(solution)/shard_map/ppermute | solution.py:305
  504.8 20.2 %copy-start = (bf16[2,576,1152]{2,1,0:T(8,128)(2,1)S(1)}, bf16[2,576,1152]{2,1,0:T(8,128)(2,1)}, u32[]{:S(2)}) copy-start(bf16[2,576,1152]{2,1,0:T(8,128)(2,1)} %get-tuple-element.20) | copy-start | bytes 7962628
  534.7 38.6 %collective-permute-start.6 = (bf16[2,576,1152]{2,1,0:T(8,128)(2,1)}, bf16[2,576,1152]{2,1,0:T(8,128)(2,1)}, u32[]{:S(2)}, u32[]{:S(2)}) collective-permute-start(bf16[2,576,1152]{2,1,0:T(8,128)(2,1)} %collective-permute-done.refs_2_), channel_id=1, source_target_pairs={{0,1},{1,0},{2,3},{3,2},{4,5},{5,4},{6,7},{7,6}} | collective-permute-start | bytes 7962632 | tf_op jit(solution)/shard_map/ppermute | solution.py:305
  535.2 38.1 %collective-permute-start.5 = (bf16[2,576,1152]{2,1,0:T(8,128)(2,1)}, bf16[2,576,1152]{2,1,0:T(8,128)(2,1)}, u32[]{:S(2)}, u32[]{:S(2)}) collective-permute-start(bf16[2,576,1152]{2,1,0:T(8,128)(2,1)} %collective-permute-done.3.refs_1_), channel_id=1, source_target_pairs={{0,1},{1,0},{2,3},{3,2},{4,5},{5,4},{6,7},{7,6}} | collective-permute-start | bytes 7962632 | tf_op jit(solution)/shard_map/ppermute | solution.py:305
  536.5 48.4 %collective-permute-start.2 = (bf16[2,576,1152]{2,1,0:T(8,128)(2,1)}, bf16[2,576,1152]{2,1,0:T(8,128)(2,1)}, u32[]{:S(2)}, u32[]{:S(2)}) collective-permute-start(bf16[2,576,1152]{2,1,0:T(8,128)(2,1)} %collective-permute-done.1.refs_0_), channel_id=1, source_target_pairs={{0,1},{1,0},{2,3},{3,2},{4,5},{5,4},{6,7},{7,6}} | collective-permute-start | bytes 7962632 | tf_op jit(solution)/shard_map/ppermute | solution.py:305
  536.5 20.2 %copy-start.1 = (bf16[2,144,4608]{2,1,0:T(8,128)(2,1)S(1)}, bf16[2,144,4608]{2,1,0:T(8,128)(2,1)}, u32[]{:S(2)}) copy-start(bf16[2,144,4608]{2,1,0:T(8,128)(2,1)} %get-tuple-element.18) | copy-start | bytes 7962628

commit v3 on v2

--- a/solution.py
+++ b/solution.py
@@ -73,14 +73,15 @@
 
 
 OWN, PART, SENDA, KEEPA, SENDB, KEEPB, GOUT, WNEW = 2, 2, 3, 3, 2, 3, 2, 4
-L_OWN, L_PART, L_RECVA, L_RECVB, L_M, L_V, L_W, L_G, L_WN, L_ALL = 0, 2, 4, 5, 6, 7, 8, 9, 11, 15
-
-
-def body(chunks, group, kinds, outside, *refs):
+L_OWN, L_PART, L_RECVA, L_RECVB, L_M, L_V, L_W, L_G, L_WN, L_AG, L_ALL = 0, 2, 4, 5, 6, 7, 8, 9, 11, 15, 19
+
+
+def body(chunks, group, kinds, outside, firsts, *refs):
     g, w, m, v = refs[0:3], refs[3:6], refs[6:9], refs[9:12]
-    wn, gs, pland, aland, bland = refs[12:15], refs[15:18], refs[18:21], refs[21:24], refs[24:27]
-    bufs = (refs[27:40], refs[40:53])
-    send, recv, local = refs[53:56]
+    own_block, own_pieces, refs = refs[12], refs[13 : 13 + len(firsts)], refs[:12] + refs[13 + len(firsts) :]
+    wn, gs, pland, aland, bland = refs[12:14], refs[14:17], refs[17:20], refs[20:23], refs[23:26]
+    bufs = (refs[26:39], refs[39:52])
+    last_a, last_b, send, recv, local = refs[52:57]
 
     me = lax.axis_index("dp")
     x, y, c = me // 4, (me // 2) % 2, me % 2
@@ -107,17 +108,23 @@
 
     def exchange(k):
         wi, layer, rs, _, _, _ = at(k)
-        cp.start_remote(("d", k), g[wi].at[layer, :, 1 - c, rs, :], pland[wi].at[layer, :, rs, :], mate)
+        land = pland[wi].at[layer, :, rs, :]
+        if k < PART:
+            land = bufs[kinds[wi]][1].at[k, :, pl.ds(0, chunks[k][3]), :]
+        cp.start_remote(("d", k), g[wi].at[layer, :, 1 - c, rs, :], land, mate)
 
     def load_terms(k):
         wi, layer, rs, rows, b, _ = at(k)
+        cp.start(("own", k), L_OWN + k % OWN, g[wi].at[layer, :, c, rs, :], b[0].at[k % OWN, :, pl.ds(0, rows), :])
         cp.wait_recv(("d", k))
-        cp.start(("own", k), L_OWN + k % OWN, g[wi].at[layer, :, c, rs, :], b[0].at[k % OWN, :, pl.ds(0, rows), :])
-        cp.start(("part", k), L_PART + k % PART, pland[wi].at[layer, :, rs, :], b[1].at[k % PART, :, pl.ds(0, rows), :])
+        if k >= PART:
+            cp.start(("part", k), L_PART + k % PART, pland[wi].at[layer, :, rs, :], b[1].at[k % PART, :, pl.ds(0, rows), :])
 
     def load_a(k):
         wi, layer, rs, rows, b, _ = at(k)
         cp.wait_recv(("a", k))
+        if k == count - 1:
+            return
         cp.start(("recva", k), L_RECVA, aland[wi].at[layer, :, rs, :], b[4].at[:, pl.ds(0, rows), :])
 
     def load_b(k):
@@ -127,7 +134,8 @@
         cp.start(("v", k), L_V, v[wi].at[layer, rs, :], b[9].at[top, :])
         cp.start(("w", k), L_W, w[wi].at[layer, xy, c, rs, :], b[10].at[top, :])
         cp.wait_recv(("b", k))
-        cp.start(("recvb", k), L_RECVB, bland[wi].at[layer, rs, :], b[7].at[top, :])
+        if k < count - 1:
+            cp.start(("recvb", k), L_RECVB, bland[wi].at[layer, rs, :], b[7].at[top, :])
 
     def forward_b(k):
         wi, layer, rs, _, _, _ = at(k)
@@ -162,7 +170,7 @@
             return 0
 
         lax.fori_loop(0, rows // step, sums, 0)
-        cp.start_remote(("a", k), senda.at[ss, :, pl.ds(0, rows), :], aland[wi].at[layer, :, rs, :], peer_a)
+        cp.start_remote(("a", k), senda.at[ss, :, pl.ds(0, rows), :], last_a if k == count - 1 else aland[wi].at[layer, :, rs, :], peer_a)
 
     def sum_a(k):
         wi, layer, rs, rows, b, step = at(k)
@@ -170,6 +178,7 @@
         cp.wait(("recva", k))
         cp.wait_send(("b", k - SENDB))
         sk, ss, sb = k % KEEPA, k % SENDB, k % KEEPB
+        recva = last_a if k == count - 1 else recva
 
         def sums(i, _):
             r = pl.ds(pl.multiple_of(i * step, step), step)
@@ -178,7 +187,7 @@
             return 0
 
         lax.fori_loop(0, rows // step, sums, 0)
-        cp.start_remote(("b", k), sendb.at[ss, pl.ds(0, rows), :], bland[wi].at[layer, rs, :], peer_b)
+        cp.start_remote(("b", k), sendb.at[ss, pl.ds(0, rows), :], last_b if k == count - 1 else bland[wi].at[layer, rs, :], peer_b)
 
     def update(k):
         wi, layer, rs, rows, b, step = at(k)
@@ -188,9 +197,11 @@
             cp.wait((kind, k))
         cp.wait(("gout", k - GOUT))
         cp.wait(("wout", k - WNEW))
+        cp.wait(("again", k - WNEW))
         for kind in ("gb", "ga", "mo"):
             cp.wait_send((kind, k - WNEW))
         sb, sg, sn = k % KEEPB, k % GOUT, k % WNEW
+        recvb = last_b if k == count - 1 else recvb
 
         def new(i, _):
             r = pl.ds(pl.multiple_of(i * step, step), step)
@@ -209,67 +220,60 @@
         if inside:
             dst = wn[wi].at[layer, xy, c, rs, :]
             cp.start_remote(("gb", k), src, dst, peer_b)
-            cp.start_remote(("ga", k), src, dst, peer_a)
+            if k != late:
+                cp.start_remote(("ga", k), src, dst, peer_a)
             cp.start_remote(("mo", k), src, dst, mate)
         else:
-            dst = wn[wi].at[layer, rs, :]
+            first = layer * m[wi].shape[1] + chunks[k][2]
+            i = sum(first >= one for one in firsts) - 1
+            dst = own_pieces[i].at[pl.ds(first - firsts[i], rows), :]
+            cp.start(("again", k), L_AG + sn, src, own_block.at[pl.ds(first, rows), :])
         cp.start(("wout", k), L_WN + sn, src, dst)
         cp.start(("gout", k), L_G + sg, gb.at[sg, top, :], gs[wi].at[layer, rs, :])
 
+    late = max(k for k in range(count) if chunks[k][0] not in outside)
+
+    def send_late():
+        wi, layer, rs, rows, b, _ = at(late)
+        cp.start_remote(("ga", late), b[12].at[late % WNEW, pl.ds(0, rows), :], wn[wi].at[layer, xy, c, rs, :], peer_a)
+        forward_b(late)
+
     def when(k, f, gathers=False):
-        if 0 <= k < count and not (gathers and chunks[k][0] in outside):
+        if 0 <= k < count and not (gathers and (chunks[k][0] in outside or k == late)):
             f(k)
 
     when(0, exchange)
     when(1, exchange)
     when(0, load_terms)
     for s in range(count + 4 * LAG):
+        if s < 2:
+            sum_mates(s)
         when(s + 2, exchange)
         when(s + 1, load_terms)
         when(s - LAG, load_a)
         when(s - 2 * LAG, load_b)
         when(s - 3 * LAG, forward_b, True)
         when(s - 4 * LAG, forward_a, True)
-        when(s, sum_mates)
+        if s >= 2:
+            when(s, sum_mates)
         when(s - LAG, sum_a)
         when(s - 2 * LAG, update)
+        if s == count - 1:
+            send_late()
+    forward_a(late)
     cp.drain()
 
 
 def copy_blocks(a):
     layers, places, cores, r, q = a.shape
-
-    def kernel(src, dst):
-        dst[...] = src[...]
-
-    spec = pl.BlockSpec((None, None, None, r, q), lambda i, j, k: (i, j, k, 0, 0))
-    return pl.pallas_call(
-        kernel,
-        out_shape=jax.ShapeDtypeStruct(a.shape, a.dtype),
-        grid=(layers, places, cores),
-        in_specs=[spec],
-        out_specs=spec,
-        cost_estimate=pl.CostEstimate(flops=4 * 10**9, bytes_accessed=4 * a.size, transcendentals=0),
-        name="copy_blocks",
-    )(a)
-
-
-def place_blocks(pieces, places, n, into=None):
-    layers, r, q = pieces[0].shape
-    count = len(pieces) * layers
-
-    def kernel(*refs):
-        src = refs[: len(pieces)]
-        dst, buf, sin, sout = refs[-4:]
-        me = lax.axis_index("dp")
-        x, y, c = me // 4, (me // 2) % 2, me % 2
-        loads, stores = [], []
-        for p in range(len(pieces)):
-            xy, core = places[p](x, y, c)
-            for l in range(layers):
-                i = p * layers + l
-                loads.append(pltpu.make_async_copy(src[p].at[l], buf.at[i], sin.at[i]))
-                stores.append(pltpu.make_async_copy(buf.at[i], dst.at[l, xy, core], sout.at[i]))
+    count = layers * places * cores
+
+    def kernel(src, dst, buf, sin, sout):
+        def where(i):
+            return i // (places * cores), (i // cores) % places, i % cores
+
+        loads = [pltpu.make_async_copy(src.at[where(i)], buf.at[i], sin.at[i]) for i in range(count)]
+        stores = [pltpu.make_async_copy(buf.at[i], dst.at[where(i)], sout.at[i]) for i in range(count)]
         for one in loads:
             one.start()
         for one, two in zip(loads, stores):
@@ -279,34 +283,71 @@
             two.wait()
 
     hbm = pl.BlockSpec(memory_space=pl.ANY)
+    return pl.pallas_call(
+        kernel,
+        out_shape=jax.ShapeDtypeStruct(a.shape, a.dtype),
+        in_specs=[hbm],
+        out_specs=hbm,
+        scratch_shapes=[pltpu.VMEM((count, r, q), a.dtype), pltpu.SemaphoreType.DMA((count,)), pltpu.SemaphoreType.DMA((count,))],
+        cost_estimate=pl.CostEstimate(flops=4 * 10**9, bytes_accessed=4 * a.size, transcendentals=0),
+        compiler_params=pltpu.CompilerParams(vmem_limit_bytes=24 * 2**20),
+        name="copy_blocks",
+    )(a)
+
+
+def place_blocks(items, shape, into=None):
+    _, _, _, r, q = shape
+    jobs = []
+    for i, (one, first, place) in enumerate(items):
+        done = 0
+        while done < one.shape[0]:
+            layer, row = divmod(first + done, r)
+            take = min(one.shape[0] - done, r - row)
+            jobs.append((i, done, layer, row, take, place))
+            done += take
+
+    def kernel(*refs):
+        dst, sems = refs[-2:]
+        me = lax.axis_index("dp")
+        x, y, c = me // 4, (me // 2) % 2, me % 2
+        stores = []
+        for n, (i, done, layer, row, take, place) in enumerate(jobs):
+            xy, core = place(x, y, c)
+            part = refs[i].at[pl.ds(done, take), :]
+            stores.append(pltpu.make_async_copy(part, dst.at[layer, xy, core, pl.ds(row, take), :], sems.at[n]))
+        for one in stores:
+            one.start()
+        for one in stores:
+            one.wait()
+
+    hbm = pl.BlockSpec(memory_space=pl.ANY)
     more = [] if into is None else [into]
     return pl.pallas_call(
         kernel,
-        out_shape=jax.ShapeDtypeStruct((layers, n // 2, 2, r, q), pieces[0].dtype),
-        in_specs=[hbm] * (len(pieces) + len(more)),
+        out_shape=jax.ShapeDtypeStruct(shape, items[0][0].dtype),
+        in_specs=[pl.BlockSpec(memory_space=pltpu.VMEM)] * len(items) + [hbm] * len(more),
         out_specs=hbm,
-        scratch_shapes=[
-            pltpu.VMEM((count, r, q), pieces[0].dtype),
-            pltpu.SemaphoreType.DMA((count,)),
-            pltpu.SemaphoreType.DMA((count,)),
-        ],
-        input_output_aliases={len(pieces): 0} if more else {},
-        cost_estimate=pl.CostEstimate(flops=10**9, bytes_accessed=4 * count * r * q, transcendentals=0),
+        scratch_shapes=[pltpu.SemaphoreType.DMA((len(jobs),))],
+        input_output_aliases={len(items): 0} if more else {},
+        cost_estimate=pl.CostEstimate(flops=10**9, bytes_accessed=4 * q * sum(job[4] for job in jobs), transcendentals=0),
         name="place_blocks",
-    )(*pieces, *more)
-
-
-def gather(own, n):
+    )(*[one[0] for one in items], *more)
+
+
+def gather(own, pieces, firsts, n, shape):
     to_a = [(d, d ^ (2 if d % 2 else 4)) for d in range(n)]
     to_b = [(d, d ^ (4 if d % 2 else 2)) for d in range(n)]
     to_mate = [(d, d ^ 1) for d in range(n)]
 
     def send(what, pairs):
-        return lax.ppermute(what, "dp", pairs)
-
-    from_b = send(own, to_b)
-    from_a = send(own, to_a)
-    mate_own = send(own, to_mate)
+        got = []
+        for one in what:
+            got.append(lax.ppermute(one, "dp", pairs))
+        return got
+
+    from_b = send(pieces, to_b)
+    from_a = send([own], to_a)
+    mate_own = send([own], to_mate)
     from_ab = send(from_b, to_a)
     mate_b = send(from_b, to_mate)
     mate_a = send(from_a, to_mate)
@@ -324,17 +365,32 @@
     def b_of(x, y, c):
         return at_y(x, y) + c * (at_x(x, y) - at_y(x, y))
 
-    places = [
-        lambda x, y, c: (2 * x + y, c),
-        lambda x, y, c: (a_of(x, y, c), c),
-        lambda x, y, c: (b_of(x, y, c), c),
-        lambda x, y, c: (2 * x + y, 1 - c),
-        lambda x, y, c: (b_of(x, y, c), 1 - c),
-        lambda x, y, c: (a_of(x, y, c), 1 - c),
+    def at_own(x, y, c):
+        return 2 * x + y, c
+
+    def at_a(x, y, c):
+        return a_of(x, y, c), c
+
+    def at_b(x, y, c):
+        return b_of(x, y, c), c
+
+    def at_ab(x, y, c):
+        return 3 - 2 * x - y, c
+
+    def of_mate(place):
+        return lambda x, y, c: place(x, y, 1 - c)
+
+    first, second = firsts
+    steps = [
+        [(own, 0, at_own), (from_a[0], 0, at_a), (from_b[0], 0, at_b), (mate_own[0], 0, of_mate(at_own)), (mate_b[0], 0, of_mate(at_b))],
+        [(from_b[1], second, at_b), (mate_a[0], 0, of_mate(at_a)), (mate_b[1], second, of_mate(at_b))],
+        [(from_ab[0], first, at_ab), (mate_ab[0], first, of_mate(at_ab))],
+        [(from_ab[1], second, at_ab), (mate_ab[1], second, of_mate(at_ab))],
     ]
-    first = place_blocks([own, from_a, from_b, mate_own, mate_a, mate_b], places, n)
-    last = [lambda x, y, c: (3 - 2 * x - y, c), lambda x, y, c: (3 - 2 * x - y, 1 - c)]
-    return place_blocks([from_ab, mate_ab], last, n, into=first)
+    whole = None
+    for items in steps:
+        whole = place_blocks(items, shape, into=whole)
+    return whole
 
 
 def solution(mesh):
@@ -359,8 +415,11 @@
         gb = [blocks(t[0], r) for t, r in zip(terms, rows)]
         wb = [blocks(t, r) for t, r in zip(weights, rows)]
         bf, f32 = jnp.bfloat16, jnp.float32
-        out = [jax.ShapeDtypeStruct((layers, n // 2, 2, r, q), bf) for r, q in zip(rows[:2], cols)]
-        out += [jax.ShapeDtypeStruct((layers, rows[2], cols[2]), bf)]
+        firsts = (0, layers * rows[2] * 2 // 3)
+        ends = (*firsts[1:], layers * rows[2])
+        out = [jax.ShapeDtypeStruct((layers * rows[2], cols[2]), bf)]
+        out += [jax.ShapeDtypeStruct((end - first, cols[2]), bf) for first, end in zip(firsts, ends)]
+        out += [jax.ShapeDtypeStruct((layers, n // 2, 2, r, q), bf) for r, q in zip(rows[:2], cols)]
         out += [jax.ShapeDtypeStruct((layers, r, q), bf) for r, q in zip(rows, cols)]
         out += [jax.ShapeDtypeStruct((layers, n // 2, r, q), bf) for r, q in zip(rows, cols)]
         out += [jax.ShapeDtypeStruct((layers, 2, r, q), bf) for r, q in zip(rows, cols)]
@@ -383,11 +442,13 @@
                 pltpu.VMEM((GOUT, *u), bf),
                 pltpu.VMEM((WNEW, *u), bf),
             ]
+        wi, _, _, short = chunks[-1]
+        scratch += [pltpu.VMEM((2, short, cols[wi]), bf), pltpu.VMEM((short, cols[wi]), bf)]
         copies = 10 * len(chunks)
         scratch += [pltpu.SemaphoreType.DMA((copies,)), pltpu.SemaphoreType.DMA((copies,)), pltpu.SemaphoreType.DMA((L_ALL,))]
         hbm = pl.BlockSpec(memory_space=pl.ANY)
         res = pl.pallas_call(
-            functools.partial(body, chunks, group, kinds, (2,)),
+            functools.partial(body, chunks, group, kinds, (2,), firsts),
             out_shape=out,
             in_specs=[hbm] * 12,
             out_specs=[hbm] * len(out),
@@ -395,10 +456,13 @@
             compiler_params=pltpu.CompilerParams(collective_id=0, has_side_effects=True, vmem_limit_bytes=60 * 2**20),
             name="sum_step_gather",
         )(*gb, *wb, *m, *v)
-        whole = [copy_blocks(one) for one in res[0:2]]
-        whole += [gather(res[2], n)]
+        own, pieces, res = res[0], res[1 : 1 + len(firsts)], res[1 + len(firsts) :]
+        whole = []
+        for one in res[0:2]:
+            whole.append(copy_blocks(one))
+        whole.append(gather(own, pieces, firsts, n, (layers, n // 2, 2, rows[2], cols[2])))
         whole = [one.reshape(w.shape) for one, w in zip(whole, weights)]
-        total = [one.astype(f32) for one in res[3:6]]
+        total = [one.astype(f32) for one in res[2:5]]
         new_m = [0.9 * a + 0.1 * t for a, t in zip(m, total)]
         new_v = [0.95 * a + 0.05 * t * t for a, t in zip(v, total)]
         return (*whole, *new_m, *new_v)

time: 591 us -> 597 us (1.010)
  Pallas kernels: 499 us -> 478 us
  local copies, waits for them, and re-layouts: 0.01 us -> 15.6 us
  waiting for transfers between devices: 60.2 us -> 69 us
    pallas_call x2, Pallas kernels: 40.4 us -> 18.5 us  [copy_blocks(): pl.pallas_call(kernel, out_shape=jax.ShapeDtypeStruct(a.shape, a.dtype),...]
    unnamed x4 -> x8, local copies, waits for them, and re-layouts: 0.01 us -> 15.6 us
    ppermute x7 -> x11, waiting for transfers between devices: 60.2 us -> 69 us  [send(): got.append(lax.ppermute(one, 'dp', pairs))]
    pallas_call x3 -> x5, Pallas kernels: 459 us -> 459 us  [the longest x1 440 us: inner(): pl.pallas_call(functools.partial(body, chunks, group, kinds, (2,), firsts...]
  transfers between devices with their start and end apart: 7 -> 11, of which waited for: 2 -> 2; matrix products, arithmetic and copies ran while one was open for 4% -> 4% of each run, Pallas kernels for 9% -> 6%
where the time goes in v3:
time: 597 us; the launch traced here: 596 us
  Pallas kernels  478 us (80%)
  waiting for transfers between devices  69 us (12%)
  other arithmetic  26.6 us (4%)
  local copies, waits for them, and re-layouts  15.6 us (3%)
  starting transfers between devices  6.36 us (1%)
    pallas_call x1, Pallas kernels, inner(): pl.pallas_call(functools.partial(body, chunks, group, kinds, (2,), firsts...  440 us
    ppermute x11, waiting for transfers between devices, send(): got.append(lax.ppermute(one, 'dp', pairs))  69 us
    add x2, other arithmetic, inner(): new_v = [0.95 * a + 0.05 * t * t for a, t in zip(v, total)]  26.6 us
    pallas_call x4, Pallas kernels, place_blocks(): pl.pallas_call(kernel, out_shape=jax.ShapeDtypeStruct(shape, items[0][0]....  19.5 us
    pallas_call x2, Pallas kernels, copy_blocks(): pl.pallas_call(kernel, out_shape=jax.ShapeDtypeStruct(a.shape, a.dtype),...  18.5 us
    unnamed x8, local copies, waits for them, and re-layouts  15.6 us
  transfers between devices with their start and end apart: 11, of which 2 were waited for; matrix products, arithmetic and copies ran while one was open for 4% of the time, Pallas kernels for 6%

profile of v3, /device:TPU:0, one launch (start us, length us, event | category | flops | bytes accessed | tf_op | source)
XLA Modules:
  0.0 596.5 jit_solution(9211212435043150183)
XLA Ops:
  0.6 440.0 %sum_step_gather.1 = (bf16[1152,1152]{1,0:T(8,128)(2,1)}, bf16[768,1152]{1,0:T(8,128)(2,1)}, bf16[384,1152]{1,0:T(8,128)(2,1)}, bf16[2,4,2,144,4608]{4,3,2,1,0:T...) custom-call(bf16[2,4,2,144,4608]{4,3,2,1,0:T(8,128)(2,1)} %bitcast.1, ...), custom_call_target="tpu_custom_call" | custom-call | tf_op jit(solution)/shard_map/sum_step_gather/pallas_call | solution.py:450
  440.7 1.2 collective-permute-start.6
  441.9 0.8 collective-permute-start.3
  442.7 1.2 collective-permute-start
  443.9 0.0 collective-permute-start.9
  444.0 56.9 %collective-permute-done.refs_0_ = bf16[384,1152]{1,0:T(8,128)(2,1)} collective-permute-done((bf16[384,1152]{1,0:T(8,128)(2,1)}, bf16[384,1152]{1,0:T(8,128)(2,1)}, u32[]{:S(2)}, u32[]{:S(2)}) %collective-permute-start) | collective-permute-done | bytes 884768 | tf_op jit(solution)/shard_map/ppermute | solution.py:345
  500.9 1.0 collective-permute-start.1
  501.8 0.0 collective-permute-done.3.refs_2_
  501.9 1.0 collective-permute-start.4
  502.9 0.0 collective-permute-done.6.refs_1_
  502.9 0.0 collective-permute-start.7
  502.9 17.6 %fusion.3 = (f32[2,144,4608]{2,1,0:T(8,128)}, f32[2,144,4608]{2,1,0:T(8,128)}, f32[2,144,4608]{2,1,0:T(8,128)}, f32[2,144,4608]{2,1,0:T(8,128)}) fusion(bf16[2,144,4608]{2,1,0:T(8,128)(2,1)} %get-tuple-element.22, f32[2,144,4608]{2,1,0:T(8,128)} %refs_9_.1, f32[2,144,4608]{2,1,0:T(8,128)} %refs_6_.1, bf16[2,144,4608]{2,1,0:T(8,128)(2,1)} %get-tuple-element.23, ...), kind=kLoop, calls=%fused_computation.9 | loop fusion | flops 21233664 | bytes 47775744 | tf_op jit(solution)/shard_map/add | solution.py:467
  520.5 0.5 collective-permute-start.8
  521.0 0.0 collective-permute-done.1.refs_0_
  521.0 0.0 collective-permute-start.10
  521.1 12.1 %collective-permute-done.4.refs_0_ = bf16[768,1152]{1,0:T(8,128)(2,1)} collective-permute-done((bf16[768,1152]{1,0:T(8,128)(2,1)}, bf16[768,1152]{1,0:T(8,128)(2,1)}, u32[]{:S(2)}, u32[]{:S(2)}) %collective-permute-start.4) | collective-permute-done | bytes 1769504 | tf_op jit(solution)/shard_map/ppermute | solution.py:345
  533.2 0.0 collective-permute-start.5
  533.2 9.0 %fusion.5 = (f32[2,576,1152]{2,1,0:T(8,128)}, f32[2,576,1152]{2,1,0:T(8,128)}) fusion(bf16[2,576,1152]{2,1,0:T(8,128)(2,1)} %get-tuple-element.24, f32[2,576,1152]{2,1,0:T(8,128)} %refs_11_.1, f32[2,576,1152]{2,1,0:T(8,128)S(1)} %copy-done.2), kind=kLoop, calls=%fused_computation.11 | loop fusion | flops 10616832 | bytes 23887872 | tf_op jit(solution)/shard_map/add | solution.py:467
  542.2 0.0 collective-permute-done.9.refs_3_
  542.2 0.5 collective-permute-start.2
  542.7 7.0 %copy-done.1 = bf16[2,4,2,144,4608]{4,3,2,1,0:T(8,128)(2,1)S(1)} copy-done((bf16[2,4,2,144,4608]{4,3,2,1,0:T(8,128)(2,1)S(1)}, bf16[2,4,2,144,4608]{4,3,2,1,0:T(8,128)(2,1)}, u32[]{:S(2)}) %copy-start.1) | copy-done | bytes 21233688
  549.7 9.2 %copy_blocks.2 = bf16[2,4,2,144,4608]{4,3,2,1,0:T(8,128)(2,1)} custom-call(bf16[2,4,2,144,4608]{4,3,2,1,0:T(8,128)(2,1)S(1)} %copy-done.1), custom_call_target="tpu_custom_call" | custom-call | flops 4000000000 | bytes 42467328 | tf_op jit(solution)/shard_map/copy_blocks/pallas_call | solution.py:286
  559.0 7.0 %copy-done = bf16[2,4,2,144,4608]{4,3,2,1,0:T(8,128)(2,1)S(1)} copy-done((bf16[2,4,2,144,4608]{4,3,2,1,0:T(8,128)(2,1)S(1)}, bf16[2,4,2,144,4608]{4,3,2,1,0:T(8,128)(2,1)}, u32[]{:S(2)}) %copy-start) | copy-done | bytes 21233688
  566.0 9.2 %copy_blocks.3 = bf16[2,4,2,144,4608]{4,3,2,1,0:T(8,128)(2,1)} custom-call(bf16[2,4,2,144,4608]{4,3,2,1,0:T(8,128)(2,1)S(1)} %copy-done), custom_call_target="tpu_custom_call" | custom-call | flops 4000000000 | bytes 42467328 | tf_op jit(solution)/shard_map/copy_blocks/pallas_call | solution.py:286
  575.3 0.0 collective-permute-done.10.refs_4_
  575.3 8.7 %place_blocks.4.refs_3_ = bf16[2,4,2,576,1152]{4,3,2,1,0:T(8,128)(2,1)} custom-call(bf16[1152,1152]{1,0:T(8,128)(2,1)} %get-tuple-element.21.refs_0_, bf16[1152,1152]{1,0:T(8,128)(2,1)} %collective-permute-done.6.refs_1_, bf16[768,1152]{1,0:T(8,128)(2,1)} %collective-permute-done.3.refs_2_, bf16[1152,1152]{1,0:T(8,128)(2,1)} %collective-permute-done.9.refs_3_, ...), custom_call_target="tpu_custom_call" | custom-call | flops 1000000000 | bytes 23003136 | tf_op jit(solution)/shard_map/place_blocks/pallas_call | solution.py:325
  583.9 0.0 collective-permute-done.7.refs_1_
  584.0 1.5 copy-done.3
  585.5 4.3 place_blocks.5.refs_2_
  589.8 0.0 collective-permute-done.5.refs_1_
  589.8 3.8 place_blocks.6.refs_2_
  593.7 2.7 place_blocks.7
  (7 shorter events, 0.0 us)
Async XLA Ops:
  440.7 62.2 %collective-permute-start.6 = (bf16[1152,1152]{1,0:T(8,128)(2,1)}, bf16[1152,1152]{1,0:T(8,128)(2,1)}, u32[]{:S(2)}, u32[]{:S(2)}) collective-permute-start(bf16[1152,1152]{1,0:T(8,128)(2,1)} %get-tuple-element.21.refs_0_), channel_id=1, source_target_pairs={{0,4},{1,3},{2,6},{3,1},{4,0},{5,7},{6,2},{7,5}} | collective-permute-start | bytes 7962632 | tf_op jit(solution)/shard_map/ppermute | solution.py:345
  441.9 59.9 %collective-permute-start.3 = (bf16[768,1152]{1,0:T(8,128)(2,1)}, bf16[768,1152]{1,0:T(8,128)(2,1)}, u32[]{:S(2)}, u32[]{:S(2)}) collective-permute-start(bf16[768,1152]{1,0:T(8,128)(2,1)} %get-tuple-element.20), channel_id=1, source_target_pairs={{0,2},{1,5},{2,0},{3,7},{4,6},{5,1},{6,4},{7,3}} | collective-permute-start | bytes 5308424 | tf_op jit(solution)/shard_map/ppermute | solution.py:345
  442.7 58.1 %collective-permute-start = (bf16[384,1152]{1,0:T(8,128)(2,1)}, bf16[384,1152]{1,0:T(8,128)(2,1)}, u32[]{:S(2)}, u32[]{:S(2)}) collective-permute-start(bf16[384,1152]{1,0:T(8,128)(2,1)} %get-tuple-element.19), channel_id=1, source_target_pairs={{0,2},{1,5},{2,0},{3,7},{4,6},{5,1},{6,4},{7,3}} | collective-permute-start | bytes 2654216 | tf_op jit(solution)/shard_map/ppermute | solution.py:345
  443.9 98.2 %collective-permute-start.9 = (bf16[1152,1152]{1,0:T(8,128)(2,1)}, bf16[1152,1152]{1,0:T(8,128)(2,1)}, u32[]{:S(2)}, u32[]{:S(2)}) collective-permute-start(bf16[1152,1152]{1,0:T(8,128)(2,1)} %get-tuple-element.21.refs_0_), channel_id=1, source_target_pairs={{0,1},{1,0},{2,3},{3,2},{4,5},{5,4},{6,7},{7,6}} | collective-permute-start | bytes 7962632 | tf_op jit(solution)/shard_map/ppermute | solution.py:345
  500.9 20.2 %collective-permute-start.1 = (bf16[384,1152]{1,0:T(8,128)(2,1)}, bf16[384,1152]{1,0:T(8,128)(2,1)}, u32[]{:S(2)}, u32[]{:S(2)}) collective-permute-start(bf16[384,1152]{1,0:T(8,128)(2,1)} %collective-permute-done.refs_0_), channel_id=1, source_target_pairs={{0,4},{1,3},{2,6},{3,1},{4,0},{5,7},{6,2},{7,5}} | collective-permute-start | bytes 2654216 | tf_op jit(solution)/shard_map/ppermute | solution.py:345
  501.9 31.3 %collective-permute-start.4 = (bf16[768,1152]{1,0:T(8,128)(2,1)}, bf16[768,1152]{1,0:T(8,128)(2,1)}, u32[]{:S(2)}, u32[]{:S(2)}) collective-permute-start(bf16[768,1152]{1,0:T(8,128)(2,1)} %collective-permute-done.3.refs_2_), channel_id=1, source_target_pairs={{0,4},{1,3},{2,6},{3,1},{4,0},{5,7},{6,2},{7,5}} | collective-permute-start | bytes 5308424 | tf_op jit(solution)/shard_map/ppermute | solution.py:345
  502.9 81.1 %collective-permute-start.7 = (bf16[1152,1152]{1,0:T(8,128)(2,1)}, bf16[1152,1152]{1,0:T(8,128)(2,1)S(1)}, u32[]{:S(2)}, u32[]{:S(2)}) collective-permute-start(bf16[1152,1152]{1,0:T(8,128)(2,1)} %collective-permute-done.6.refs_1_), channel_id=1, source_target_pairs={{0,1},{1,0},{2,3},{3,2},{4,5},{5,4},{6,7},{7,6}} | collective-permute-start | bytes 7962632 | tf_op jit(solution)/shard_map/ppermute | solution.py:345
  502.9 30.3 %copy-start.2 = (f32[2,576,1152]{2,1,0:T(8,128)S(1)}, f32[2,576,1152]{2,1,0:T(8,128)}, u32[]{:S(2)}) copy-start(f32[2,576,1152]{2,1,0:T(8,128)} %refs_8_.1) | copy-start | bytes 15925252
  520.5 63.4 %collective-permute-start.8 = (bf16[384,1152]{1,0:T(8,128)(2,1)}, bf16[384,1152]{1,0:T(8,128)(2,1)}, u32[]{:S(2)}, u32[]{:S(2)}) collective-permute-start(bf16[384,1152]{1,0:T(8,128)(2,1)} %collective-permute-done.refs_0_), channel_id=1, source_target_pairs={{0,1},{1,0},{2,3},{3,2},{4,5},{5,4},{6,7},{7,6}} | collective-permute-start | bytes 2654216 | tf_op jit(solution)/shard_map/ppermute | solution.py:345
  521.0 54.3 %collective-permute-start.10 = (bf16[768,1152]{1,0:T(8,128)(2,1)}, bf16[768,1152]{1,0:T(8,128)(2,1)}, u32[]{:S(2)}, u32[]{:S(2)}) collective-permute-start(bf16[768,1152]{1,0:T(8,128)(2,1)} %collective-permute-done.3.refs_2_), channel_id=1, source_target_pairs={{0,1},{1,0},{2,3},{3,2},{4,5},{5,4},{6,7},{7,6}} | collective-permute-start | bytes 5308424 | tf_op jit(solution)/shard_map/ppermute | solution.py:345
  533.2 56.6 %collective-permute-start.5 = (bf16[768,1152]{1,0:T(8,128)(2,1)}, bf16[768,1152]{1,0:T(8,128)(2,1)}, u32[]{:S(2)}, u32[]{:S(2)}) collective-permute-start(bf16[768,1152]{1,0:T(8,128)(2,1)} %collective-permute-done.4.refs_0_), channel_id=1, source_target_pairs={{0,1},{1,0},{2,3},{3,2},{4,5},{5,4},{6,7},{7,6}} | collective-permute-start | bytes 5308424 | tf_op jit(solution)/shard_map/ppermute | solution.py:345
  542.2 51.5 %collective-permute-start.2 = (bf16[384,1152]{1,0:T(8,128)(2,1)}, bf16[384,1152]{1,0:T(8,128)(2,1)}, u32[]{:S(2)}, u32[]{:S(2)}) collective-permute-start(bf16[384,1152]{1,0:T(8,128)(2,1)} %collective-permute-done.1.refs_0_), channel_id=1, source_target_pairs={{0,1},{1,0},{2,3},{3,2},{4,5},{5,4},{6,7},{7,6}} | collective-permute-start | bytes 2654216 | tf_op jit(solution)/shard_map/ppermute | solution.py:345
  542.7 7.0 %copy-start.1 = (bf16[2,4,2,144,4608]{4,3,2,1,0:T(8,128)(2,1)S(1)}, bf16[2,4,2,144,4608]{4,3,2,1,0:T(8,128)(2,1)}, u32[]{:S(2)}) copy-start(bf16[2,4,2,144,4608]{4,3,2,1,0:T(8,128)(2,1)} %get-tuple-element.17.src) | copy-start | bytes 63700996
  559.0 7.0 %copy-start = (bf16[2,4,2,144,4608]{4,3,2,1,0:T(8,128)(2,1)S(1)}, bf16[2,4,2,144,4608]{4,3,2,1,0:T(8,128)(2,1)}, u32[]{:S(2)}) copy-start(bf16[2,4,2,144,4608]{4,3,2,1,0:T(8,128)(2,1)} %get-tuple-element.18.src) | copy-start | bytes 63700996
  584.0 1.5 copy-start.3

commit v4 on v3

--- a/solution.py
+++ b/solution.py
@@ -29,22 +29,30 @@
     return out
 
 
+TURNS = {"d": 4, "a": 4, "b": 4, "gb": 4, "ga": 6, "gab": 4, "mo": 6, "mb": 6, "mga": 8, "mgab": 8}
+FIRST = {kind: sum(list(TURNS.values())[:i]) for i, kind in enumerate(TURNS)}
+
+
 class Copies:
     def __init__(self, send, recv, local):
         self.send, self.recv, self.local = send, recv, local
-        self.ids, self.nlocal, self.remote, self.here = {}, 0, {}, {}
+        self.remote, self.here = {}, {}
 
     def start_remote(self, key, src, dst, peer):
-        n = self.ids.setdefault(key, len(self.ids))
+        kind, k = key
+        before = (kind, k - TURNS[kind])
+        self.wait_send(before)
+        assert before not in self.remote or not self.remote[before][2]
+        n = FIRST[kind] + k % TURNS[kind]
         c = pltpu.make_async_remote_copy(src, dst, self.send.at[n], self.recv.at[n], device_id={"dp": peer}, device_id_type=MESH)
         c.start()
         self.remote[key] = [c, True, True]
 
     def wait_recv(self, key):
-        c = self.remote[key]
-        assert c[2]
-        c[0].wait_recv()
-        c[2] = False
+        c = self.remote.get(key)
+        if c is not None and c[2]:
+            c[0].wait_recv()
+            c[2] = False
 
     def wait_send(self, key):
         c = self.remote.get(key)
@@ -150,6 +158,12 @@
             cp.wait_recv((kind, k))
             part = wn[wi].at[layer, place, c, rs, :]
             cp.start_remote(("m" + kind, k), part, part, mate)
+
+    def settle(s):
+        cp.wait_recv(("mo", s - 3 * LAG))
+        cp.wait_recv(("mb", s - 4 * LAG))
+        cp.wait_recv(("mga", s - 5 * LAG))
+        cp.wait_recv(("mgab", s - 5 * LAG))
 
     def sum_mates(k):
         wi, layer, rs, rows, b, step = at(k)
@@ -254,6 +268,7 @@
         when(s - 2 * LAG, load_b)
         when(s - 3 * LAG, forward_b, True)
         when(s - 4 * LAG, forward_a, True)
+        settle(s)
         if s >= 2:
             when(s, sum_mates)
         when(s - LAG, sum_a)
@@ -265,32 +280,27 @@
 
 
 def copy_blocks(a):
-    layers, places, cores, r, q = a.shape
+    layers, places, cores, _, _ = a.shape
     count = layers * places * cores
 
-    def kernel(src, dst, buf, sin, sout):
+    def kernel(src, dst, sems):
         def where(i):
             return i // (places * cores), (i // cores) % places, i % cores
 
-        loads = [pltpu.make_async_copy(src.at[where(i)], buf.at[i], sin.at[i]) for i in range(count)]
-        stores = [pltpu.make_async_copy(buf.at[i], dst.at[where(i)], sout.at[i]) for i in range(count)]
-        for one in loads:
+        stores = [pltpu.make_async_copy(src.at[where(i)], dst.at[where(i)], sems.at[i]) for i in range(count)]
+        for one in stores:
             one.start()
-        for one, two in zip(loads, stores):
+        for one in stores:
             one.wait()
-            two.start()
-        for two in stores:
-            two.wait()
-
-    hbm = pl.BlockSpec(memory_space=pl.ANY)
+
     return pl.pallas_call(
         kernel,
         out_shape=jax.ShapeDtypeStruct(a.shape, a.dtype),
-        in_specs=[hbm],
-        out_specs=hbm,
-        scratch_shapes=[pltpu.VMEM((count, r, q), a.dtype), pltpu.SemaphoreType.DMA((count,)), pltpu.SemaphoreType.DMA((count,))],
+        in_specs=[pl.BlockSpec(memory_space=pltpu.VMEM)],
+        out_specs=pl.BlockSpec(memory_space=pl.ANY),
+        scratch_shapes=[pltpu.SemaphoreType.DMA((count,))],
         cost_estimate=pl.CostEstimate(flops=4 * 10**9, bytes_accessed=4 * a.size, transcendentals=0),
-        compiler_params=pltpu.CompilerParams(vmem_limit_bytes=24 * 2**20),
+        compiler_params=pltpu.CompilerParams(vmem_limit_bytes=2 * a.size + 2**20),
         name="copy_blocks",
     )(a)
 
@@ -330,6 +340,7 @@
         scratch_shapes=[pltpu.SemaphoreType.DMA((len(jobs),))],
         input_output_aliases={len(items): 0} if more else {},
         cost_estimate=pl.CostEstimate(flops=10**9, bytes_accessed=4 * q * sum(job[4] for job in jobs), transcendentals=0),
+        compiler_params=pltpu.CompilerParams(vmem_limit_bytes=2 * q * sum(job[4] for job in jobs) + 2**20),
         name="place_blocks",
     )(*[one[0] for one in items], *more)
 
@@ -444,7 +455,7 @@
             ]
         wi, _, _, short = chunks[-1]
         scratch += [pltpu.VMEM((2, short, cols[wi]), bf), pltpu.VMEM((short, cols[wi]), bf)]
-        copies = 10 * len(chunks)
+        copies = sum(TURNS.values())
         scratch += [pltpu.SemaphoreType.DMA((copies,)), pltpu.SemaphoreType.DMA((copies,)), pltpu.SemaphoreType.DMA((L_ALL,))]
         hbm = pl.BlockSpec(memory_space=pl.ANY)
         res = pl.pallas_call(

time: 597 us -> 588 us (0.985)
  Pallas kernels: 478 us -> 468 us
    unnamed x8 -> x6, local copies, waits for them, and re-layouts: 15.6 us -> 14.1 us
  transfers between devices with their start and end apart: 11 -> 11, of which waited for: 2 -> 2; matrix products, arithmetic and copies ran while one was open for 4% -> 5% of each run, Pallas kernels for 6% -> 5%
where the time goes in v4:
time: 588 us; the launch traced here: 587 us
  Pallas kernels  468 us (80%)
  waiting for transfers between devices  69.4 us (12%)
  other arithmetic  27.8 us (5%)
  local copies, waits for them, and re-layouts  14.1 us (2%)
  starting transfers between devices  6.36 us (1%)
    pallas_call x1, Pallas kernels, inner(): pl.pallas_call(functools.partial(body, chunks, group, kinds, (2,), firsts...  437 us
    ppermute x11, waiting for transfers between devices, send(): got.append(lax.ppermute(one, 'dp', pairs))  69.4 us
    add x2, other arithmetic, inner(): new_v = [0.95 * a + 0.05 * t * t for a, t in zip(v, total)]  27.8 us
    pallas_call x4, Pallas kernels, place_blocks(): pl.pallas_call(kernel, out_shape=jax.ShapeDtypeStruct(shape, items[0][0]....  16.1 us
    pallas_call x2, Pallas kernels, copy_blocks(): pl.pallas_call(kernel, out_shape=jax.ShapeDtypeStruct(a.shape, a.dtype),...  15 us
    unnamed x6, local copies, waits for them, and re-layouts  14.1 us
  transfers between devices with their start and end apart: 11, of which 2 were waited for; matrix products, arithmetic and copies ran while one was open for 5% of the time, Pallas kernels for 5%

profile of v4, /device:TPU:0, one launch (start us, length us, event | category | flops | bytes accessed | tf_op | source)
XLA Modules:
  0.0 586.8 jit_solution(11408680924983407312)
XLA Ops:
  0.6 437.4 %sum_step_gather.1 = (bf16[1152,1152]{1,0:T(8,128)(2,1)}, bf16[768,1152]{1,0:T(8,128)(2,1)}, bf16[384,1152]{1,0:T(8,128)(2,1)}, bf16[2,4,2,144,4608]{4,3,2,1,0:T...) custom-call(bf16[2,4,2,144,4608]{4,3,2,1,0:T(8,128)(2,1)} %bitcast.1, ...), custom_call_target="tpu_custom_call" | custom-call | tf_op jit(solution)/shard_map/sum_step_gather/pallas_call | solution.py:461
  438.1 1.2 collective-permute-start.6
  439.3 0.8 collective-permute-start.3
  440.1 1.2 collective-permute-start
  441.3 0.0 collective-permute-start.9
  441.3 56.9 %collective-permute-done.refs_0_ = bf16[384,1152]{1,0:T(8,128)(2,1)} collective-permute-done((bf16[384,1152]{1,0:T(8,128)(2,1)}, bf16[384,1152]{1,0:T(8,128)(2,1)}, u32[]{:S(2)}, u32[]{:S(2)}) %collective-permute-start) | collective-permute-done | bytes 884768 | tf_op jit(solution)/shard_map/ppermute | solution.py:356
  498.2 1.0 collective-permute-start.1
  499.2 0.0 collective-permute-done.3.refs_2_
  499.2 1.0 collective-permute-start.4
  500.3 0.0 collective-permute-done.6.refs_1_
  500.3 0.0 collective-permute-start.7
  500.3 17.3 %fusion.3 = (f32[2,144,4608]{2,1,0:T(8,128)}, f32[2,144,4608]{2,1,0:T(8,128)}, f32[2,144,4608]{2,1,0:T(8,128)}, f32[2,144,4608]{2,1,0:T(8,128)}) fusion(bf16[2,144,4608]{2,1,0:T(8,128)(2,1)} %get-tuple-element.22, f32[2,144,4608]{2,1,0:T(8,128)} %refs_9_.1, f32[2,144,4608]{2,1,0:T(8,128)} %refs_6_.1, bf16[2,144,4608]{2,1,0:T(8,128)(2,1)} %get-tuple-element.23, ...), kind=kLoop, calls=%fused_computation.9 | loop fusion | flops 21233664 | bytes 47775744 | tf_op jit(solution)/shard_map/add | solution.py:478
  517.6 0.5 collective-permute-start.8
  518.1 0.0 collective-permute-done.1.refs_0_
  518.1 0.0 collective-permute-start.10
  518.1 12.4 %collective-permute-done.4.refs_0_ = bf16[768,1152]{1,0:T(8,128)(2,1)} collective-permute-done((bf16[768,1152]{1,0:T(8,128)(2,1)}, bf16[768,1152]{1,0:T(8,128)(2,1)}, u32[]{:S(2)}, u32[]{:S(2)}) %collective-permute-start.4) | collective-permute-done | bytes 1769504 | tf_op jit(solution)/shard_map/ppermute | solution.py:356
  530.6 0.0 collective-permute-start.5
  530.6 10.5 %fusion.5 = (f32[2,576,1152]{2,1,0:T(8,128)}, f32[2,576,1152]{2,1,0:T(8,128)}) fusion(bf16[2,576,1152]{2,1,0:T(8,128)(2,1)} %get-tuple-element.24, f32[2,576,1152]{2,1,0:T(8,128)} %refs_11_.1, f32[2,576,1152]{2,1,0:T(8,128)} %refs_8_.1), kind=kLoop, calls=%fused_computation.11 | loop fusion | flops 10616832 | bytes 23887872 | tf_op jit(solution)/shard_map/add | solution.py:478
  541.0 0.0 collective-permute-done.9.refs_3_
  541.0 0.5 collective-permute-start.2
  541.5 7.0 %copy-done.1 = bf16[2,4,2,144,4608]{4,3,2,1,0:T(8,128)(2,1)S(1)} copy-done((bf16[2,4,2,144,4608]{4,3,2,1,0:T(8,128)(2,1)S(1)}, bf16[2,4,2,144,4608]{4,3,2,1,0:T(8,128)(2,1)}, u32[]{:S(2)}) %copy-start.1) | copy-done | bytes 21233688
  548.6 7.3 %copy_blocks.2 = bf16[2,4,2,144,4608]{4,3,2,1,0:T(8,128)(2,1)} custom-call(bf16[2,4,2,144,4608]{4,3,2,1,0:T(8,128)(2,1)S(1)} %copy-done.1), custom_call_target="tpu_custom_call" | custom-call | flops 4000000000 | bytes 42467328 | tf_op jit(solution)/shard_map/copy_blocks/pallas_call | solution.py:296
  555.9 7.0 %copy-done = bf16[2,4,2,144,4608]{4,3,2,1,0:T(8,128)(2,1)S(1)} copy-done((bf16[2,4,2,144,4608]{4,3,2,1,0:T(8,128)(2,1)S(1)}, bf16[2,4,2,144,4608]{4,3,2,1,0:T(8,128)(2,1)}, u32[]{:S(2)}) %copy-start) | copy-done | bytes 21233688
  563.0 7.6 %copy_blocks.3 = bf16[2,4,2,144,4608]{4,3,2,1,0:T(8,128)(2,1)} custom-call(bf16[2,4,2,144,4608]{4,3,2,1,0:T(8,128)(2,1)S(1)} %copy-done), custom_call_target="tpu_custom_call" | custom-call | flops 4000000000 | bytes 42467328 | tf_op jit(solution)/shard_map/copy_blocks/pallas_call | solution.py:296
  570.6 0.0 collective-permute-done.10.refs_4_
  570.6 6.3 %place_blocks.4.refs_3_ = bf16[2,4,2,576,1152]{4,3,2,1,0:T(8,128)(2,1)} custom-call(bf16[1152,1152]{1,0:T(8,128)(2,1)S(1)} %copy-done.2, bf16[1152,1152]{1,0:T(8,128)(2,1)S(1)} %collective-permute-done.6.refs_1_, bf16[768,1152]{1,0:T(8,128)(2,1)} %collective-permute-done.3.refs_2_, bf16[1152,1152]{1,0:T(8,128)(2,1)S(1)} %collective-permute-done.9.refs_3_, ...), custom_call_target="tpu_custom_call" | custom-call | flops 1000000000 | bytes 23003136 | tf_op jit(solution)/shard_map/place_blocks/pallas_call | solution.py:335
  577.0 0.0 collective-permute-done.8.refs_2_
  577.0 0.0 collective-permute-done.7.refs_1_
  577.0 3.5 place_blocks.5.refs_2_
  580.6 3.8 place_blocks.6.refs_2_
  584.4 0.0 collective-permute-done.2.refs_1_
  584.4 2.4 place_blocks.7
  (5 shorter events, 0.0 us)
Async XLA Ops:
  438.1 62.2 %collective-permute-start.6 = (bf16[1152,1152]{1,0:T(8,128)(2,1)}, bf16[1152,1152]{1,0:T(8,128)(2,1)S(1)}, u32[]{:S(2)}, u32[]{:S(2)}) collective-permute-start(bf16[1152,1152]{1,0:T(8,128)(2,1)} %get-tuple-element.21.refs_0_), channel_id=1, source_target_pairs={{0,4},{1,3},{2,6},{3,1},{4,0},{5,7},{6,2},{7,5}} | collective-permute-start | bytes 7962632 | tf_op jit(solution)/shard_map/ppermute | solution.py:356
  439.3 59.9 %collective-permute-start.3 = (bf16[768,1152]{1,0:T(8,128)(2,1)}, bf16[768,1152]{1,0:T(8,128)(2,1)}, u32[]{:S(2)}, u32[]{:S(2)}) collective-permute-start(bf16[768,1152]{1,0:T(8,128)(2,1)} %get-tuple-element.20), channel_id=1, source_target_pairs={{0,2},{1,5},{2,0},{3,7},{4,6},{5,1},{6,4},{7,3}} | collective-permute-start | bytes 5308424 | tf_op jit(solution)/shard_map/ppermute | solution.py:356
  440.1 58.1 %collective-permute-start = (bf16[384,1152]{1,0:T(8,128)(2,1)}, bf16[384,1152]{1,0:T(8,128)(2,1)}, u32[]{:S(2)}, u32[]{:S(2)}) collective-permute-start(bf16[384,1152]{1,0:T(8,128)(2,1)} %get-tuple-element.19), channel_id=1, source_target_pairs={{0,2},{1,5},{2,0},{3,7},{4,6},{5,1},{6,4},{7,3}} | collective-permute-start | bytes 2654216 | tf_op jit(solution)/shard_map/ppermute | solution.py:356
  441.3 99.7 %collective-permute-start.9 = (bf16[1152,1152]{1,0:T(8,128)(2,1)}, bf16[1152,1152]{1,0:T(8,128)(2,1)S(1)}, u32[]{:S(2)}, u32[]{:S(2)}) collective-permute-start(bf16[1152,1152]{1,0:T(8,128)(2,1)} %get-tuple-element.21.refs_0_), channel_id=1, source_target_pairs={{0,1},{1,0},{2,3},{3,2},{4,5},{5,4},{6,7},{7,6}} | collective-permute-start | bytes 7962632 | tf_op jit(solution)/shard_map/ppermute | solution.py:356
  498.2 19.8 %collective-permute-start.1 = (bf16[384,1152]{1,0:T(8,128)(2,1)}, bf16[384,1152]{1,0:T(8,128)(2,1)}, u32[]{:S(2)}, u32[]{:S(2)}) collective-permute-start(bf16[384,1152]{1,0:T(8,128)(2,1)} %collective-permute-done.refs_0_), channel_id=1, source_target_pairs={{0,4},{1,3},{2,6},{3,1},{4,0},{5,7},{6,2},{7,5}} | collective-permute-start | bytes 2654216 | tf_op jit(solution)/shard_map/ppermute | solution.py:356
  499.2 31.3 %collective-permute-start.4 = (bf16[768,1152]{1,0:T(8,128)(2,1)}, bf16[768,1152]{1,0:T(8,128)(2,1)}, u32[]{:S(2)}, u32[]{:S(2)}) collective-permute-start(bf16[768,1152]{1,0:T(8,128)(2,1)} %collective-permute-done.3.refs_2_), channel_id=1, source_target_pairs={{0,4},{1,3},{2,6},{3,1},{4,0},{5,7},{6,2},{7,5}} | collective-permute-start | bytes 5308424 | tf_op jit(solution)/shard_map/ppermute | solution.py:356
  500.3 76.7 %collective-permute-start.7 = (bf16[1152,1152]{1,0:T(8,128)(2,1)S(1)}, bf16[1152,1152]{1,0:T(8,128)(2,1)S(1)}, u32[]{:S(2)}, u32[]{:S(2)}) collective-permute-start(bf16[1152,1152]{1,0:T(8,128)(2,1)S(1)} %collective-permute-done.6.refs_1_), channel_id=1, source_target_pairs={{0,1},{1,0},{2,3},{3,2},{4,5},{5,4},{6,7},{7,6}} | collective-permute-start | bytes 7962632 | tf_op jit(solution)/shard_map/ppermute | solution.py:356
  517.6 59.4 %collective-permute-start.8 = (bf16[384,1152]{1,0:T(8,128)(2,1)}, bf16[384,1152]{1,0:T(8,128)(2,1)}, u32[]{:S(2)}, u32[]{:S(2)}) collective-permute-start(bf16[384,1152]{1,0:T(8,128)(2,1)} %collective-permute-done.refs_0_), channel_id=1, source_target_pairs={{0,1},{1,0},{2,3},{3,2},{4,5},{5,4},{6,7},{7,6}} | collective-permute-start | bytes 2654216 | tf_op jit(solution)/shard_map/ppermute | solution.py:356
  518.1 52.5 %collective-permute-start.10 = (bf16[768,1152]{1,0:T(8,128)(2,1)}, bf16[768,1152]{1,0:T(8,128)(2,1)}, u32[]{:S(2)}, u32[]{:S(2)}) collective-permute-start(bf16[768,1152]{1,0:T(8,128)(2,1)} %collective-permute-done.3.refs_2_), channel_id=1, source_target_pairs={{0,1},{1,0},{2,3},{3,2},{4,5},{5,4},{6,7},{7,6}} | collective-permute-start | bytes 5308424 | tf_op jit(solution)/shard_map/ppermute | solution.py:356
  530.6 50.0 %collective-permute-start.5 = (bf16[768,1152]{1,0:T(8,128)(2,1)}, bf16[768,1152]{1,0:T(8,128)(2,1)}, u32[]{:S(2)}, u32[]{:S(2)}) collective-permute-start(bf16[768,1152]{1,0:T(8,128)(2,1)} %collective-permute-done.4.refs_0_), channel_id=1, source_target_pairs={{0,1},{1,0},{2,3},{3,2},{4,5},{5,4},{6,7},{7,6}} | collective-permute-start | bytes 5308424 | tf_op jit(solution)/shard_map/ppermute | solution.py:356
  541.0 43.4 %collective-permute-start.2 = (bf16[384,1152]{1,0:T(8,128)(2,1)}, bf16[384,1152]{1,0:T(8,128)(2,1)S(1)}, u32[]{:S(2)}, u32[]{:S(2)}) collective-permute-start(bf16[384,1152]{1,0:T(8,128)(2,1)} %collective-permute-done.1.refs_0_), channel_id=1, source_target_pairs={{0,1},{1,0},{2,3},{3,2},{4,5},{5,4},{6,7},{7,6}} | collective-permute-start | bytes 2654216 | tf_op jit(solution)/shard_map/ppermute | solution.py:356
  541.5 7.0 %copy-start.1 = (bf16[2,4,2,144,4608]{4,3,2,1,0:T(8,128)(2,1)S(1)}, bf16[2,4,2,144,4608]{4,3,2,1,0:T(8,128)(2,1)}, u32[]{:S(2)}) copy-start(bf16[2,4,2,144,4608]{4,3,2,1,0:T(8,128)(2,1)} %get-tuple-element.17.src) | copy-start | bytes 63700996
  555.9 7.0 %copy-start = (bf16[2,4,2,144,4608]{4,3,2,1,0:T(8,128)(2,1)S(1)}, bf16[2,4,2,144,4608]{4,3,2,1,0:T(8,128)(2,1)}, u32[]{:S(2)}) copy-start(bf16[2,4,2,144,4608]{4,3,2,1,0:T(8,128)(2,1)} %get-tuple-element.18.src) | copy-start | bytes 63700996
  563.0 7.7 %copy-start.2 = (bf16[1152,1152]{1,0:T(8,128)(2,1)S(1)}, bf16[1152,1152]{1,0:T(8,128)(2,1)}, u32[]{:S(2)}) copy-start(bf16[1152,1152]{1,0:T(8,128)(2,1)} %get-tuple-element.21.refs_0_) | copy-start | bytes 7962628

commit v5 on v4

--- a/solution.py
+++ b/solution.py
@@ -21,7 +21,7 @@
         if i == 0:
             parts = [1, 2, 3, 3]
         if i == len(pairs) - 1:
-            parts = [3, 3, 2, 1]
+            parts = [3, 2, 3, 1]
         first = 0
         for p in parts:
             out.append((w, l, first * unit, p * unit))
@@ -29,7 +29,7 @@
     return out
 
 
-TURNS = {"d": 4, "a": 4, "b": 4, "gb": 4, "ga": 6, "gab": 4, "mo": 6, "mb": 6, "mga": 8, "mgab": 8}
+TURNS = {"d": 4, "a": 4, "b": 4, "gb": 4, "ga": 6, "gab": 4, "mo": 6, "mb": 6, "mga": 8, "mgab": 8, "ah": 2}
 FIRST = {kind: sum(list(TURNS.values())[:i]) for i, kind in enumerate(TURNS)}
 
 
@@ -81,12 +81,13 @@
 
 
 OWN, PART, SENDA, KEEPA, SENDB, KEEPB, GOUT, WNEW = 2, 2, 3, 3, 2, 3, 2, 4
-L_OWN, L_PART, L_RECVA, L_RECVB, L_M, L_V, L_W, L_G, L_WN, L_AG, L_ALL = 0, 2, 4, 5, 6, 7, 8, 9, 11, 15, 19
-
-
-def body(chunks, group, kinds, outside, firsts, *refs):
+L_OWN, L_PART, L_RECVA, L_RECVB, L_M, L_V, L_W, L_G, L_WN, L_BLOCK, L_REST, L_ALL = 0, 2, 4, 5, 6, 7, 8, 9, 11, 15, 19, 23
+
+
+def body(chunks, group, kinds, outside, firsts, ahead, *refs):
     g, w, m, v = refs[0:3], refs[3:6], refs[6:9], refs[9:12]
-    own_block, own_pieces, refs = refs[12], refs[13 : 13 + len(firsts)], refs[:12] + refs[13 + len(firsts) :]
+    from_a, own_block, own_rest = refs[12:15]
+    own_pieces, refs = refs[15 : 15 + len(firsts)], refs[:12] + refs[15 + len(firsts) :]
     wn, gs, pland, aland, bland = refs[12:14], refs[14:17], refs[17:20], refs[20:23], refs[23:26]
     bufs = (refs[26:39], refs[39:52])
     last_a, last_b, send, recv, local = refs[52:57]
@@ -211,7 +212,8 @@
             cp.wait((kind, k))
         cp.wait(("gout", k - GOUT))
         cp.wait(("wout", k - WNEW))
-        cp.wait(("again", k - WNEW))
+        cp.wait(("block", k - WNEW))
+        cp.wait(("rest", k - WNEW))
         for kind in ("gb", "ga", "mo"):
             cp.wait_send((kind, k - WNEW))
         sb, sg, sn = k % KEEPB, k % GOUT, k % WNEW
@@ -234,26 +236,28 @@
         if inside:
             dst = wn[wi].at[layer, xy, c, rs, :]
             cp.start_remote(("gb", k), src, dst, peer_b)
-            if k != late:
-                cp.start_remote(("ga", k), src, dst, peer_a)
+            cp.start_remote(("ga", k), src, dst, peer_a)
             cp.start_remote(("mo", k), src, dst, mate)
         else:
             first = layer * m[wi].shape[1] + chunks[k][2]
             i = sum(first >= one for one in firsts) - 1
             dst = own_pieces[i].at[pl.ds(first - firsts[i], rows), :]
-            cp.start(("again", k), L_AG + sn, src, own_block.at[pl.ds(first, rows), :])
+            cp.start(("block", k), L_BLOCK + sn, src, own_block.at[pl.ds(first, rows), :])
+            if first >= ahead:
+                cp.start(("rest", k), L_REST + sn, src, own_rest.at[pl.ds(first - ahead, rows), :])
         cp.start(("wout", k), L_WN + sn, src, dst)
         cp.start(("gout", k), L_G + sg, gb.at[sg, top, :], gs[wi].at[layer, rs, :])
 
-    late = max(k for k in range(count) if chunks[k][0] not in outside)
-
-    def send_late():
-        wi, layer, rs, rows, b, _ = at(late)
-        cp.start_remote(("ga", late), b[12].at[late % WNEW, pl.ds(0, rows), :], wn[wi].at[layer, xy, c, rs, :], peer_a)
-        forward_b(late)
+    def send_ahead():
+        for k, (wi, layer, first, rows) in enumerate(chunks):
+            row = layer * m[wi].shape[1] + first
+            if wi in outside and row < ahead:
+                cp.wait(("block", k))
+                part = pl.ds(row, rows)
+                cp.start_remote(("ah", k), own_block.at[part, :], from_a.at[part, :], peer_a)
 
     def when(k, f, gathers=False):
-        if 0 <= k < count and not (gathers and (chunks[k][0] in outside or k == late)):
+        if 0 <= k < count and not (gathers and chunks[k][0] in outside):
             f(k)
 
     when(0, exchange)
@@ -274,8 +278,7 @@
         when(s - LAG, sum_a)
         when(s - 2 * LAG, update)
         if s == count - 1:
-            send_late()
-    forward_a(late)
+            send_ahead()
     cp.drain()
 
 
@@ -345,7 +348,7 @@
     )(*[one[0] for one in items], *more)
 
 
-def gather(own, pieces, firsts, n, shape):
+def gather(own, a_ahead, rest, pieces, firsts, n, shape):
     to_a = [(d, d ^ (2 if d % 2 else 4)) for d in range(n)]
     to_b = [(d, d ^ (4 if d % 2 else 2)) for d in range(n)]
     to_mate = [(d, d ^ 1) for d in range(n)]
@@ -357,7 +360,7 @@
         return got
 
     from_b = send(pieces, to_b)
-    from_a = send([own], to_a)
+    from_a = [a_ahead] + send([rest], to_a)
     mate_own = send([own], to_mate)
     from_ab = send(from_b, to_a)
     mate_b = send(from_b, to_mate)
@@ -392,9 +395,18 @@
         return lambda x, y, c: place(x, y, 1 - c)
 
     first, second = firsts
+    ahead = a_ahead.shape[0]
     steps = [
-        [(own, 0, at_own), (from_a[0], 0, at_a), (from_b[0], 0, at_b), (mate_own[0], 0, of_mate(at_own)), (mate_b[0], 0, of_mate(at_b))],
-        [(from_b[1], second, at_b), (mate_a[0], 0, of_mate(at_a)), (mate_b[1], second, of_mate(at_b))],
+        [
+            (own, 0, at_own),
+            (from_a[0], 0, at_a),
+            (from_a[1], ahead, at_a),
+            (from_b[0], 0, at_b),
+            (mate_own[0], 0, of_mate(at_own)),
+            (mate_a[0], 0, of_mate(at_a)),
+            (mate_b[0], 0, of_mate(at_b)),
+        ],
+        [(from_b[1], second, at_b), (mate_a[1], ahead, of_mate(at_a)), (mate_b[1], second, of_mate(at_b))],
         [(from_ab[0], first, at_ab), (mate_ab[0], first, of_mate(at_ab))],
         [(from_ab[1], second, at_ab), (mate_ab[1], second, of_mate(at_ab))],
     ]
@@ -426,9 +438,10 @@
         gb = [blocks(t[0], r) for t, r in zip(terms, rows)]
         wb = [blocks(t, r) for t, r in zip(weights, rows)]
         bf, f32 = jnp.bfloat16, jnp.float32
-        firsts = (0, layers * rows[2] * 2 // 3)
-        ends = (*firsts[1:], layers * rows[2])
-        out = [jax.ShapeDtypeStruct((layers * rows[2], cols[2]), bf)]
+        tall = layers * rows[2]
+        firsts, ahead = (0, tall * 7 // 9), tall // 3
+        ends = (*firsts[1:], tall)
+        out = [jax.ShapeDtypeStruct((r, cols[2]), bf) for r in (ahead, tall, tall - ahead)]
         out += [jax.ShapeDtypeStruct((end - first, cols[2]), bf) for first, end in zip(firsts, ends)]
         out += [jax.ShapeDtypeStruct((layers, n // 2, 2, r, q), bf) for r, q in zip(rows[:2], cols)]
         out += [jax.ShapeDtypeStruct((layers, r, q), bf) for r, q in zip(rows, cols)]
@@ -459,7 +472,7 @@
         scratch += [pltpu.SemaphoreType.DMA((copies,)), pltpu.SemaphoreType.DMA((copies,)), pltpu.SemaphoreType.DMA((L_ALL,))]
         hbm = pl.BlockSpec(memory_space=pl.ANY)
         res = pl.pallas_call(
-            functools.partial(body, chunks, group, kinds, (2,), firsts),
+            functools.partial(body, chunks, group, kinds, (2,), firsts, ahead),
             out_shape=out,
             in_specs=[hbm] * 12,
             out_specs=[hbm] * len(out),
@@ -467,11 +480,11 @@
             compiler_params=pltpu.CompilerParams(collective_id=0, has_side_effects=True, vmem_limit_bytes=60 * 2**20),
             name="sum_step_gather",
         )(*gb, *wb, *m, *v)
-        own, pieces, res = res[0], res[1 : 1 + len(firsts)], res[1 + len(firsts) :]
+        a_ahead, own, rest, pieces, res = *res[:3], res[3 : 3 + len(firsts)], res[3 + len(firsts) :]
         whole = []
         for one in res[0:2]:
             whole.append(copy_blocks(one))
-        whole.append(gather(own, pieces, firsts, n, (layers, n // 2, 2, rows[2], cols[2])))
+        whole.append(gather(own, a_ahead, rest, pieces, firsts, n, (layers, n // 2, 2, rows[2], cols[2])))
         whole = [one.reshape(w.shape) for one, w in zip(whole, weights)]
         total = [one.astype(f32) for one in res[2:5]]
         new_m = [0.9 * a + 0.1 * t for a, t in zip(m, total)]

time: 588 us -> 576 us (0.980)
  waiting for transfers between devices: 69.4 us -> 49.3 us
  Pallas kernels: 468 us -> 480 us
    ppermute x11 -> x12, waiting for transfers between devices: 69.4 us -> 49.3 us  [send(): got.append(lax.ppermute(one, 'dp', pairs))]
    pallas_call x1, Pallas kernels: 437 us -> 445 us  [inner(): pl.pallas_call(functools.partial(body, chunks, group, kinds, (2,), firsts...]
    unnamed x6 -> x28, local copies, waits for them, and re-layouts: 14.1 us -> 10.8 us
  transfers between devices with their start and end apart: 11 -> 12, of which waited for: 2 -> 2; matrix products, arithmetic and copies ran while one was open for 5% -> 5% of each run, Pallas kernels for 5% -> 6%
where the time goes in v5:
time: 576 us; the launch traced here: 575 us
  Pallas kernels  480 us (83%)
  waiting for transfers between devices  49.3 us (9%)
  other arithmetic  27.3 us (5%)
  local copies, waits for them, and re-layouts  10.8 us (2%)
  starting transfers between devices  6.71 us (1%)
    pallas_call x1, Pallas kernels, inner(): pl.pallas_call(functools.partial(body, chunks, group, kinds, (2,), firsts...  445 us
    ppermute x12, waiting for transfers between devices, send(): got.append(lax.ppermute(one, 'dp', pairs))  49.3 us
    add x2, other arithmetic, inner(): new_v = [0.95 * a + 0.05 * t * t for a, t in zip(v, total)]  27.3 us
    pallas_call x2, Pallas kernels, copy_blocks(): pl.pallas_call(kernel, out_shape=jax.ShapeDtypeStruct(a.shape, a.dtype),...  18.7 us
    pallas_call x4, Pallas kernels, place_blocks(): pl.pallas_call(kernel, out_shape=jax.ShapeDtypeStruct(shape, items[0][0]....  16.5 us
  transfers between devices with their start and end apart: 12, of which 2 were waited for; matrix products, arithmetic and copies ran while one was open for 5% of the time, Pallas kernels for 6%

profile of v5, /device:TPU:0, one launch (start us, length us, event | category | flops | bytes accessed | tf_op | source)
XLA Modules:
  0.0 575.4 jit_solution(16430234225589989113)
XLA Ops:
  0.6 445.2 %sum_step_gather.1 = (bf16[384,1152]{1,0:T(8,128)(2,1)}, bf16[1152,1152]{1,0:T(8,128)(2,1)}, bf16[768,1152]{1,0:T(8,128)(2,1)}, bf16[896,1152]{1,0:T(8,128)(2,1)...) custom-call(bf16[2,4,2,144,4608]{4,3,2,1,0:T(8,128)(2,1)} %bitcast.1, ...), custom_call_target="tpu_custom_call" | custom-call | tf_op jit(solution)/shard_map/sum_step_gather/pallas_call | solution.py:474
  445.9 1.0 collective-permute-start.3
  446.9 1.1 collective-permute-start
  447.9 0.5 collective-permute-start.6
  448.5 0.7 collective-permute-start.9
  449.1 41.6 %collective-permute-done.3.refs_3_ = bf16[896,1152]{1,0:T(8,128)(2,1)S(1)} collective-permute-done((bf16[896,1152]{1,0:T(8,128)(2,1)}, bf16[896,1152]{1,0:T(8,128)(2,1)S(1)}, u32[]{:S(2)}, u32[]{:S(2)}) %collective-permute-start.3) | collective-permute-done | bytes 2064416 | tf_op jit(solution)/shard_map/ppermute | solution.py:359
  490.8 0.5 collective-permute-start.4
  491.3 17.4 %fusion.3 = (f32[2,144,4608]{2,1,0:T(8,128)}, f32[2,144,4608]{2,1,0:T(8,128)}, f32[2,144,4608]{2,1,0:T(8,128)}, f32[2,144,4608]{2,1,0:T(8,128)}) fusion(bf16[2,144,4608]{2,1,0:T(8,128)(2,1)} %get-tuple-element.26, f32[2,144,4608]{2,1,0:T(8,128)} %refs_9_.1, f32[2,144,4608]{2,1,0:T(8,128)} %refs_6_.1, bf16[2,144,4608]{2,1,0:T(8,128)(2,1)} %get-tuple-element.27, ...), kind=kLoop, calls=%fused_computation.9 | loop fusion | flops 21233664 | bytes 47775744 | tf_op jit(solution)/shard_map/add | solution.py:491
  508.7 0.0 collective-permute-done.refs_0_
  508.7 1.5 collective-permute-start.1
  510.3 0.0 collective-permute-done.6.refs_2_
  510.3 0.0 collective-permute-start.7
  510.3 0.0 collective-permute-done.10.refs_5_
  510.3 0.0 copy-start.3
  510.3 0.5 collective-permute-start.11
  510.8 7.7 %collective-permute-done.4.refs_0_ = bf16[896,1152]{1,0:T(8,128)(2,1)} collective-permute-done((bf16[896,1152]{1,0:T(8,128)(2,1)S(1)}, bf16[896,1152]{1,0:T(8,128)(2,1)}, u32[]{:S(2)}, u32[]{:S(2)}) %collective-permute-start.4) | collective-permute-done | bytes 2064416 | tf_op jit(solution)/shard_map/ppermute | solution.py:359
  518.5 0.9 collective-permute-start.5
  519.3 9.8 %fusion.5 = (f32[2,576,1152]{2,1,0:T(8,128)}, f32[2,576,1152]{2,1,0:T(8,128)}) fusion(bf16[2,576,1152]{2,1,0:T(8,128)(2,1)S(1)} %copy-done.7, f32[2,576,1152]{2,1,0:T(8,128)} %refs_11_.1, f32[2,576,1152]{2,1,0:T(8,128)} %refs_8_.1), kind=kLoop, calls=%fused_computation.11 | loop fusion | flops 10616832 | bytes 23887872 | tf_op jit(solution)/shard_map/add | solution.py:491
  529.2 0.0 collective-permute-start.8
  529.2 0.8 copy-done.5
  530.0 7.2 %copy-done = bf16[2,4,2,144,4608]{4,3,2,1,0:T(8,128)(2,1)S(1)} copy-done((bf16[2,4,2,144,4608]{4,3,2,1,0:T(8,128)(2,1)S(1)}, bf16[2,4,2,144,4608]{4,3,2,1,0:T(8,128)(2,1)}, u32[]{:S(2)}) %copy-start) | copy-done | bytes 21233688
  537.2 10.4 %copy_blocks.2 = bf16[2,4,2,144,4608]{4,3,2,1,0:T(8,128)(2,1)} custom-call(bf16[2,4,2,144,4608]{4,3,2,1,0:T(8,128)(2,1)S(1)} %copy-done), custom_call_target="tpu_custom_call" | custom-call | flops 4000000000 | bytes 42467328 | tf_op jit(solution)/shard_map/copy_blocks/pallas_call | solution.py:299
  547.6 0.0 collective-permute-start.2
  547.7 1.6 slice-done.3
  549.3 1.2 slice-done.4
  550.5 8.3 %copy_blocks.3 = bf16[2,4,2,144,4608]{4,3,2,1,0:T(8,128)(2,1)} custom-call(bf16[2,4,2,144,4608]{4,3,2,1,0:T(8,128)(2,1)S(1)} %bitcast.10), custom_call_target="tpu_custom_call" | custom-call | flops 4000000000 | bytes 42467328 | tf_op jit(solution)/shard_map/copy_blocks/pallas_call | solution.py:299
  558.8 0.0 collective-permute-done.11.refs_6_
  558.9 7.7 %place_blocks.4.refs_3_ = bf16[2,4,2,576,1152]{4,3,2,1,0:T(8,128)(2,1)} custom-call(bf16[1152,1152]{1,0:T(8,128)(2,1)S(1)} %copy-done.1, bf16[384,1152]{1,0:T(8,128)(2,1)S(1)} %copy-done.2, bf16[768,1152]{1,0:T(8,128)(2,1)} %collective-permute-done.6.refs_2_, bf16[896,1152]{1,0:T(8,128)(2,1)S(1)} %collective-permute-done.3.refs_3_, ...), custom_call_target="tpu_custom_call" | custom-call | flops 1000000000 | bytes 25952256 | tf_op jit(solution)/shard_map/place_blocks/pallas_call | solution.py:338
  566.6 3.4 place_blocks.5.refs_2_
  570.0 0.0 collective-permute-done.5.refs_1_
  570.0 4.3 place_blocks.6.refs_2_
  574.4 1.1 place_blocks.7
  (30 shorter events, 0.1 us)
Async XLA Ops:
  445.9 44.9 %collective-permute-start.3 = (bf16[896,1152]{1,0:T(8,128)(2,1)}, bf16[896,1152]{1,0:T(8,128)(2,1)S(1)}, u32[]{:S(2)}, u32[]{:S(2)}) collective-permute-start(bf16[896,1152]{1,0:T(8,128)(2,1)} %get-tuple-element.22), channel_id=1, source_target_pairs={{0,2},{1,5},{2,0},{3,7},{4,6},{5,1},{6,4},{7,3}} | collective-permute-start | bytes 6193160 | tf_op jit(solution)/shard_map/ppermute | solution.py:359
  446.9 61.9 %collective-permute-start = (bf16[256,1152]{1,0:T(8,128)(2,1)}, bf16[256,1152]{1,0:T(8,128)(2,1)}, u32[]{:S(2)}, u32[]{:S(2)}) collective-permute-start(bf16[256,1152]{1,0:T(8,128)(2,1)} %get-tuple-element.21), channel_id=1, source_target_pairs={{0,2},{1,5},{2,0},{3,7},{4,6},{5,1},{6,4},{7,3}} | collective-permute-start | bytes 1769480 | tf_op jit(solution)/shard_map/ppermute | solution.py:359
  447.9 62.3 %collective-permute-start.10 = (bf16[384,1152]{1,0:T(8,128)(2,1)}, bf16[384,1152]{1,0:T(8,128)(2,1)S(1)}, u32[]{:S(2)}, u32[]{:S(2)}) collective-permute-start(bf16[384,1152]{1,0:T(8,128)(2,1)} %get-tuple-element.25.refs_1_), channel_id=1, source_target_pairs={{0,1},{1,0},{2,3},{3,2},{4,5},{5,4},{6,7},{7,6}} | collective-permute-start | bytes 2654216 | tf_op jit(solution)/shard_map/ppermute | solution.py:359
  447.9 62.3 %collective-permute-start.6 = (bf16[768,1152]{1,0:T(8,128)(2,1)}, bf16[768,1152]{1,0:T(8,128)(2,1)}, u32[]{:S(2)}, u32[]{:S(2)}) collective-permute-start(bf16[768,1152]{1,0:T(8,128)(2,1)} %get-tuple-element.23), channel_id=1, source_target_pairs={{0,4},{1,3},{2,6},{3,1},{4,0},{5,7},{6,2},{7,5}} | collective-permute-start | bytes 5308424 | tf_op jit(solution)/shard_map/ppermute | solution.py:359
  448.5 99.1 %collective-permute-start.9 = (bf16[1152,1152]{1,0:T(8,128)(2,1)}, bf16[1152,1152]{1,0:T(8,128)(2,1)}, u32[]{:S(2)}, u32[]{:S(2)}) collective-permute-start(bf16[1152,1152]{1,0:T(8,128)(2,1)} %get-tuple-element.24.refs_0_), channel_id=1, source_target_pairs={{0,1},{1,0},{2,3},{3,2},{4,5},{5,4},{6,7},{7,6}} | collective-permute-start | bytes 7962632 | tf_op jit(solution)/shard_map/ppermute | solution.py:359
  490.8 27.7 %collective-permute-start.4 = (bf16[896,1152]{1,0:T(8,128)(2,1)S(1)}, bf16[896,1152]{1,0:T(8,128)(2,1)}, u32[]{:S(2)}, u32[]{:S(2)}) collective-permute-start(bf16[896,1152]{1,0:T(8,128)(2,1)S(1)} %collective-permute-done.3.refs_3_), channel_id=1, source_target_pairs={{0,4},{1,3},{2,6},{3,1},{4,0},{5,7},{6,2},{7,5}} | collective-permute-start | bytes 6193160 | tf_op jit(solution)/shard_map/ppermute | solution.py:359
  491.3 28.0 %copy-start.7 = (bf16[2,576,1152]{2,1,0:T(8,128)(2,1)S(1)}, bf16[2,576,1152]{2,1,0:T(8,128)(2,1)}, u32[]{:S(2)}) copy-start(bf16[2,576,1152]{2,1,0:T(8,128)(2,1)} %get-tuple-element.28) | copy-start | bytes 7962628
  508.7 20.4 %collective-permute-start.1 = (bf16[256,1152]{1,0:T(8,128)(2,1)}, bf16[256,1152]{1,0:T(8,128)(2,1)S(1)}, u32[]{:S(2)}, u32[]{:S(2)}) collective-permute-start(bf16[256,1152]{1,0:T(8,128)(2,1)} %collective-permute-done.refs_0_), channel_id=1, source_target_pairs={{0,4},{1,3},{2,6},{3,1},{4,0},{5,7},{6,2},{7,5}} | collective-permute-start | bytes 1769480 | tf_op jit(solution)/shard_map/ppermute | solution.py:359
  510.3 56.3 %collective-permute-start.7 = (bf16[768,1152]{1,0:T(8,128)(2,1)}, bf16[768,1152]{1,0:T(8,128)(2,1)}, u32[]{:S(2)}, u32[]{:S(2)}) collective-permute-start(bf16[768,1152]{1,0:T(8,128)(2,1)} %collective-permute-done.6.refs_2_), channel_id=1, source_target_pairs={{0,1},{1,0},{2,3},{3,2},{4,5},{5,4},{6,7},{7,6}} | collective-permute-start | bytes 5308424 | tf_op jit(solution)/shard_map/ppermute | solution.py:359
  510.3 18.9 %copy-start.3 = (bf16[384,1152]{1,0:T(8,128)(2,1)}, bf16[384,1152]{1,0:T(8,128)(2,1)S(1)}, u32[]{:S(2)}) copy-start(bf16[384,1152]{1,0:T(8,128)(2,1)S(1)} %collective-permute-done.10.refs_5_) | copy-start | bytes 2654212
  510.3 48.5 %collective-permute-start.11 = (bf16[896,1152]{1,0:T(8,128)(2,1)S(1)}, bf16[896,1152]{1,0:T(8,128)(2,1)}, u32[]{:S(2)}, u32[]{:S(2)}) collective-permute-start(bf16[896,1152]{1,0:T(8,128)(2,1)S(1)} %collective-permute-done.3.refs_3_), channel_id=1, source_target_pairs={{0,1},{1,0},{2,3},{3,2},{4,5},{5,4},{6,7},{7,6}} | collective-permute-start | bytes 6193160 | tf_op jit(solution)/shard_map/ppermute | solution.py:359
  518.5 51.6 %collective-permute-start.5 = (bf16[896,1152]{1,0:T(8,128)(2,1)}, bf16[896,1152]{1,0:T(8,128)(2,1)}, u32[]{:S(2)}, u32[]{:S(2)}) collective-permute-start(bf16[896,1152]{1,0:T(8,128)(2,1)} %collective-permute-done.4.refs_0_), channel_id=1, source_target_pairs={{0,1},{1,0},{2,3},{3,2},{4,5},{5,4},{6,7},{7,6}} | collective-permute-start | bytes 6193160 | tf_op jit(solution)/shard_map/ppermute | solution.py:359
  529.2 0.8 copy-start.5
  529.2 37.4 %collective-permute-start.8 = (bf16[256,1152]{1,0:T(8,128)(2,1)}, bf16[256,1152]{1,0:T(8,128)(2,1)}, u32[]{:S(2)}, u32[]{:S(2)}) collective-permute-start(bf16[256,1152]{1,0:T(8,128)(2,1)} %collective-permute-done.refs_0_), channel_id=1, source_target_pairs={{0,1},{1,0},{2,3},{3,2},{4,5},{5,4},{6,7},{7,6}} | collective-permute-start | bytes 1769480 | tf_op jit(solution)/shard_map/ppermute | solution.py:359
  530.0 17.7 %slice-start = ((s8[21233664]{0:T(1024)(128)(4,1)}), s8[4194304]{0:T(1024)(128)(4,1)S(1)}, s32[]{:S(2)}) async-start(s8[21233664]{0:T(1024)(128)(4,1)} %bitcast.9), calls=%async_computation | async-start | bytes 8388608
  530.0 7.2 %copy-start = (bf16[2,4,2,144,4608]{4,3,2,1,0:T(8,128)(2,1)S(1)}, bf16[2,4,2,144,4608]{4,3,2,1,0:T(8,128)(2,1)}, u32[]{:S(2)}) copy-start(bf16[2,4,2,144,4608]{4,3,2,1,0:T(8,128)(2,1)} %get-tuple-element.19.src) | copy-start | bytes 63700996
  537.2 10.5 %slice-start.1 = ((s8[21233664]{0:T(1024)(128)(4,1)}), s8[4194304]{0:T(1024)(128)(4,1)S(1)}, s32[]{:S(2)}) async-start(s8[21233664]{0:T(1024)(128)(4,1)} %bitcast.9), calls=%async_computation.1 | async-start | bytes 8388608
  537.2 10.5 %slice-start.2 = ((s8[21233664]{0:T(1024)(128)(4,1)}), s8[4194304]{0:T(1024)(128)(4,1)S(1)}, s32[]{:S(2)}) async-start(s8[21233664]{0:T(1024)(128)(4,1)} %bitcast.9), calls=%async_computation.2 | async-start | bytes 8388608
  537.2 12.1 %slice-start.3 = ((s8[21233664]{0:T(1024)(128)(4,1)}), s8[4194304]{0:T(1024)(128)(4,1)S(1)}, s32[]{:S(2)}) async-start(s8[21233664]{0:T(1024)(128)(4,1)} %bitcast.9), calls=%async_computation.3 | async-start | bytes 8388608
  537.2 13.3 %slice-start.4 = ((s8[21233664]{0:T(1024)(128)(4,1)}), s8[4194304]{0:T(1024)(128)(4,1)S(1)}, s32[]{:S(2)}) async-start(s8[21233664]{0:T(1024)(128)(4,1)} %bitcast.9), calls=%async_computation.4 | async-start | bytes 8388608
  537.2 13.3 %slice-start.5 = ((s8[21233664]{0:T(1024)(128)(4,1)}), s8[262144]{0:T(1024)(128)(4,1)S(1)}, s32[]{:S(2)}) async-start(s8[21233664]{0:T(1024)(128)(4,1)} %bitcast.9), calls=%async_computation.5 | async-start | bytes 524288
  547.6 26.7 %collective-permute-start.2 = (bf16[256,1152]{1,0:T(8,128)(2,1)}, bf16[256,1152]{1,0:T(8,128)(2,1)S(1)}, u32[]{:S(2)}, u32[]{:S(2)}) collective-permute-start(bf16[256,1152]{1,0:T(8,128)(2,1)} %copy-done.5), channel_id=1, source_target_pairs={{0,1},{1,0},{2,3},{3,2},{4,5},{5,4},{6,7},{7,6}} | collective-permute-start | bytes 1769480 | tf_op jit(solution)/shard_map/ppermute | solution.py:359
  550.5 8.3 %copy-start.1 = (bf16[1152,1152]{1,0:T(8,128)(2,1)S(1)}, bf16[1152,1152]{1,0:T(8,128)(2,1)}, u32[]{:S(2)}) copy-start(bf16[1152,1152]{1,0:T(8,128)(2,1)} %get-tuple-element.24.refs_0_) | copy-start | bytes 7962628
  550.5 8.3 %copy-start.2 = (bf16[384,1152]{1,0:T(8,128)(2,1)S(1)}, bf16[384,1152]{1,0:T(8,128)(2,1)}, u32[]{:S(2)}) copy-start(bf16[384,1152]{1,0:T(8,128)(2,1)} %get-tuple-element.25.refs_1_) | copy-start | bytes 2654212
  550.5 8.3 %copy-start.4 = (bf16[384,1152]{1,0:T(8,128)(2,1)S(1)}, bf16[384,1152]{1,0:T(8,128)(2,1)}, u32[]{:S(2)}) copy-start(bf16[384,1152]{1,0:T(8,128)(2,1)} %copy-done.3) | copy-start | bytes 2654212
  570.0 4.3 copy-start.6

commit v6 on v5

--- a/solution.py
+++ b/solution.py
@@ -29,8 +29,16 @@
     return out
 
 
-TURNS = {"d": 4, "a": 4, "b": 4, "gb": 4, "ga": 6, "gab": 4, "mo": 6, "mb": 6, "mga": 8, "mgab": 8, "ah": 2}
-FIRST = {kind: sum(list(TURNS.values())[:i]) for i, kind in enumerate(TURNS)}
+TURNS = {"d": (3, 4), "a": (3, 4), "b": (2, 4), "gb": (3, 4), "ga": (3, 6), "gab": (3, 4), "mo": (3, 0), "ah": (2, 2), "d0": (4, 4), "a0": (4, 4)}
+SLICES = 4
+SHARED = 2
+
+
+def first_of(kind, end):
+    return sum(turns[end] for one, turns in list(TURNS.items())[: list(TURNS).index(kind)])
+
+
+SENDS, RECVS = (sum(turns[end] for turns in TURNS.values()) for end in (0, 1))
 
 
 class Copies:
@@ -38,15 +46,24 @@
         self.send, self.recv, self.local = send, recv, local
         self.remote, self.here = {}, {}
 
-    def start_remote(self, key, src, dst, peer):
+    def start_remote(self, key, src, dst, peer, shared=None):
         kind, k = key
-        before = (kind, k - TURNS[kind])
-        self.wait_send(before)
-        assert before not in self.remote or not self.remote[before][2]
-        n = FIRST[kind] + k % TURNS[kind]
-        c = pltpu.make_async_remote_copy(src, dst, self.send.at[n], self.recv.at[n], device_id={"dp": peer}, device_id_type=MESH)
+        sends, recvs = TURNS.get(kind, (0, 0))
+        if sends:
+            self.wait_send((kind, k - sends))
+        before = self.remote.get((kind, k - recvs)) if recvs else None
+        assert before is None or not before[2]
+        n = first_of(kind, 0) + k % sends if sends else SENDS + shared
+        i = first_of(kind, 1) + k % recvs if recvs else RECVS + shared
+        c = pltpu.make_async_remote_copy(src, dst, self.send.at[n], self.recv.at[i], device_id={"dp": peer}, device_id_type=MESH)
         c.start()
-        self.remote[key] = [c, True, True]
+        self.remote[key] = [c, sends > 0, recvs > 0]
+
+    def wait_shared(self, shared, sent, got, peer):
+        c = pltpu.make_async_remote_copy(sent, sent, self.send.at[SENDS + shared], self.recv.at[0], device_id={"dp": peer}, device_id_type=MESH)
+        c.wait_send()
+        c = pltpu.make_async_remote_copy(got, got, self.send.at[0], self.recv.at[RECVS + shared], device_id={"dp": peer}, device_id_type=MESH)
+        c.wait_recv()
 
     def wait_recv(self, key):
         c = self.remote.get(key)
@@ -115,12 +132,20 @@
         wi, layer, first, rows = chunks[k]
         return wi, layer, pl.ds(first, rows), rows, bufs[kinds[wi]], group[wi]
 
+    def slices(wi):
+        width = m[wi].shape[2] // SLICES
+        return [pl.ds(i * width, width) for i in range(SLICES)]
+
     def exchange(k):
         wi, layer, rs, _, _, _ = at(k)
         land = pland[wi].at[layer, :, rs, :]
         if k < PART:
             land = bufs[kinds[wi]][1].at[k, :, pl.ds(0, chunks[k][3]), :]
-        cp.start_remote(("d", k), g[wi].at[layer, :, 1 - c, rs, :], land, mate)
+        if k:
+            cp.start_remote(("d", k), g[wi].at[layer, :, 1 - c, rs, :], land, mate)
+            return
+        for i, part in enumerate(slices(wi)):
+            cp.start_remote(("d0", i), g[wi].at[layer, :, 1 - c, rs, part], bufs[kinds[wi]][1].at[k, :, pl.ds(0, chunks[k][3]), part], mate)
 
     def load_terms(k):
         wi, layer, rs, rows, b, _ = at(k)
@@ -132,6 +157,9 @@
     def load_a(k):
         wi, layer, rs, rows, b, _ = at(k)
         cp.wait_recv(("a", k))
+        if k == 0:
+            for i in range(SLICES):
+                cp.wait_recv(("a0", i))
         if k == count - 1:
             return
         cp.start(("recva", k), L_RECVA, aland[wi].at[layer, :, rs, :], b[4].at[:, pl.ds(0, rows), :])
@@ -151,20 +179,14 @@
         cp.wait_recv(("gb", k))
         part = wn[wi].at[layer, xy_b, c, rs, :]
         cp.start_remote(("gab", k), part, part, peer_a)
-        cp.start_remote(("mb", k), part, part, mate)
+        cp.start_remote(("mb", k), part, part, mate, wi)
 
     def forward_a(k):
         wi, layer, rs, _, _, _ = at(k)
         for kind, place in (("ga", xy_a), ("gab", xy_ab)):
             cp.wait_recv((kind, k))
             part = wn[wi].at[layer, place, c, rs, :]
-            cp.start_remote(("m" + kind, k), part, part, mate)
-
-    def settle(s):
-        cp.wait_recv(("mo", s - 3 * LAG))
-        cp.wait_recv(("mb", s - 4 * LAG))
-        cp.wait_recv(("mga", s - 5 * LAG))
-        cp.wait_recv(("mgab", s - 5 * LAG))
+            cp.start_remote(("m" + kind, k), part, part, mate, wi)
 
     def sum_mates(k):
         wi, layer, rs, rows, b, step = at(k)
@@ -172,19 +194,31 @@
         cp.wait(("own", k))
         cp.wait(("part", k))
         cp.wait_send(("a", k - SENDA))
+        if k == SENDA:
+            for i in range(SLICES):
+                cp.wait_send(("a0", i))
         so, sp, ss, sk = k % OWN, k % PART, k % SENDA, k % KEEPA
 
-        def sums(i, _):
-            r = pl.ds(pl.multiple_of(i * step, step), step)
-            for j, place in ((0, xy_ab), (1, xy_a)):
-                t = own[so, place, r, :].astype(jnp.float32) + part[sp, place, r, :].astype(jnp.float32)
-                senda[ss, j, r, :] = t.astype(jnp.bfloat16)
-            for j, place in ((0, xy_b), (1, xy)):
-                t = own[so, place, r, :].astype(jnp.float32) + part[sp, place, r, :].astype(jnp.float32)
-                keepa[sk, j, r, :] = t
-            return 0
-
-        lax.fori_loop(0, rows // step, sums, 0)
+        def sums(cols):
+            def some(i, _):
+                r = pl.ds(pl.multiple_of(i * step, step), step)
+                for j, place in ((0, xy_ab), (1, xy_a)):
+                    t = own[so, place, r, cols].astype(jnp.float32) + part[sp, place, r, cols].astype(jnp.float32)
+                    senda[ss, j, r, cols] = t.astype(jnp.bfloat16)
+                for j, place in ((0, xy_b), (1, xy)):
+                    t = own[so, place, r, cols].astype(jnp.float32) + part[sp, place, r, cols].astype(jnp.float32)
+                    keepa[sk, j, r, cols] = t
+                return 0
+
+            lax.fori_loop(0, rows // step, some, 0)
+
+        if k == 0:
+            for i, cols in enumerate(slices(wi)):
+                cp.wait_recv(("d0", i))
+                sums(cols)
+                cp.start_remote(("a0", i), senda.at[ss, :, pl.ds(0, rows), cols], aland[wi].at[layer, :, rs, cols], peer_a)
+            return
+        sums(slice(None))
         cp.start_remote(("a", k), senda.at[ss, :, pl.ds(0, rows), :], last_a if k == count - 1 else aland[wi].at[layer, :, rs, :], peer_a)
 
     def sum_a(k):
@@ -237,7 +271,7 @@
             dst = wn[wi].at[layer, xy, c, rs, :]
             cp.start_remote(("gb", k), src, dst, peer_b)
             cp.start_remote(("ga", k), src, dst, peer_a)
-            cp.start_remote(("mo", k), src, dst, mate)
+            cp.start_remote(("mo", k), src, dst, mate, wi)
         else:
             first = layer * m[wi].shape[1] + chunks[k][2]
             i = sum(first >= one for one in firsts) - 1
@@ -272,13 +306,14 @@
         when(s - 2 * LAG, load_b)
         when(s - 3 * LAG, forward_b, True)
         when(s - 4 * LAG, forward_a, True)
-        settle(s)
         if s >= 2:
             when(s, sum_mates)
         when(s - LAG, sum_a)
         when(s - 2 * LAG, update)
         if s == count - 1:
             send_ahead()
+    for wi in range(len(wn)):
+        cp.wait_shared(wi, wn[wi].at[:, pl.ds(0, 3), c], wn[wi].at[:, :, 1 - c], mate)
     cp.drain()
 
 
@@ -468,8 +503,7 @@
             ]
         wi, _, _, short = chunks[-1]
         scratch += [pltpu.VMEM((2, short, cols[wi]), bf), pltpu.VMEM((short, cols[wi]), bf)]
-        copies = sum(TURNS.values())
-        scratch += [pltpu.SemaphoreType.DMA((copies,)), pltpu.SemaphoreType.DMA((copies,)), pltpu.SemaphoreType.DMA((L_ALL,))]
+        scratch += [pltpu.SemaphoreType.DMA((SENDS + SHARED,)), pltpu.SemaphoreType.DMA((RECVS + SHARED,)), pltpu.SemaphoreType.DMA((L_ALL,))]
         hbm = pl.BlockSpec(memory_space=pl.ANY)
         res = pl.pallas_call(
             functools.partial(body, chunks, group, kinds, (2,), firsts, ahead),

time: 576 us -> 575 us (level)
  no operation moved by 1% of the time
where the time goes in v6:
time: 575 us
  Pallas kernels  480 us (83%)
  waiting for transfers between devices  49.6 us (9%)
  other arithmetic  27.3 us (5%)
  local copies, waits for them, and re-layouts  10.8 us (2%)
  starting transfers between devices  6.45 us (1%)
    pallas_call x1, Pallas kernels, inner(): pl.pallas_call(functools.partial(body, chunks, group, kinds, (2,), firsts...  445 us
    ppermute x12, waiting for transfers between devices, send(): got.append(lax.ppermute(one, 'dp', pairs))  49.6 us
    add x2, other arithmetic, inner(): new_v = [0.95 * a + 0.05 * t * t for a, t in zip(v, total)]  27.3 us
    pallas_call x2, Pallas kernels, copy_blocks(): pl.pallas_call(kernel, out_shape=jax.ShapeDtypeStruct(a.shape, a.dtype),...  18.7 us
    pallas_call x4, Pallas kernels, place_blocks(): pl.pallas_call(kernel, out_shape=jax.ShapeDtypeStruct(shape, items[0][0]....  16.5 us
  transfers between devices with their start and end apart: 12, of which 2 were waited for; matrix products, arithmetic and copies ran while one was open for 5% of the time, Pallas kernels for 6%

profile of v6, /device:TPU:0, one launch (start us, length us, event | category | flops | bytes accessed | tf_op | source)
XLA Modules:
  0.0 574.7 jit_solution(7388978177920709577)
XLA Ops:
  0.6 444.6 %sum_step_gather.1 = (bf16[384,1152]{1,0:T(8,128)(2,1)}, bf16[1152,1152]{1,0:T(8,128)(2,1)}, bf16[768,1152]{1,0:T(8,128)(2,1)}, bf16[896,1152]{1,0:T(8,128)(2,1)...) custom-call(bf16[2,4,2,144,4608]{4,3,2,1,0:T(8,128)(2,1)} %bitcast.1, ...), custom_call_target="tpu_custom_call" | custom-call | tf_op jit(solution)/shard_map/sum_step_gather/pallas_call | solution.py:508
  445.2 0.5 collective-permute-start.3
  445.8 1.5 collective-permute-start
  447.3 0.0 collective-permute-start.10
  447.3 0.5 collective-permute-start.6
  447.8 0.2 collective-permute-start.9
  448.0 42.1 %collective-permute-done.3.refs_3_ = bf16[896,1152]{1,0:T(8,128)(2,1)S(1)} collective-permute-done((bf16[896,1152]{1,0:T(8,128)(2,1)}, bf16[896,1152]{1,0:T(8,128)(2,1)S(1)}, u32[]{:S(2)}, u32[]{:S(2)}) %collective-permute-start.3) | collective-permute-done | bytes 2064416 | tf_op jit(solution)/shard_map/ppermute | solution.py:394
  490.1 0.5 collective-permute-start.4
  490.7 17.4 %fusion.3 = (f32[2,144,4608]{2,1,0:T(8,128)}, f32[2,144,4608]{2,1,0:T(8,128)}, f32[2,144,4608]{2,1,0:T(8,128)}, f32[2,144,4608]{2,1,0:T(8,128)}) fusion(bf16[2,144,4608]{2,1,0:T(8,128)(2,1)} %get-tuple-element.26, f32[2,144,4608]{2,1,0:T(8,128)} %refs_9_.1, f32[2,144,4608]{2,1,0:T(8,128)} %refs_6_.1, bf16[2,144,4608]{2,1,0:T(8,128)(2,1)} %get-tuple-element.27, ...), kind=kLoop, calls=%fused_computation.9 | loop fusion | flops 21233664 | bytes 47775744 | tf_op jit(solution)/shard_map/add | solution.py:525
  508.1 0.0 collective-permute-done.refs_0_
  508.1 1.5 collective-permute-start.1
  509.6 0.0 collective-permute-done.6.refs_2_
  509.6 0.0 collective-permute-start.7
  509.6 0.0 collective-permute-done.10.refs_5_
  509.6 0.0 copy-start.3
  509.6 0.5 collective-permute-start.11
  510.1 7.5 %collective-permute-done.4.refs_0_ = bf16[896,1152]{1,0:T(8,128)(2,1)} collective-permute-done((bf16[896,1152]{1,0:T(8,128)(2,1)S(1)}, bf16[896,1152]{1,0:T(8,128)(2,1)}, u32[]{:S(2)}, u32[]{:S(2)}) %collective-permute-start.4) | collective-permute-done | bytes 2064416 | tf_op jit(solution)/shard_map/ppermute | solution.py:394
  517.6 1.0 collective-permute-start.5
  518.7 9.8 %fusion.5 = (f32[2,576,1152]{2,1,0:T(8,128)}, f32[2,576,1152]{2,1,0:T(8,128)}) fusion(bf16[2,576,1152]{2,1,0:T(8,128)(2,1)S(1)} %copy-done.7, f32[2,576,1152]{2,1,0:T(8,128)} %refs_11_.1, f32[2,576,1152]{2,1,0:T(8,128)} %refs_8_.1), kind=kLoop, calls=%fused_computation.11 | loop fusion | flops 10616832 | bytes 23887872 | tf_op jit(solution)/shard_map/add | solution.py:525
  528.5 0.0 collective-permute-done.1.refs_0_
  528.5 0.0 collective-permute-start.8
  528.6 0.8 copy-done.5
  529.3 7.2 %copy-done = bf16[2,4,2,144,4608]{4,3,2,1,0:T(8,128)(2,1)S(1)} copy-done((bf16[2,4,2,144,4608]{4,3,2,1,0:T(8,128)(2,1)S(1)}, bf16[2,4,2,144,4608]{4,3,2,1,0:T(8,128)(2,1)}, u32[]{:S(2)}) %copy-start) | copy-done | bytes 21233688
  536.5 10.4 %copy_blocks.2 = bf16[2,4,2,144,4608]{4,3,2,1,0:T(8,128)(2,1)} custom-call(bf16[2,4,2,144,4608]{4,3,2,1,0:T(8,128)(2,1)S(1)} %copy-done), custom_call_target="tpu_custom_call" | custom-call | flops 4000000000 | bytes 42467328 | tf_op jit(solution)/shard_map/copy_blocks/pallas_call | solution.py:334
  547.0 0.0 collective-permute-start.2
  547.0 1.6 slice-done.3
  548.7 1.2 slice-done.4
  549.9 8.3 %copy_blocks.3 = bf16[2,4,2,144,4608]{4,3,2,1,0:T(8,128)(2,1)} custom-call(bf16[2,4,2,144,4608]{4,3,2,1,0:T(8,128)(2,1)S(1)} %bitcast.10), custom_call_target="tpu_custom_call" | custom-call | flops 4000000000 | bytes 42467328 | tf_op jit(solution)/shard_map/copy_blocks/pallas_call | solution.py:334
  558.2 7.7 %place_blocks.4.refs_3_ = bf16[2,4,2,576,1152]{4,3,2,1,0:T(8,128)(2,1)} custom-call(bf16[1152,1152]{1,0:T(8,128)(2,1)S(1)} %copy-done.1, bf16[384,1152]{1,0:T(8,128)(2,1)S(1)} %copy-done.2, bf16[768,1152]{1,0:T(8,128)(2,1)} %collective-permute-done.6.refs_2_, bf16[896,1152]{1,0:T(8,128)(2,1)S(1)} %collective-permute-done.3.refs_3_, ...), custom_call_target="tpu_custom_call" | custom-call | flops 1000000000 | bytes 25952256 | tf_op jit(solution)/shard_map/place_blocks/pallas_call | solution.py:373
  566.0 3.4 place_blocks.5.refs_2_
  569.4 4.3 place_blocks.6.refs_2_
  573.7 1.1 place_blocks.7
  (30 shorter events, 0.1 us)
Async XLA Ops:
  445.2 44.9 %collective-permute-start.3 = (bf16[896,1152]{1,0:T(8,128)(2,1)}, bf16[896,1152]{1,0:T(8,128)(2,1)S(1)}, u32[]{:S(2)}, u32[]{:S(2)}) collective-permute-start(bf16[896,1152]{1,0:T(8,128)(2,1)} %get-tuple-element.22), channel_id=1, source_target_pairs={{0,2},{1,5},{2,0},{3,7},{4,6},{5,1},{6,4},{7,3}} | collective-permute-start | bytes 6193160 | tf_op jit(solution)/shard_map/ppermute | solution.py:394
  445.8 62.3 %collective-permute-start = (bf16[256,1152]{1,0:T(8,128)(2,1)}, bf16[256,1152]{1,0:T(8,128)(2,1)}, u32[]{:S(2)}, u32[]{:S(2)}) collective-permute-start(bf16[256,1152]{1,0:T(8,128)(2,1)} %get-tuple-element.21), channel_id=1, source_target_pairs={{0,2},{1,5},{2,0},{3,7},{4,6},{5,1},{6,4},{7,3}} | collective-permute-start | bytes 1769480 | tf_op jit(solution)/shard_map/ppermute | solution.py:394
  447.3 62.3 %collective-permute-start.10 = (bf16[384,1152]{1,0:T(8,128)(2,1)}, bf16[384,1152]{1,0:T(8,128)(2,1)S(1)}, u32[]{:S(2)}, u32[]{:S(2)}) collective-permute-start(bf16[384,1152]{1,0:T(8,128)(2,1)} %get-tuple-element.25.refs_1_), channel_id=1, source_target_pairs={{0,1},{1,0},{2,3},{3,2},{4,5},{5,4},{6,7},{7,6}} | collective-permute-start | bytes 2654216 | tf_op jit(solution)/shard_map/ppermute | solution.py:394
  447.3 62.3 %collective-permute-start.6 = (bf16[768,1152]{1,0:T(8,128)(2,1)}, bf16[768,1152]{1,0:T(8,128)(2,1)}, u32[]{:S(2)}, u32[]{:S(2)}) collective-permute-start(bf16[768,1152]{1,0:T(8,128)(2,1)} %get-tuple-element.23), channel_id=1, source_target_pairs={{0,4},{1,3},{2,6},{3,1},{4,0},{5,7},{6,2},{7,5}} | collective-permute-start | bytes 5308424 | tf_op jit(solution)/shard_map/ppermute | solution.py:394
  447.8 99.1 %collective-permute-start.9 = (bf16[1152,1152]{1,0:T(8,128)(2,1)}, bf16[1152,1152]{1,0:T(8,128)(2,1)}, u32[]{:S(2)}, u32[]{:S(2)}) collective-permute-start(bf16[1152,1152]{1,0:T(8,128)(2,1)} %get-tuple-element.24.refs_0_), channel_id=1, source_target_pairs={{0,1},{1,0},{2,3},{3,2},{4,5},{5,4},{6,7},{7,6}} | collective-permute-start | bytes 7962632 | tf_op jit(solution)/shard_map/ppermute | solution.py:394
  490.1 27.5 %collective-permute-start.4 = (bf16[896,1152]{1,0:T(8,128)(2,1)S(1)}, bf16[896,1152]{1,0:T(8,128)(2,1)}, u32[]{:S(2)}, u32[]{:S(2)}) collective-permute-start(bf16[896,1152]{1,0:T(8,128)(2,1)S(1)} %collective-permute-done.3.refs_3_), channel_id=1, source_target_pairs={{0,4},{1,3},{2,6},{3,1},{4,0},{5,7},{6,2},{7,5}} | collective-permute-start | bytes 6193160 | tf_op jit(solution)/shard_map/ppermute | solution.py:394
  490.6 28.0 %copy-start.7 = (bf16[2,576,1152]{2,1,0:T(8,128)(2,1)S(1)}, bf16[2,576,1152]{2,1,0:T(8,128)(2,1)}, u32[]{:S(2)}) copy-start(bf16[2,576,1152]{2,1,0:T(8,128)(2,1)} %get-tuple-element.28) | copy-start | bytes 7962628
  508.1 20.4 %collective-permute-start.1 = (bf16[256,1152]{1,0:T(8,128)(2,1)}, bf16[256,1152]{1,0:T(8,128)(2,1)S(1)}, u32[]{:S(2)}, u32[]{:S(2)}) collective-permute-start(bf16[256,1152]{1,0:T(8,128)(2,1)} %collective-permute-done.refs_0_), channel_id=1, source_target_pairs={{0,4},{1,3},{2,6},{3,1},{4,0},{5,7},{6,2},{7,5}} | collective-permute-start | bytes 1769480 | tf_op jit(solution)/shard_map/ppermute | solution.py:394
  509.6 56.3 %collective-permute-start.7 = (bf16[768,1152]{1,0:T(8,128)(2,1)}, bf16[768,1152]{1,0:T(8,128)(2,1)}, u32[]{:S(2)}, u32[]{:S(2)}) collective-permute-start(bf16[768,1152]{1,0:T(8,128)(2,1)} %collective-permute-done.6.refs_2_), channel_id=1, source_target_pairs={{0,1},{1,0},{2,3},{3,2},{4,5},{5,4},{6,7},{7,6}} | collective-permute-start | bytes 5308424 | tf_op jit(solution)/shard_map/ppermute | solution.py:394
  509.6 18.9 %copy-start.3 = (bf16[384,1152]{1,0:T(8,128)(2,1)}, bf16[384,1152]{1,0:T(8,128)(2,1)S(1)}, u32[]{:S(2)}) copy-start(bf16[384,1152]{1,0:T(8,128)(2,1)S(1)} %collective-permute-done.10.refs_5_) | copy-start | bytes 2654212
  509.6 48.5 %collective-permute-start.11 = (bf16[896,1152]{1,0:T(8,128)(2,1)S(1)}, bf16[896,1152]{1,0:T(8,128)(2,1)}, u32[]{:S(2)}, u32[]{:S(2)}) collective-permute-start(bf16[896,1152]{1,0:T(8,128)(2,1)S(1)} %collective-permute-done.3.refs_3_), channel_id=1, source_target_pairs={{0,1},{1,0},{2,3},{3,2},{4,5},{5,4},{6,7},{7,6}} | collective-permute-start | bytes 6193160 | tf_op jit(solution)/shard_map/ppermute | solution.py:394
  517.6 51.8 %collective-permute-start.5 = (bf16[896,1152]{1,0:T(8,128)(2,1)}, bf16[896,1152]{1,0:T(8,128)(2,1)}, u32[]{:S(2)}, u32[]{:S(2)}) collective-permute-start(bf16[896,1152]{1,0:T(8,128)(2,1)} %collective-permute-done.4.refs_0_), channel_id=1, source_target_pairs={{0,1},{1,0},{2,3},{3,2},{4,5},{5,4},{6,7},{7,6}} | collective-permute-start | bytes 6193160 | tf_op jit(solution)/shard_map/ppermute | solution.py:394
  528.5 0.8 copy-start.5
  528.5 37.4 %collective-permute-start.8 = (bf16[256,1152]{1,0:T(8,128)(2,1)}, bf16[256,1152]{1,0:T(8,128)(2,1)}, u32[]{:S(2)}, u32[]{:S(2)}) collective-permute-start(bf16[256,1152]{1,0:T(8,128)(2,1)} %collective-permute-done.refs_0_), channel_id=1, source_target_pairs={{0,1},{1,0},{2,3},{3,2},{4,5},{5,4},{6,7},{7,6}} | collective-permute-start | bytes 1769480 | tf_op jit(solution)/shard_map/ppermute | solution.py:394
  529.3 17.7 %slice-start = ((s8[21233664]{0:T(1024)(128)(4,1)}), s8[4194304]{0:T(1024)(128)(4,1)S(1)}, s32[]{:S(2)}) async-start(s8[21233664]{0:T(1024)(128)(4,1)} %bitcast.9), calls=%async_computation | async-start | bytes 8388608
  529.3 7.2 %copy-start = (bf16[2,4,2,144,4608]{4,3,2,1,0:T(8,128)(2,1)S(1)}, bf16[2,4,2,144,4608]{4,3,2,1,0:T(8,128)(2,1)}, u32[]{:S(2)}) copy-start(bf16[2,4,2,144,4608]{4,3,2,1,0:T(8,128)(2,1)} %get-tuple-element.19.src) | copy-start | bytes 63700996
  536.5 10.5 %slice-start.1 = ((s8[21233664]{0:T(1024)(128)(4,1)}), s8[4194304]{0:T(1024)(128)(4,1)S(1)}, s32[]{:S(2)}) async-start(s8[21233664]{0:T(1024)(128)(4,1)} %bitcast.9), calls=%async_computation.1 | async-start | bytes 8388608
  536.5 10.5 %slice-start.2 = ((s8[21233664]{0:T(1024)(128)(4,1)}), s8[4194304]{0:T(1024)(128)(4,1)S(1)}, s32[]{:S(2)}) async-start(s8[21233664]{0:T(1024)(128)(4,1)} %bitcast.9), calls=%async_computation.2 | async-start | bytes 8388608
  536.5 12.1 %slice-start.3 = ((s8[21233664]{0:T(1024)(128)(4,1)}), s8[4194304]{0:T(1024)(128)(4,1)S(1)}, s32[]{:S(2)}) async-start(s8[21233664]{0:T(1024)(128)(4,1)} %bitcast.9), calls=%async_computation.3 | async-start | bytes 8388608
  536.5 13.3 %slice-start.4 = ((s8[21233664]{0:T(1024)(128)(4,1)}), s8[4194304]{0:T(1024)(128)(4,1)S(1)}, s32[]{:S(2)}) async-start(s8[21233664]{0:T(1024)(128)(4,1)} %bitcast.9), calls=%async_computation.4 | async-start | bytes 8388608
  536.5 13.3 %slice-start.5 = ((s8[21233664]{0:T(1024)(128)(4,1)}), s8[262144]{0:T(1024)(128)(4,1)S(1)}, s32[]{:S(2)}) async-start(s8[21233664]{0:T(1024)(128)(4,1)} %bitcast.9), calls=%async_computation.5 | async-start | bytes 524288
  547.0 26.7 %collective-permute-start.2 = (bf16[256,1152]{1,0:T(8,128)(2,1)}, bf16[256,1152]{1,0:T(8,128)(2,1)S(1)}, u32[]{:S(2)}, u32[]{:S(2)}) collective-permute-start(bf16[256,1152]{1,0:T(8,128)(2,1)} %copy-done.5), channel_id=1, source_target_pairs={{0,1},{1,0},{2,3},{3,2},{4,5},{5,4},{6,7},{7,6}} | collective-permute-start | bytes 1769480 | tf_op jit(solution)/shard_map/ppermute | solution.py:394
  549.9 8.3 %copy-start.1 = (bf16[1152,1152]{1,0:T(8,128)(2,1)S(1)}, bf16[1152,1152]{1,0:T(8,128)(2,1)}, u32[]{:S(2)}) copy-start(bf16[1152,1152]{1,0:T(8,128)(2,1)} %get-tuple-element.24.refs_0_) | copy-start | bytes 7962628
  549.9 8.3 %copy-start.2 = (bf16[384,1152]{1,0:T(8,128)(2,1)S(1)}, bf16[384,1152]{1,0:T(8,128)(2,1)}, u32[]{:S(2)}) copy-start(bf16[384,1152]{1,0:T(8,128)(2,1)} %get-tuple-element.25.refs_1_) | copy-start | bytes 2654212
  549.9 8.3 %copy-start.4 = (bf16[384,1152]{1,0:T(8,128)(2,1)S(1)}, bf16[384,1152]{1,0:T(8,128)(2,1)}, u32[]{:S(2)}) copy-start(bf16[384,1152]{1,0:T(8,128)(2,1)} %copy-done.3) | copy-start | bytes 2654212
  569.4 4.3 copy-start.6

commit v7 on v6

--- a/solution.py
+++ b/solution.py
@@ -98,7 +98,7 @@
 
 
 OWN, PART, SENDA, KEEPA, SENDB, KEEPB, GOUT, WNEW = 2, 2, 3, 3, 2, 3, 2, 4
-L_OWN, L_PART, L_RECVA, L_RECVB, L_M, L_V, L_W, L_G, L_WN, L_BLOCK, L_REST, L_ALL = 0, 2, 4, 5, 6, 7, 8, 9, 11, 15, 19, 23
+L_OWN, L_PART, L_RECVA, L_RECVB, L_M, L_V, L_W, L_G, L_WN, L_BLOCK, L_REST, L_STAGE, L_ALL = 0, 2, 4, 5, 6, 7, 8, 9, 11, 15, 19, 23, 24
 
 
 def body(chunks, group, kinds, outside, firsts, ahead, *refs):
@@ -107,7 +107,7 @@
     own_pieces, refs = refs[15 : 15 + len(firsts)], refs[:12] + refs[15 + len(firsts) :]
     wn, gs, pland, aland, bland = refs[12:14], refs[14:17], refs[17:20], refs[20:23], refs[23:26]
     bufs = (refs[26:39], refs[39:52])
-    last_a, last_b, send, recv, local = refs[52:57]
+    last_a, last_b, stage, send, recv, local = refs[52:58]
 
     me = lax.axis_index("dp")
     x, y, c = me // 4, (me // 2) % 2, me % 2
@@ -120,6 +120,14 @@
     xy_b = xy_y + c * (xy_x - xy_y)
     xy_ab = 3 - xy
 
+    wi, layer, first, rows = chunks[0]
+    early = [
+        pltpu.make_async_copy(g[wi].at[layer, :, 1 - c, pl.ds(first, rows), :], stage, local.at[L_STAGE]),
+        pltpu.make_async_copy(g[wi].at[layer, :, c, pl.ds(first, rows), :], bufs[kinds[wi]][0].at[0, :, pl.ds(0, rows), :], local.at[L_OWN]),
+    ]
+    for one in early:
+        one.start()
+
     barrier = pltpu.get_barrier_semaphore()
     for peer in (peer_a, peer_b, mate):
         pl.semaphore_signal(barrier, inc=1, device_id={"dp": peer}, device_id_type=MESH)
@@ -144,12 +152,14 @@
         if k:
             cp.start_remote(("d", k), g[wi].at[layer, :, 1 - c, rs, :], land, mate)
             return
+        early[0].wait()
         for i, part in enumerate(slices(wi)):
-            cp.start_remote(("d0", i), g[wi].at[layer, :, 1 - c, rs, part], bufs[kinds[wi]][1].at[k, :, pl.ds(0, chunks[k][3]), part], mate)
+            cp.start_remote(("d0", i), stage.at[:, :, part], bufs[kinds[wi]][1].at[k, :, pl.ds(0, chunks[k][3]), part], mate)
 
     def load_terms(k):
         wi, layer, rs, rows, b, _ = at(k)
-        cp.start(("own", k), L_OWN + k % OWN, g[wi].at[layer, :, c, rs, :], b[0].at[k % OWN, :, pl.ds(0, rows), :])
+        if k:
+            cp.start(("own", k), L_OWN + k % OWN, g[wi].at[layer, :, c, rs, :], b[0].at[k % OWN, :, pl.ds(0, rows), :])
         cp.wait_recv(("d", k))
         if k >= PART:
             cp.start(("part", k), L_PART + k % PART, pland[wi].at[layer, :, rs, :], b[1].at[k % PART, :, pl.ds(0, rows), :])
@@ -192,6 +202,8 @@
         wi, layer, rs, rows, b, step = at(k)
         own, part, senda, keepa = b[0], b[1], b[2], b[3]
         cp.wait(("own", k))
+        if k == 0:
+            early[1].wait()
         cp.wait(("part", k))
         cp.wait_send(("a", k - SENDA))
         if k == SENDA:
@@ -443,7 +455,8 @@
         ],
         [(from_b[1], second, at_b), (mate_a[1], ahead, of_mate(at_a)), (mate_b[1], second, of_mate(at_b))],
         [(from_ab[0], first, at_ab), (mate_ab[0], first, of_mate(at_ab))],
-        [(from_ab[1], second, at_ab), (mate_ab[1], second, of_mate(at_ab))],
+        [(from_ab[1], second, at_ab)],
+        [(mate_ab[1], second, of_mate(at_ab))],
     ]
     whole = None
     for items in steps:
@@ -503,6 +516,7 @@
             ]
         wi, _, _, short = chunks[-1]
         scratch += [pltpu.VMEM((2, short, cols[wi]), bf), pltpu.VMEM((short, cols[wi]), bf)]
+        scratch += [pltpu.VMEM((n // 2, chunks[0][3], cols[chunks[0][0]]), bf)]
         scratch += [pltpu.SemaphoreType.DMA((SENDS + SHARED,)), pltpu.SemaphoreType.DMA((RECVS + SHARED,)), pltpu.SemaphoreType.DMA((L_ALL,))]
         hbm = pl.BlockSpec(memory_space=pl.ANY)
         res = pl.pallas_call(

time: 575 us -> 575 us (level)
    pallas_call x4 -> x5, Pallas kernels: 16.5 us -> 17.1 us  [place_blocks(): pl.pallas_call(kernel, out_shape=jax.ShapeDtypeStruct(shape, items[0][0]....]
where the time goes in v7:
time: 575 us
  Pallas kernels  480 us (83%)
  waiting for transfers between devices  49 us (9%)
  other arithmetic  27.3 us (5%)
  local copies, waits for them, and re-layouts  10.8 us (2%)
  starting transfers between devices  7.08 us (1%)
    pallas_call x1, Pallas kernels, inner(): pl.pallas_call(functools.partial(body, chunks, group, kinds, (2,), firsts...  444 us
    ppermute x12, waiting for transfers between devices, send(): got.append(lax.ppermute(one, 'dp', pairs))  49 us
    add x2, other arithmetic, inner(): new_v = [0.95 * a + 0.05 * t * t for a, t in zip(v, total)]  27.3 us
    pallas_call x2, Pallas kernels, copy_blocks(): pl.pallas_call(kernel, out_shape=jax.ShapeDtypeStruct(a.shape, a.dtype),...  18.7 us
    pallas_call x5, Pallas kernels, place_blocks(): pl.pallas_call(kernel, out_shape=jax.ShapeDtypeStruct(shape, items[0][0]....  17.1 us
  transfers between devices with their start and end apart: 12, of which 2 were waited for; matrix products, arithmetic and copies ran while one was open for 5% of the time, Pallas kernels for 6%

profile of v7, /device:TPU:0, one launch (start us, length us, event | category | flops | bytes accessed | tf_op | source)
XLA Modules:
  0.0 574.8 jit_solution(1349906791452844478)
XLA Ops:
  0.6 443.9 %sum_step_gather.1 = (bf16[384,1152]{1,0:T(8,128)(2,1)}, bf16[1152,1152]{1,0:T(8,128)(2,1)}, bf16[768,1152]{1,0:T(8,128)(2,1)}, bf16[896,1152]{1,0:T(8,128)(2,1)...) custom-call(bf16[2,4,2,144,4608]{4,3,2,1,0:T(8,128)(2,1)} %bitcast.1, ...), custom_call_target="tpu_custom_call" | custom-call | tf_op jit(solution)/shard_map/sum_step_gather/pallas_call | solution.py:522
  444.6 1.4 collective-permute-start.3
  446.0 0.7 collective-permute-start
  446.6 0.6 collective-permute-start.6
  447.2 1.0 collective-permute-start.9
  448.2 41.3 %collective-permute-done.3.refs_3_ = bf16[896,1152]{1,0:T(8,128)(2,1)S(1)} collective-permute-done((bf16[896,1152]{1,0:T(8,128)(2,1)}, bf16[896,1152]{1,0:T(8,128)(2,1)S(1)}, u32[]{:S(2)}, u32[]{:S(2)}) %collective-permute-start.3) | collective-permute-done | bytes 2064416 | tf_op jit(solution)/shard_map/ppermute | solution.py:406
  489.5 0.5 collective-permute-start.4
  490.0 17.4 %fusion.3 = (f32[2,144,4608]{2,1,0:T(8,128)}, f32[2,144,4608]{2,1,0:T(8,128)}, f32[2,144,4608]{2,1,0:T(8,128)}, f32[2,144,4608]{2,1,0:T(8,128)}) fusion(bf16[2,144,4608]{2,1,0:T(8,128)(2,1)} %get-tuple-element.26, f32[2,144,4608]{2,1,0:T(8,128)} %refs_9_.1, f32[2,144,4608]{2,1,0:T(8,128)} %refs_6_.1, bf16[2,144,4608]{2,1,0:T(8,128)(2,1)} %get-tuple-element.27, ...), kind=kLoop, calls=%fused_computation.9 | loop fusion | flops 21233664 | bytes 47775744 | tf_op jit(solution)/shard_map/add | solution.py:539
  507.4 0.0 collective-permute-done.refs_0_
  507.4 1.5 collective-permute-start.1
  509.0 0.0 collective-permute-done.6.refs_2_
  509.0 0.0 collective-permute-start.7
  509.0 0.0 collective-permute-done.10.refs_5_
  509.0 0.0 copy-start.3
  509.0 0.5 collective-permute-start.11
  509.5 7.7 %collective-permute-done.4.refs_0_ = bf16[896,1152]{1,0:T(8,128)(2,1)} collective-permute-done((bf16[896,1152]{1,0:T(8,128)(2,1)S(1)}, bf16[896,1152]{1,0:T(8,128)(2,1)}, u32[]{:S(2)}, u32[]{:S(2)}) %collective-permute-start.4) | collective-permute-done | bytes 2064416 | tf_op jit(solution)/shard_map/ppermute | solution.py:406
  517.2 0.9 collective-permute-start.5
  518.0 9.8 %fusion.5 = (f32[2,576,1152]{2,1,0:T(8,128)}, f32[2,576,1152]{2,1,0:T(8,128)}) fusion(bf16[2,576,1152]{2,1,0:T(8,128)(2,1)S(1)} %copy-done.7, f32[2,576,1152]{2,1,0:T(8,128)} %refs_11_.1, f32[2,576,1152]{2,1,0:T(8,128)} %refs_8_.1), kind=kLoop, calls=%fused_computation.11 | loop fusion | flops 10616832 | bytes 23887872 | tf_op jit(solution)/shard_map/add | solution.py:539
  527.9 0.0 collective-permute-start.8
  527.9 0.8 copy-done.5
  528.7 7.2 %copy-done = bf16[2,4,2,144,4608]{4,3,2,1,0:T(8,128)(2,1)S(1)} copy-done((bf16[2,4,2,144,4608]{4,3,2,1,0:T(8,128)(2,1)S(1)}, bf16[2,4,2,144,4608]{4,3,2,1,0:T(8,128)(2,1)}, u32[]{:S(2)}) %copy-start) | copy-done | bytes 21233688
  535.9 0.0 slice-start.5
  535.9 10.4 %copy_blocks.2 = bf16[2,4,2,144,4608]{4,3,2,1,0:T(8,128)(2,1)} custom-call(bf16[2,4,2,144,4608]{4,3,2,1,0:T(8,128)(2,1)S(1)} %copy-done), custom_call_target="tpu_custom_call" | custom-call | flops 4000000000 | bytes 42467328 | tf_op jit(solution)/shard_map/copy_blocks/pallas_call | solution.py:346
  546.3 0.0 collective-permute-start.2
  546.4 1.6 slice-done.3
  548.0 1.2 slice-done.4
  549.2 8.3 %copy_blocks.3 = bf16[2,4,2,144,4608]{4,3,2,1,0:T(8,128)(2,1)} custom-call(bf16[2,4,2,144,4608]{4,3,2,1,0:T(8,128)(2,1)S(1)} %bitcast.10), custom_call_target="tpu_custom_call" | custom-call | flops 4000000000 | bytes 42467328 | tf_op jit(solution)/shard_map/copy_blocks/pallas_call | solution.py:346
  557.6 7.7 %place_blocks.5.refs_3_ = bf16[2,4,2,576,1152]{4,3,2,1,0:T(8,128)(2,1)} custom-call(bf16[1152,1152]{1,0:T(8,128)(2,1)S(1)} %copy-done.1, bf16[384,1152]{1,0:T(8,128)(2,1)S(1)} %copy-done.2, bf16[768,1152]{1,0:T(8,128)(2,1)} %collective-permute-done.6.refs_2_, bf16[896,1152]{1,0:T(8,128)(2,1)S(1)} %collective-permute-done.3.refs_3_, ...), custom_call_target="tpu_custom_call" | custom-call | flops 1000000000 | bytes 25952256 | tf_op jit(solution)/shard_map/place_blocks/pallas_call | solution.py:385
  565.3 3.4 place_blocks.6.refs_2_
  568.7 4.3 place_blocks.7.refs_1_
  573.0 0.8 place_blocks.8.refs_1_
  573.9 0.8 place_blocks.9
  (31 shorter events, 0.1 us)
Async XLA Ops:
  444.6 44.9 %collective-permute-start.3 = (bf16[896,1152]{1,0:T(8,128)(2,1)}, bf16[896,1152]{1,0:T(8,128)(2,1)S(1)}, u32[]{:S(2)}, u32[]{:S(2)}) collective-permute-start(bf16[896,1152]{1,0:T(8,128)(2,1)} %get-tuple-element.22), channel_id=1, source_target_pairs={{0,2},{1,5},{2,0},{3,7},{4,6},{5,1},{6,4},{7,3}} | collective-permute-start | bytes 6193160 | tf_op jit(solution)/shard_map/ppermute | solution.py:406
  446.0 61.5 %collective-permute-start = (bf16[256,1152]{1,0:T(8,128)(2,1)}, bf16[256,1152]{1,0:T(8,128)(2,1)}, u32[]{:S(2)}, u32[]{:S(2)}) collective-permute-start(bf16[256,1152]{1,0:T(8,128)(2,1)} %get-tuple-element.21), channel_id=1, source_target_pairs={{0,2},{1,5},{2,0},{3,7},{4,6},{5,1},{6,4},{7,3}} | collective-permute-start | bytes 1769480 | tf_op jit(solution)/shard_map/ppermute | solution.py:406
  446.6 62.3 %collective-permute-start.10 = (bf16[384,1152]{1,0:T(8,128)(2,1)}, bf16[384,1152]{1,0:T(8,128)(2,1)S(1)}, u32[]{:S(2)}, u32[]{:S(2)}) collective-permute-start(bf16[384,1152]{1,0:T(8,128)(2,1)} %get-tuple-element.25.refs_1_), channel_id=1, source_target_pairs={{0,1},{1,0},{2,3},{3,2},{4,5},{5,4},{6,7},{7,6}} | collective-permute-start | bytes 2654216 | tf_op jit(solution)/shard_map/ppermute | solution.py:406
  446.6 62.3 %collective-permute-start.6 = (bf16[768,1152]{1,0:T(8,128)(2,1)}, bf16[768,1152]{1,0:T(8,128)(2,1)}, u32[]{:S(2)}, u32[]{:S(2)}) collective-permute-start(bf16[768,1152]{1,0:T(8,128)(2,1)} %get-tuple-element.23), channel_id=1, source_target_pairs={{0,4},{1,3},{2,6},{3,1},{4,0},{5,7},{6,2},{7,5}} | collective-permute-start | bytes 5308424 | tf_op jit(solution)/shard_map/ppermute | solution.py:406
  447.2 99.1 %collective-permute-start.9 = (bf16[1152,1152]{1,0:T(8,128)(2,1)}, bf16[1152,1152]{1,0:T(8,128)(2,1)}, u32[]{:S(2)}, u32[]{:S(2)}) collective-permute-start(bf16[1152,1152]{1,0:T(8,128)(2,1)} %get-tuple-element.24.refs_0_), channel_id=1, source_target_pairs={{0,1},{1,0},{2,3},{3,2},{4,5},{5,4},{6,7},{7,6}} | collective-permute-start | bytes 7962632 | tf_op jit(solution)/shard_map/ppermute | solution.py:406
  489.5 27.7 %collective-permute-start.4 = (bf16[896,1152]{1,0:T(8,128)(2,1)S(1)}, bf16[896,1152]{1,0:T(8,128)(2,1)}, u32[]{:S(2)}, u32[]{:S(2)}) collective-permute-start(bf16[896,1152]{1,0:T(8,128)(2,1)S(1)} %collective-permute-done.3.refs_3_), channel_id=1, source_target_pairs={{0,4},{1,3},{2,6},{3,1},{4,0},{5,7},{6,2},{7,5}} | collective-permute-start | bytes 6193160 | tf_op jit(solution)/shard_map/ppermute | solution.py:406
  490.0 28.0 %copy-start.7 = (bf16[2,576,1152]{2,1,0:T(8,128)(2,1)S(1)}, bf16[2,576,1152]{2,1,0:T(8,128)(2,1)}, u32[]{:S(2)}) copy-start(bf16[2,576,1152]{2,1,0:T(8,128)(2,1)} %get-tuple-element.28) | copy-start | bytes 7962628
  507.4 20.4 %collective-permute-start.1 = (bf16[256,1152]{1,0:T(8,128)(2,1)}, bf16[256,1152]{1,0:T(8,128)(2,1)S(1)}, u32[]{:S(2)}, u32[]{:S(2)}) collective-permute-start(bf16[256,1152]{1,0:T(8,128)(2,1)} %collective-permute-done.refs_0_), channel_id=1, source_target_pairs={{0,4},{1,3},{2,6},{3,1},{4,0},{5,7},{6,2},{7,5}} | collective-permute-start | bytes 1769480 | tf_op jit(solution)/shard_map/ppermute | solution.py:406
  509.0 56.3 %collective-permute-start.7 = (bf16[768,1152]{1,0:T(8,128)(2,1)}, bf16[768,1152]{1,0:T(8,128)(2,1)}, u32[]{:S(2)}, u32[]{:S(2)}) collective-permute-start(bf16[768,1152]{1,0:T(8,128)(2,1)} %collective-permute-done.6.refs_2_), channel_id=1, source_target_pairs={{0,1},{1,0},{2,3},{3,2},{4,5},{5,4},{6,7},{7,6}} | collective-permute-start | bytes 5308424 | tf_op jit(solution)/shard_map/ppermute | solution.py:406
  509.0 18.9 %copy-start.3 = (bf16[384,1152]{1,0:T(8,128)(2,1)}, bf16[384,1152]{1,0:T(8,128)(2,1)S(1)}, u32[]{:S(2)}) copy-start(bf16[384,1152]{1,0:T(8,128)(2,1)S(1)} %collective-permute-done.10.refs_5_) | copy-start | bytes 2654212
  509.0 48.5 %collective-permute-start.11 = (bf16[896,1152]{1,0:T(8,128)(2,1)S(1)}, bf16[896,1152]{1,0:T(8,128)(2,1)}, u32[]{:S(2)}, u32[]{:S(2)}) collective-permute-start(bf16[896,1152]{1,0:T(8,128)(2,1)S(1)} %collective-permute-done.3.refs_3_), channel_id=1, source_target_pairs={{0,1},{1,0},{2,3},{3,2},{4,5},{5,4},{6,7},{7,6}} | collective-permute-start | bytes 6193160 | tf_op jit(solution)/shard_map/ppermute | solution.py:406
  517.2 51.6 %collective-permute-start.5 = (bf16[896,1152]{1,0:T(8,128)(2,1)}, bf16[896,1152]{1,0:T(8,128)(2,1)}, u32[]{:S(2)}, u32[]{:S(2)}) collective-permute-start(bf16[896,1152]{1,0:T(8,128)(2,1)} %collective-permute-done.4.refs_0_), channel_id=1, source_target_pairs={{0,1},{1,0},{2,3},{3,2},{4,5},{5,4},{6,7},{7,6}} | collective-permute-start | bytes 6193160 | tf_op jit(solution)/shard_map/ppermute | solution.py:406
  527.9 0.8 copy-start.5
  527.9 37.4 %collective-permute-start.8 = (bf16[256,1152]{1,0:T(8,128)(2,1)}, bf16[256,1152]{1,0:T(8,128)(2,1)}, u32[]{:S(2)}, u32[]{:S(2)}) collective-permute-start(bf16[256,1152]{1,0:T(8,128)(2,1)} %collective-permute-done.refs_0_), channel_id=1, source_target_pairs={{0,1},{1,0},{2,3},{3,2},{4,5},{5,4},{6,7},{7,6}} | collective-permute-start | bytes 1769480 | tf_op jit(solution)/shard_map/ppermute | solution.py:406
  528.7 17.7 %slice-start = ((s8[21233664]{0:T(1024)(128)(4,1)}), s8[4194304]{0:T(1024)(128)(4,1)S(1)}, s32[]{:S(2)}) async-start(s8[21233664]{0:T(1024)(128)(4,1)} %bitcast.9), calls=%async_computation | async-start | bytes 8388608
  528.7 7.2 %copy-start = (bf16[2,4,2,144,4608]{4,3,2,1,0:T(8,128)(2,1)S(1)}, bf16[2,4,2,144,4608]{4,3,2,1,0:T(8,128)(2,1)}, u32[]{:S(2)}) copy-start(bf16[2,4,2,144,4608]{4,3,2,1,0:T(8,128)(2,1)} %get-tuple-element.19.src) | copy-start | bytes 63700996
  535.9 10.5 %slice-start.1 = ((s8[21233664]{0:T(1024)(128)(4,1)}), s8[4194304]{0:T(1024)(128)(4,1)S(1)}, s32[]{:S(2)}) async-start(s8[21233664]{0:T(1024)(128)(4,1)} %bitcast.9), calls=%async_computation.1 | async-start | bytes 8388608
  535.9 10.5 %slice-start.2 = ((s8[21233664]{0:T(1024)(128)(4,1)}), s8[4194304]{0:T(1024)(128)(4,1)S(1)}, s32[]{:S(2)}) async-start(s8[21233664]{0:T(1024)(128)(4,1)} %bitcast.9), calls=%async_computation.2 | async-start | bytes 8388608
  535.9 12.1 %slice-start.3 = ((s8[21233664]{0:T(1024)(128)(4,1)}), s8[4194304]{0:T(1024)(128)(4,1)S(1)}, s32[]{:S(2)}) async-start(s8[21233664]{0:T(1024)(128)(4,1)} %bitcast.9), calls=%async_computation.3 | async-start | bytes 8388608
  535.9 13.3 %slice-start.4 = ((s8[21233664]{0:T(1024)(128)(4,1)}), s8[4194304]{0:T(1024)(128)(4,1)S(1)}, s32[]{:S(2)}) async-start(s8[21233664]{0:T(1024)(128)(4,1)} %bitcast.9), calls=%async_computation.4 | async-start | bytes 8388608
  535.9 13.3 %slice-start.5 = ((s8[21233664]{0:T(1024)(128)(4,1)}), s8[262144]{0:T(1024)(128)(4,1)S(1)}, s32[]{:S(2)}) async-start(s8[21233664]{0:T(1024)(128)(4,1)} %bitcast.9), calls=%async_computation.5 | async-start | bytes 524288
  546.3 27.6 %collective-permute-start.2 = (bf16[256,1152]{1,0:T(8,128)(2,1)}, bf16[256,1152]{1,0:T(8,128)(2,1)S(1)}, u32[]{:S(2)}, u32[]{:S(2)}) collective-permute-start(bf16[256,1152]{1,0:T(8,128)(2,1)} %copy-done.5), channel_id=1, source_target_pairs={{0,1},{1,0},{2,3},{3,2},{4,5},{5,4},{6,7},{7,6}} | collective-permute-start | bytes 1769480 | tf_op jit(solution)/shard_map/ppermute | solution.py:406
  549.2 8.3 %copy-start.1 = (bf16[1152,1152]{1,0:T(8,128)(2,1)S(1)}, bf16[1152,1152]{1,0:T(8,128)(2,1)}, u32[]{:S(2)}) copy-start(bf16[1152,1152]{1,0:T(8,128)(2,1)} %get-tuple-element.24.refs_0_) | copy-start | bytes 7962628
  549.2 8.3 %copy-start.2 = (bf16[384,1152]{1,0:T(8,128)(2,1)S(1)}, bf16[384,1152]{1,0:T(8,128)(2,1)}, u32[]{:S(2)}) copy-start(bf16[384,1152]{1,0:T(8,128)(2,1)} %get-tuple-element.25.refs_1_) | copy-start | bytes 2654212
  549.2 8.3 %copy-start.4 = (bf16[384,1152]{1,0:T(8,128)(2,1)S(1)}, bf16[384,1152]{1,0:T(8,128)(2,1)}, u32[]{:S(2)}) copy-start(bf16[384,1152]{1,0:T(8,128)(2,1)} %copy-done.3) | copy-start | bytes 2654212
  568.7 4.3 copy-start.6

commit v8 on v7

--- a/solution.py
+++ b/solution.py
@@ -29,7 +29,7 @@
     return out
 
 
-TURNS = {"d": (3, 4), "a": (3, 4), "b": (2, 4), "gb": (3, 4), "ga": (3, 6), "gab": (3, 4), "mo": (3, 0), "ah": (2, 2), "d0": (4, 4), "a0": (4, 4)}
+TURNS = {"d": (2, 4), "a": (3, 4), "b": (2, 4), "gb": (2, 4), "ga": (2, 6), "gab": (2, 4), "mo": (3, 0), "ah": (2, 2), "d0": (4, 4), "a0": (4, 4)}
 SLICES = 4
 SHARED = 2
 
@@ -454,7 +454,8 @@
             (mate_b[0], 0, of_mate(at_b)),
         ],
         [(from_b[1], second, at_b), (mate_a[1], ahead, of_mate(at_a)), (mate_b[1], second, of_mate(at_b))],
-        [(from_ab[0], first, at_ab), (mate_ab[0], first, of_mate(at_ab))],
+        [(from_ab[0], first, at_ab)],
+        [(mate_ab[0], first, of_mate(at_ab))],
         [(from_ab[1], second, at_ab)],
         [(mate_ab[1], second, of_mate(at_ab))],
     ]

time: 575 us -> 576 us (level)
    pallas_call x5 -> x6, Pallas kernels: 17.1 us -> 17.7 us  [place_blocks(): pl.pallas_call(kernel, out_shape=jax.ShapeDtypeStruct(shape, items[0][0]....]
where the time goes in v8:
time: 576 us; the launch traced here: 575 us
  Pallas kernels  480 us (83%)
  waiting for transfers between devices  48.9 us (8%)
  other arithmetic  27.3 us (5%)
  local copies, waits for them, and re-layouts  10.9 us (2%)
  starting transfers between devices  7.19 us (1%)
    pallas_call x1, Pallas kernels, inner(): pl.pallas_call(functools.partial(body, chunks, group, kinds, (2,), firsts...  444 us
    ppermute x12, waiting for transfers between devices, send(): got.append(lax.ppermute(one, 'dp', pairs))  48.9 us
    add x2, other arithmetic, inner(): new_v = [0.95 * a + 0.05 * t * t for a, t in zip(v, total)]  27.3 us
    pallas_call x2, Pallas kernels, copy_blocks(): pl.pallas_call(kernel, out_shape=jax.ShapeDtypeStruct(a.shape, a.dtype),...  18.7 us
    pallas_call x6, Pallas kernels, place_blocks(): pl.pallas_call(kernel, out_shape=jax.ShapeDtypeStruct(shape, items[0][0]....  17.7 us
  transfers between devices with their start and end apart: 12, of which 2 were waited for; matrix products, arithmetic and copies ran while one was open for 5% of the time, Pallas kernels for 6%

profile of v8, /device:TPU:0, one launch (start us, length us, event | category | flops | bytes accessed | tf_op | source)
XLA Modules:
  0.0 575.4 jit_solution(8955218969424430550)
XLA Ops:
  0.6 443.9 %sum_step_gather.1 = (bf16[384,1152]{1,0:T(8,128)(2,1)}, bf16[1152,1152]{1,0:T(8,128)(2,1)}, bf16[768,1152]{1,0:T(8,128)(2,1)}, bf16[896,1152]{1,0:T(8,128)(2,1)...) custom-call(bf16[2,4,2,144,4608]{4,3,2,1,0:T(8,128)(2,1)} %bitcast.1, ...), custom_call_target="tpu_custom_call" | custom-call | tf_op jit(solution)/shard_map/sum_step_gather/pallas_call | solution.py:523
  444.6 1.4 collective-permute-start.3
  445.9 0.7 collective-permute-start
  446.6 0.0 collective-permute-start.10
  446.6 0.6 collective-permute-start.6
  447.2 1.0 collective-permute-start.9
  448.2 41.4 %collective-permute-done.3.refs_3_ = bf16[896,1152]{1,0:T(8,128)(2,1)} collective-permute-done((bf16[896,1152]{1,0:T(8,128)(2,1)}, bf16[896,1152]{1,0:T(8,128)(2,1)}, u32[]{:S(2)}, u32[]{:S(2)}) %collective-permute-start.3) | collective-permute-done | bytes 2064416 | tf_op jit(solution)/shard_map/ppermute | solution.py:406
  489.5 0.5 collective-permute-start.4
  490.1 17.4 %fusion.3 = (f32[2,144,4608]{2,1,0:T(8,128)}, f32[2,144,4608]{2,1,0:T(8,128)}, f32[2,144,4608]{2,1,0:T(8,128)}, f32[2,144,4608]{2,1,0:T(8,128)}) fusion(bf16[2,144,4608]{2,1,0:T(8,128)(2,1)} %get-tuple-element.26, f32[2,144,4608]{2,1,0:T(8,128)} %refs_9_.1, f32[2,144,4608]{2,1,0:T(8,128)} %refs_6_.1, bf16[2,144,4608]{2,1,0:T(8,128)(2,1)} %get-tuple-element.27, ...), kind=kLoop, calls=%fused_computation.9 | loop fusion | flops 21233664 | bytes 47775744 | tf_op jit(solution)/shard_map/add | solution.py:540
  507.5 0.0 collective-permute-done.refs_0_
  507.5 1.5 collective-permute-start.1
  509.0 0.0 collective-permute-done.6.refs_2_
  509.0 0.0 collective-permute-start.7
  509.0 0.0 copy-start.3
  509.0 0.5 collective-permute-start.11
  509.5 7.5 %collective-permute-done.4.refs_0_ = bf16[896,1152]{1,0:T(8,128)(2,1)S(1)} collective-permute-done((bf16[896,1152]{1,0:T(8,128)(2,1)}, bf16[896,1152]{1,0:T(8,128)(2,1)S(1)}, u32[]{:S(2)}, u32[]{:S(2)}) %collective-permute-start.4) | collective-permute-done | bytes 2064416 | tf_op jit(solution)/shard_map/ppermute | solution.py:406
  517.0 1.0 collective-permute-start.5
  518.0 9.8 %fusion.5 = (f32[2,576,1152]{2,1,0:T(8,128)}, f32[2,576,1152]{2,1,0:T(8,128)}) fusion(bf16[2,576,1152]{2,1,0:T(8,128)(2,1)S(1)} %copy-done.7, f32[2,576,1152]{2,1,0:T(8,128)} %refs_11_.1, f32[2,576,1152]{2,1,0:T(8,128)} %refs_8_.1), kind=kLoop, calls=%fused_computation.11 | loop fusion | flops 10616832 | bytes 23887872 | tf_op jit(solution)/shard_map/add | solution.py:540
  527.8 0.0 collective-permute-start.8
  527.9 0.8 copy-done.5
  528.7 7.2 %copy-done = bf16[2,4,2,144,4608]{4,3,2,1,0:T(8,128)(2,1)S(1)} copy-done((bf16[2,4,2,144,4608]{4,3,2,1,0:T(8,128)(2,1)S(1)}, bf16[2,4,2,144,4608]{4,3,2,1,0:T(8,128)(2,1)}, u32[]{:S(2)}) %copy-start) | copy-done | bytes 21233688
  535.9 10.4 %copy_blocks.2 = bf16[2,4,2,144,4608]{4,3,2,1,0:T(8,128)(2,1)} custom-call(bf16[2,4,2,144,4608]{4,3,2,1,0:T(8,128)(2,1)S(1)} %copy-done), custom_call_target="tpu_custom_call" | custom-call | flops 4000000000 | bytes 42467328 | tf_op jit(solution)/shard_map/copy_blocks/pallas_call | solution.py:346
  546.3 0.0 collective-permute-start.2
  546.4 1.6 slice-done.3
  548.0 1.2 slice-done.4
  549.2 8.3 %copy_blocks.3 = bf16[2,4,2,144,4608]{4,3,2,1,0:T(8,128)(2,1)} custom-call(bf16[2,4,2,144,4608]{4,3,2,1,0:T(8,128)(2,1)S(1)} %bitcast.10), custom_call_target="tpu_custom_call" | custom-call | flops 4000000000 | bytes 42467328 | tf_op jit(solution)/shard_map/copy_blocks/pallas_call | solution.py:346
  557.6 8.3 %place_blocks.6.refs_3_ = bf16[2,4,2,576,1152]{4,3,2,1,0:T(8,128)(2,1)} custom-call(bf16[1152,1152]{1,0:T(8,128)(2,1)S(1)} %copy-done.1, bf16[384,1152]{1,0:T(8,128)(2,1)S(1)} %copy-done.2, bf16[768,1152]{1,0:T(8,128)(2,1)} %collective-permute-done.6.refs_2_, bf16[896,1152]{1,0:T(8,128)(2,1)} %collective-permute-done.3.refs_3_, ...), custom_call_target="tpu_custom_call" | custom-call | flops 1000000000 | bytes 25952256 | tf_op jit(solution)/shard_map/place_blocks/pallas_call | solution.py:385
  565.9 3.4 place_blocks.7.refs_1_
  569.3 1.3 place_blocks.8.refs_1_
  570.7 3.0 place_blocks.9.refs_1_
  573.6 0.8 place_blocks.10.refs_1_
  574.5 0.8 place_blocks.11
  (32 shorter events, 0.1 us)
Async XLA Ops:
  444.6 45.0 %collective-permute-start.3 = (bf16[896,1152]{1,0:T(8,128)(2,1)}, bf16[896,1152]{1,0:T(8,128)(2,1)}, u32[]{:S(2)}, u32[]{:S(2)}) collective-permute-start(bf16[896,1152]{1,0:T(8,128)(2,1)} %get-tuple-element.22), channel_id=1, source_target_pairs={{0,2},{1,5},{2,0},{3,7},{4,6},{5,1},{6,4},{7,3}} | collective-permute-start | bytes 6193160 | tf_op jit(solution)/shard_map/ppermute | solution.py:406
  445.9 61.6 %collective-permute-start = (bf16[256,1152]{1,0:T(8,128)(2,1)}, bf16[256,1152]{1,0:T(8,128)(2,1)}, u32[]{:S(2)}, u32[]{:S(2)}) collective-permute-start(bf16[256,1152]{1,0:T(8,128)(2,1)} %get-tuple-element.21), channel_id=1, source_target_pairs={{0,2},{1,5},{2,0},{3,7},{4,6},{5,1},{6,4},{7,3}} | collective-permute-start | bytes 1769480 | tf_op jit(solution)/shard_map/ppermute | solution.py:406
  446.6 62.4 %collective-permute-start.10 = (bf16[384,1152]{1,0:T(8,128)(2,1)}, bf16[384,1152]{1,0:T(8,128)(2,1)S(1)}, u32[]{:S(2)}, u32[]{:S(2)}) collective-permute-start(bf16[384,1152]{1,0:T(8,128)(2,1)} %get-tuple-element.25.refs_1_), channel_id=1, source_target_pairs={{0,1},{1,0},{2,3},{3,2},{4,5},{5,4},{6,7},{7,6}} | collective-permute-start | bytes 2654216 | tf_op jit(solution)/shard_map/ppermute | solution.py:406
  446.6 62.4 %collective-permute-start.6 = (bf16[768,1152]{1,0:T(8,128)(2,1)}, bf16[768,1152]{1,0:T(8,128)(2,1)}, u32[]{:S(2)}, u32[]{:S(2)}) collective-permute-start(bf16[768,1152]{1,0:T(8,128)(2,1)} %get-tuple-element.23), channel_id=1, source_target_pairs={{0,4},{1,3},{2,6},{3,1},{4,0},{5,7},{6,2},{7,5}} | collective-permute-start | bytes 5308424 | tf_op jit(solution)/shard_map/ppermute | solution.py:406
  447.2 99.1 %collective-permute-start.9 = (bf16[1152,1152]{1,0:T(8,128)(2,1)}, bf16[1152,1152]{1,0:T(8,128)(2,1)}, u32[]{:S(2)}, u32[]{:S(2)}) collective-permute-start(bf16[1152,1152]{1,0:T(8,128)(2,1)} %get-tuple-element.24.refs_0_), channel_id=1, source_target_pairs={{0,1},{1,0},{2,3},{3,2},{4,5},{5,4},{6,7},{7,6}} | collective-permute-start | bytes 7962632 | tf_op jit(solution)/shard_map/ppermute | solution.py:406
  489.5 27.5 %collective-permute-start.4 = (bf16[896,1152]{1,0:T(8,128)(2,1)}, bf16[896,1152]{1,0:T(8,128)(2,1)S(1)}, u32[]{:S(2)}, u32[]{:S(2)}) collective-permute-start(bf16[896,1152]{1,0:T(8,128)(2,1)} %collective-permute-done.3.refs_3_), channel_id=1, source_target_pairs={{0,4},{1,3},{2,6},{3,1},{4,0},{5,7},{6,2},{7,5}} | collective-permute-start | bytes 6193160 | tf_op jit(solution)/shard_map/ppermute | solution.py:406
  490.1 27.9 %copy-start.7 = (bf16[2,576,1152]{2,1,0:T(8,128)(2,1)S(1)}, bf16[2,576,1152]{2,1,0:T(8,128)(2,1)}, u32[]{:S(2)}) copy-start(bf16[2,576,1152]{2,1,0:T(8,128)(2,1)} %get-tuple-element.28) | copy-start | bytes 7962628
  507.5 20.3 %collective-permute-start.1 = (bf16[256,1152]{1,0:T(8,128)(2,1)}, bf16[256,1152]{1,0:T(8,128)(2,1)S(1)}, u32[]{:S(2)}, u32[]{:S(2)}) collective-permute-start(bf16[256,1152]{1,0:T(8,128)(2,1)} %collective-permute-done.refs_0_), channel_id=1, source_target_pairs={{0,4},{1,3},{2,6},{3,1},{4,0},{5,7},{6,2},{7,5}} | collective-permute-start | bytes 1769480 | tf_op jit(solution)/shard_map/ppermute | solution.py:406
  509.0 56.9 %collective-permute-start.7 = (bf16[768,1152]{1,0:T(8,128)(2,1)}, bf16[768,1152]{1,0:T(8,128)(2,1)}, u32[]{:S(2)}, u32[]{:S(2)}) collective-permute-start(bf16[768,1152]{1,0:T(8,128)(2,1)} %collective-permute-done.6.refs_2_), channel_id=1, source_target_pairs={{0,1},{1,0},{2,3},{3,2},{4,5},{5,4},{6,7},{7,6}} | collective-permute-start | bytes 5308424 | tf_op jit(solution)/shard_map/ppermute | solution.py:406
  509.0 18.8 %copy-start.3 = (bf16[384,1152]{1,0:T(8,128)(2,1)}, bf16[384,1152]{1,0:T(8,128)(2,1)S(1)}, u32[]{:S(2)}) copy-start(bf16[384,1152]{1,0:T(8,128)(2,1)S(1)} %collective-permute-done.10.refs_5_) | copy-start | bytes 2654212
  509.0 48.5 %collective-permute-start.11 = (bf16[896,1152]{1,0:T(8,128)(2,1)}, bf16[896,1152]{1,0:T(8,128)(2,1)}, u32[]{:S(2)}, u32[]{:S(2)}) collective-permute-start(bf16[896,1152]{1,0:T(8,128)(2,1)} %collective-permute-done.3.refs_3_), channel_id=1, source_target_pairs={{0,1},{1,0},{2,3},{3,2},{4,5},{5,4},{6,7},{7,6}} | collective-permute-start | bytes 6193160 | tf_op jit(solution)/shard_map/ppermute | solution.py:406
  517.0 53.6 %collective-permute-start.5 = (bf16[896,1152]{1,0:T(8,128)(2,1)S(1)}, bf16[896,1152]{1,0:T(8,128)(2,1)}, u32[]{:S(2)}, u32[]{:S(2)}) collective-permute-start(bf16[896,1152]{1,0:T(8,128)(2,1)S(1)} %collective-permute-done.4.refs_0_), channel_id=1, source_target_pairs={{0,1},{1,0},{2,3},{3,2},{4,5},{5,4},{6,7},{7,6}} | collective-permute-start | bytes 6193160 | tf_op jit(solution)/shard_map/ppermute | solution.py:406
  527.8 0.9 copy-start.5
  527.8 38.0 %collective-permute-start.8 = (bf16[256,1152]{1,0:T(8,128)(2,1)}, bf16[256,1152]{1,0:T(8,128)(2,1)}, u32[]{:S(2)}, u32[]{:S(2)}) collective-permute-start(bf16[256,1152]{1,0:T(8,128)(2,1)} %collective-permute-done.refs_0_), channel_id=1, source_target_pairs={{0,1},{1,0},{2,3},{3,2},{4,5},{5,4},{6,7},{7,6}} | collective-permute-start | bytes 1769480 | tf_op jit(solution)/shard_map/ppermute | solution.py:406
  528.7 17.7 %slice-start = ((s8[21233664]{0:T(1024)(128)(4,1)}), s8[4194304]{0:T(1024)(128)(4,1)S(1)}, s32[]{:S(2)}) async-start(s8[21233664]{0:T(1024)(128)(4,1)} %bitcast.9), calls=%async_computation | async-start | bytes 8388608
  528.7 7.2 %copy-start = (bf16[2,4,2,144,4608]{4,3,2,1,0:T(8,128)(2,1)S(1)}, bf16[2,4,2,144,4608]{4,3,2,1,0:T(8,128)(2,1)}, u32[]{:S(2)}) copy-start(bf16[2,4,2,144,4608]{4,3,2,1,0:T(8,128)(2,1)} %get-tuple-element.19.src) | copy-start | bytes 63700996
  535.9 10.5 %slice-start.1 = ((s8[21233664]{0:T(1024)(128)(4,1)}), s8[4194304]{0:T(1024)(128)(4,1)S(1)}, s32[]{:S(2)}) async-start(s8[21233664]{0:T(1024)(128)(4,1)} %bitcast.9), calls=%async_computation.1 | async-start | bytes 8388608
  535.9 10.5 %slice-start.2 = ((s8[21233664]{0:T(1024)(128)(4,1)}), s8[4194304]{0:T(1024)(128)(4,1)S(1)}, s32[]{:S(2)}) async-start(s8[21233664]{0:T(1024)(128)(4,1)} %bitcast.9), calls=%async_computation.2 | async-start | bytes 8388608
  535.9 12.1 %slice-start.3 = ((s8[21233664]{0:T(1024)(128)(4,1)}), s8[4194304]{0:T(1024)(128)(4,1)S(1)}, s32[]{:S(2)}) async-start(s8[21233664]{0:T(1024)(128)(4,1)} %bitcast.9), calls=%async_computation.3 | async-start | bytes 8388608
  535.9 13.3 %slice-start.4 = ((s8[21233664]{0:T(1024)(128)(4,1)}), s8[4194304]{0:T(1024)(128)(4,1)S(1)}, s32[]{:S(2)}) async-start(s8[21233664]{0:T(1024)(128)(4,1)} %bitcast.9), calls=%async_computation.4 | async-start | bytes 8388608
  535.9 13.3 %slice-start.5 = ((s8[21233664]{0:T(1024)(128)(4,1)}), s8[262144]{0:T(1024)(128)(4,1)S(1)}, s32[]{:S(2)}) async-start(s8[21233664]{0:T(1024)(128)(4,1)} %bitcast.9), calls=%async_computation.5 | async-start | bytes 524288
  546.3 28.2 %collective-permute-start.2 = (bf16[256,1152]{1,0:T(8,128)(2,1)}, bf16[256,1152]{1,0:T(8,128)(2,1)S(1)}, u32[]{:S(2)}, u32[]{:S(2)}) collective-permute-start(bf16[256,1152]{1,0:T(8,128)(2,1)} %copy-done.5), channel_id=1, source_target_pairs={{0,1},{1,0},{2,3},{3,2},{4,5},{5,4},{6,7},{7,6}} | collective-permute-start | bytes 1769480 | tf_op jit(solution)/shard_map/ppermute | solution.py:406
  549.2 8.3 %copy-start.1 = (bf16[1152,1152]{1,0:T(8,128)(2,1)S(1)}, bf16[1152,1152]{1,0:T(8,128)(2,1)}, u32[]{:S(2)}) copy-start(bf16[1152,1152]{1,0:T(8,128)(2,1)} %get-tuple-element.24.refs_0_) | copy-start | bytes 7962628
  549.2 8.3 %copy-start.2 = (bf16[384,1152]{1,0:T(8,128)(2,1)S(1)}, bf16[384,1152]{1,0:T(8,128)(2,1)}, u32[]{:S(2)}) copy-start(bf16[384,1152]{1,0:T(8,128)(2,1)} %get-tuple-element.25.refs_1_) | copy-start | bytes 2654212
  549.2 8.3 %copy-start.4 = (bf16[384,1152]{1,0:T(8,128)(2,1)S(1)}, bf16[384,1152]{1,0:T(8,128)(2,1)}, u32[]{:S(2)}) copy-start(bf16[384,1152]{1,0:T(8,128)(2,1)} %copy-done.3) | copy-start | bytes 2654212
  570.7 3.0 copy-start.6
